TPU v7x, 32 devices: a whole 2x2x4 slice. The times are simulated.
32 devices in a mesh: fsdp: 16 (over z, y, core), tp: 2 (over x).
Axes of the slice: x: 2, y: 2, z: 4, core: 2. Of those that a mesh axis runs over, the one named last changes fastest.
Arguments:
- frames: bfloat16 [4096, 768], P('fsdp'), may hold values from -6 to 6
- cotangent: bfloat16 [4096, 768], P('fsdp'), may hold values from -6 to 6
- w_qkv: float32 [2, 768, 3, 768], P(None, 'fsdp', None, 'tp'), may hold values from -0.21875 to 0.21875
- w_out: float32 [2, 768, 768], P(None, 'tp', 'fsdp'), may hold values from -0.4375 to 0.4375
- w_up: float32 [2, 768, 3072], P(None, 'fsdp', 'tp'), may hold values from -0.21875 to 0.21875
- w_down: float32 [2, 3072, 768], P(None, 'tp', 'fsdp'), may hold values from -0.109375 to 0.109375
- b_qv: float32 [2, 2, 12, 64], P(None, None, 'tp', 'fsdp'), may hold values from -1.5 to 1.5
- b_up: float32 [2, 48, 64], P(None, 'tp', 'fsdp'), may hold values from -1.5 to 1.5
- vectors: float32 [2, 6, 768], P(None, None, 'fsdp'), may hold values from -0.6 to 1.5, as said below
- first_qkv: float32 [2, 768, 3, 768], P(None, 'fsdp', None, 'tp'), may hold values from -12 to 12
- first_out: float32 [2, 768, 768], P(None, 'tp', 'fsdp'), may hold values from -12 to 12
- first_up: float32 [2, 768, 3072], P(None, 'fsdp', 'tp'), may hold values from -12 to 12
- first_down: float32 [2, 3072, 768], P(None, 'tp', 'fsdp'), may hold values from -12 to 12
- first_bqv: float32 [2, 2, 12, 64], P(None, None, 'tp', 'fsdp'), may hold values from -12 to 12
- first_bup: float32 [2, 48, 64], P(None, 'tp', 'fsdp'), may hold values from -12 to 12
- first_vec: float32 [2, 6, 768], P(None, None, 'fsdp'), may hold values from -12 to 12
- second_qkv: float32 [2, 768, 3, 768], P(None, 'fsdp', None, 'tp'), may hold values from 0.4096 to 4.096
- second_out: float32 [2, 768, 768], P(None, 'tp', 'fsdp'), may hold values from 0.4096 to 4.096
- second_up: float32 [2, 768, 3072], P(None, 'fsdp', 'tp'), may hold values from 0.4096 to 4.096
- second_down: float32 [2, 3072, 768], P(None, 'tp', 'fsdp'), may hold values from 0.4096 to 4.096
- second_bqv: float32 [2, 2, 12, 64], P(None, None, 'tp', 'fsdp'), may hold values from 0.4096 to 4.096
- second_bup: float32 [2, 48, 64], P(None, 'tp', 'fsdp'), may hold values from 0.4096 to 4.096
- second_vec: float32 [2, 6, 768], P(None, None, 'fsdp'), may hold values from 0.4096 to 4.096
Outputs:
- output: bfloat16 [4096, 768], P('fsdp')
- grad_input: float32 [4096, 768], P('fsdp')
- grad_qkv: float32 [2, 768, 3, 768], P(None, 'fsdp', None, 'tp')
- grad_out: float32 [2, 768, 768], P(None, 'tp', 'fsdp')
- grad_up: float32 [2, 768, 3072], P(None, 'fsdp', 'tp')
- grad_down: float32 [2, 3072, 768], P(None, 'tp', 'fsdp')
- grad_bqv: float32 [2, 2, 12, 64], P(None, None, 'tp', 'fsdp')
- grad_bup: float32 [2, 48, 64], P(None, 'tp', 'fsdp')
- grad_vec: float32 [2, 6, 768], P(None, None, 'fsdp')
- next_qkv: float32 [2, 768, 3, 768], P(None, 'fsdp', None, 'tp')
- next_out: float32 [2, 768, 768], P(None, 'tp', 'fsdp')
- next_up: float32 [2, 768, 3072], P(None, 'fsdp', 'tp')
- next_down: float32 [2, 3072, 768], P(None, 'tp', 'fsdp')
- next_bqv: float32 [2, 2, 12, 64], P(None, None, 'tp', 'fsdp')
- next_bup: float32 [2, 48, 64], P(None, 'tp', 'fsdp')
- next_vec: float32 [2, 6, 768], P(None, None, 'fsdp')
- next_first_qkv: float32 [2, 768, 3, 768], P(None, 'fsdp', None, 'tp')
- next_first_out: float32 [2, 768, 768], P(None, 'tp', 'fsdp')
- next_first_up: float32 [2, 768, 3072], P(None, 'fsdp', 'tp')
- next_first_down: float32 [2, 3072, 768], P(None, 'tp', 'fsdp')
- next_first_bqv: float32 [2, 2, 12, 64], P(None, None, 'tp', 'fsdp')
- next_first_bup: float32 [2, 48, 64], P(None, 'tp', 'fsdp')
- next_first_vec: float32 [2, 6, 768], P(None, None, 'fsdp')
- next_second_qkv: float32 [2, 768, 3, 768], P(None, 'fsdp', None, 'tp')
- next_second_out: float32 [2, 768, 768], P(None, 'tp', 'fsdp')
- next_second_up: float32 [2, 768, 3072], P(None, 'fsdp', 'tp')
- next_second_down: float32 [2, 3072, 768], P(None, 'tp', 'fsdp')
- next_second_bqv: float32 [2, 2, 12, 64], P(None, None, 'tp', 'fsdp')
- next_second_bup: float32 [2, 48, 64], P(None, 'tp', 'fsdp')
- next_second_vec: float32 [2, 6, 768], P(None, None, 'fsdp')
Inputs may be any that keep to these rules, and one draw needn't show every extreme that they name: `vectors`: rows 0 and 2 of each layer (norm gains) lie in 0.5 to 1.5, the other rows in -0.6 to 0.6.
All inputs are finite; a program needn't handle non-finite values.
Results may differ from a plain program's by a relative error of at most 0.017.
Values may be sent and summed in bfloat16 or wider, within the bound.
A program may use at most 128 MiB of HBM per device.

v0:
```python
import jax
import jax.numpy as jnp
from jax import lax
from jax.sharding import PartitionSpec as P

HD = 64
SEQ = 256
LAYERS = 2
STEP = 3


norm_eps = 1e-05
beta_one = 0.9
beta_two = 0.999
adam_eps = 1e-08
decay_rate = 0.1
rate_matrix = 0.01
rate_vector = 0.2
root_half = 0.7071067811865476
inv_root_two_pi = 0.3989422804014327


def layer_norm(rows, gains, shifts):
    average = jnp.mean(rows, axis=-1, keepdims=True)
    centred = rows - average
    inverse = lax.rsqrt(jnp.mean(centred * centred, axis=-1, keepdims=True) + norm_eps)
    normed = centred * inverse
    return (normed * gains + shifts, normed, inverse)


def norm_back(upstream, normed, inverse, gains):
    scaled = upstream * gains
    return inverse * (
        scaled
        - jnp.mean(scaled, axis=-1, keepdims=True)
        - normed * jnp.mean(scaled * normed, axis=-1, keepdims=True)
    )


def gelu_value(before):
    return 0.5 * before * (1.0 + jax.scipy.special.erf(before * root_half))


def gelu_slope(before):
    return (
        0.5 * (1.0 + jax.scipy.special.erf(before * root_half))
        + before * jnp.exp(-0.5 * before * before) * inv_root_two_pi
    )


def split_heads(rows, clips):
    heads = rows.shape[1] // HD
    return rows.reshape(clips, SEQ, heads, HD).transpose(0, 2, 1, 3).reshape(clips * heads, SEQ, HD)


def join_heads(items, clips):
    heads = items.shape[0] // clips
    return (
        items.reshape(clips, heads, SEQ, HD).transpose(0, 2, 1, 3).reshape(clips * SEQ, heads * HD)
    )


def head_forward(item):
    query_head, key_head, value_head = item
    scores = jnp.einsum(
        "qd,kd->qk", query_head, key_head, preferred_element_type=jnp.float32
    ) * HD ** (-0.5)
    highest = jnp.max(scores, axis=1, keepdims=True)
    logsum = highest + jnp.log(jnp.sum(jnp.exp(scores - highest), axis=1, keepdims=True))
    weights = jnp.exp(scores - logsum).astype(jnp.bfloat16)
    context = jnp.dot(weights, value_head, preferred_element_type=jnp.float32).astype(jnp.bfloat16)
    return (context, logsum[:, 0])


def head_backward(item):
    query_head, key_head, value_head, logsum, grad_head = item
    scale = HD ** (-0.5)
    scores = (
        jnp.einsum("qd,kd->qk", query_head, key_head, preferred_element_type=jnp.float32) * scale
    )
    probs = jnp.exp(scores - logsum[:, None])
    weights = probs.astype(jnp.bfloat16)
    grad_values = jnp.einsum("qk,qd->kd", weights, grad_head, preferred_element_type=jnp.float32)
    grad_probs = jnp.einsum("qd,kd->qk", grad_head, value_head, preferred_element_type=jnp.float32)
    inner = jnp.sum(probs * grad_probs, axis=1, keepdims=True)
    grad_scores = (probs * (grad_probs - inner) * scale).astype(jnp.bfloat16)
    grad_query = jnp.dot(grad_scores, key_head, preferred_element_type=jnp.float32)
    grad_keys = jnp.einsum("qk,qd->kd", grad_scores, query_head, preferred_element_type=jnp.float32)
    return (grad_query, grad_keys, grad_values)


def unpack(gathered):
    wqkv, wout, wup, wdown, bqv, bup, vecs = gathered
    return (wqkv, wout, wup, wdown, bqv.reshape(2, -1), bup.reshape(-1), vecs)


def fetch_forward(masters, which_layer):
    piece_qkv, piece_out, piece_up, piece_down, piece_bqv, piece_bup, piece_vec = tuple(
        (master[which_layer].astype(jnp.bfloat16) for master in masters)
    )
    gathered = (
        lax.all_gather(piece_qkv, "fsdp", axis=0, tiled=True),
        lax.all_gather(piece_out, "fsdp", axis=1, tiled=True),
        lax.all_gather(piece_up, "fsdp", axis=0, tiled=True),
        lax.all_gather(piece_down, "fsdp", axis=1, tiled=True),
        lax.all_gather(piece_bqv, "fsdp", axis=2, tiled=True),
        lax.all_gather(piece_bup, "fsdp", axis=1, tiled=True),
        lax.all_gather(piece_vec, "fsdp", axis=1, tiled=True),
    )
    return unpack(gathered)


def fetch_again(masters, which_layer):
    piece_qkv, piece_out, piece_up, piece_down, piece_bqv, piece_bup, piece_vec = tuple(
        (master[which_layer].astype(jnp.bfloat16) for master in masters)
    )
    gathered = (
        lax.all_gather(piece_qkv, "fsdp", axis=0, tiled=True),
        lax.all_gather(piece_out, "fsdp", axis=1, tiled=True),
        lax.all_gather(piece_up, "fsdp", axis=0, tiled=True),
        lax.all_gather(piece_down, "fsdp", axis=1, tiled=True),
        lax.all_gather(piece_bqv, "fsdp", axis=2, tiled=True),
        lax.all_gather(piece_bup, "fsdp", axis=1, tiled=True),
        lax.all_gather(piece_vec, "fsdp", axis=1, tiled=True),
    )
    return unpack(gathered)


def layer_forward(resid, params, clips):
    wqkv, wout, wup, wdown, bqv, bup, vecs = params
    half = wqkv.shape[2]
    normed_one, hat_one, inv_one = layer_norm(resid, vecs[0], vecs[1])
    act_one = normed_one.astype(jnp.bfloat16)
    projected = jnp.dot(
        act_one, wqkv.reshape(-1, 3 * half), preferred_element_type=jnp.float32
    ).reshape(-1, 3, half)
    queries = (projected[:, 0] + bqv[0]).astype(jnp.bfloat16)
    key_rows = projected[:, 1].astype(jnp.bfloat16)
    values = (projected[:, 2] + bqv[1]).astype(jnp.bfloat16)
    head_items = (
        split_heads(queries, clips),
        split_heads(key_rows, clips),
        split_heads(values, clips),
    )
    context_items, logsum = lax.map(head_forward, head_items)
    context = join_heads(context_items, clips)
    head_terms = jnp.dot(context, wout, preferred_element_type=jnp.float32)
    middle = resid + lax.psum(head_terms.astype(jnp.bfloat16), "tp").astype(jnp.float32) + vecs[4]
    normed_two, hat_two, inv_two = layer_norm(middle, vecs[2], vecs[3])
    act_two = normed_two.astype(jnp.bfloat16)
    before = jnp.dot(act_two, wup, preferred_element_type=jnp.float32) + bup
    hidden = gelu_value(before).astype(jnp.bfloat16)
    column_terms = jnp.dot(hidden, wdown, preferred_element_type=jnp.float32)
    result = (
        middle + lax.psum(column_terms.astype(jnp.bfloat16), "tp").astype(jnp.float32) + vecs[5]
    )
    saved = (
        act_one,
        hat_one,
        inv_one,
        head_items,
        context,
        logsum,
        act_two,
        hat_two,
        inv_two,
        before,
        hidden,
    )
    return (result, saved)


def layer_backward(upstream, saved, params, clips):
    wqkv, wout, wup, wdown, bqv, bup, vecs = params
    (
        act_one,
        hat_one,
        inv_one,
        head_items,
        context,
        logsum,
        act_two,
        hat_two,
        inv_two,
        before,
        hidden,
    ) = saved
    half = wqkv.shape[2]
    grad_shift_out = jnp.sum(upstream, axis=0)
    upstream_low = upstream.astype(jnp.bfloat16)
    grad_down = jnp.einsum("rf,rd->fd", hidden, upstream_low, preferred_element_type=jnp.float32)
    grad_before = jnp.einsum(
        "rd,fd->rf", upstream_low, wdown, preferred_element_type=jnp.float32
    ) * gelu_slope(before)
    grad_bup = jnp.sum(grad_before, axis=0)
    before_low = grad_before.astype(jnp.bfloat16)
    grad_up = jnp.einsum("rd,rf->df", act_two, before_low, preferred_element_type=jnp.float32)
    column_grads = jnp.einsum("rf,df->rd", before_low, wup, preferred_element_type=jnp.float32)
    grad_act_two = lax.psum(column_grads.astype(jnp.bfloat16), "tp").astype(jnp.float32)
    grad_gain_two = jnp.sum(grad_act_two * hat_two, axis=0)
    grad_shift_two = jnp.sum(grad_act_two, axis=0)
    grad_middle = upstream + norm_back(grad_act_two, hat_two, inv_two, vecs[2])
    grad_bias_out = jnp.sum(grad_middle, axis=0)
    middle_low = grad_middle.astype(jnp.bfloat16)
    grad_wout = jnp.einsum("rc,rd->cd", context, middle_low, preferred_element_type=jnp.float32)
    grad_context = jnp.einsum(
        "rd,cd->rc", middle_low, wout, preferred_element_type=jnp.float32
    ).astype(jnp.bfloat16)
    back_items = lax.map(
        head_backward,
        (head_items[0], head_items[1], head_items[2], logsum, split_heads(grad_context, clips)),
    )
    grad_query = join_heads(back_items[0], clips)
    grad_keys = join_heads(back_items[1], clips)
    grad_values = join_heads(back_items[2], clips)
    grad_bqv = jnp.stack([jnp.sum(grad_query, axis=0), jnp.sum(grad_values, axis=0)])
    stacked = (
        jnp.stack([grad_query, grad_keys, grad_values], axis=1)
        .astype(jnp.bfloat16)
        .reshape(-1, 3 * half)
    )
    flat_qkv = wqkv.reshape(-1, 3 * half)
    grad_qkv = jnp.einsum(
        "rd,rc->dc", act_one, stacked, preferred_element_type=jnp.float32
    ).reshape(-1, 3, half)
    head_grads = jnp.einsum("rc,dc->rd", stacked, flat_qkv, preferred_element_type=jnp.float32)
    grad_act_one = lax.psum(head_grads.astype(jnp.bfloat16), "tp").astype(jnp.float32)
    grad_gain_one = jnp.sum(grad_act_one * hat_one, axis=0)
    grad_shift_one = jnp.sum(grad_act_one, axis=0)
    grad_resid = grad_middle + norm_back(grad_act_one, hat_one, inv_one, vecs[0])
    grad_vectors = jnp.stack(
        [
            grad_gain_one,
            grad_shift_one,
            grad_gain_two,
            grad_shift_two,
            grad_bias_out,
            grad_shift_out,
        ]
    )
    grads = (
        grad_qkv,
        grad_wout,
        grad_up,
        grad_down,
        grad_bqv.reshape(2, -1, HD),
        grad_bup.reshape(-1, HD),
        grad_vectors,
    )
    return (grad_resid, grads)


def scatter_layer(grads):
    grad_qkv, grad_wout, grad_up, grad_down, grad_bqv, grad_bup, grad_vectors = grads
    return (
        lax.psum_scatter(grad_qkv, "fsdp", scatter_dimension=0, tiled=True),
        lax.psum_scatter(grad_wout, "fsdp", scatter_dimension=1, tiled=True),
        lax.psum_scatter(grad_up, "fsdp", scatter_dimension=0, tiled=True),
        lax.psum_scatter(grad_down, "fsdp", scatter_dimension=1, tiled=True),
        lax.psum_scatter(grad_bqv, "fsdp", scatter_dimension=2, tiled=True),
        lax.psum_scatter(grad_bup, "fsdp", scatter_dimension=1, tiled=True),
        lax.psum_scatter(grad_vectors, "fsdp", scatter_dimension=1, tiled=True),
    )


def adamw(weight, gradient, first, second, rate, decay):
    first_new = beta_one * first + (1.0 - beta_one) * gradient
    second_new = beta_two * second + (1.0 - beta_two) * gradient * gradient
    first_hat = first_new / (1.0 - beta_one**STEP)
    second_hat = second_new / (1.0 - beta_two**STEP)
    weight_new = weight - rate * (first_hat / (jnp.sqrt(second_hat) + adam_eps) + decay * weight)
    return (weight_new, first_new, second_new)


def on_device(
    frames,
    cotangent,
    w_qkv,
    w_out,
    w_up,
    w_down,
    b_qv,
    b_up,
    vectors,
    first_qkv,
    first_out,
    first_up,
    first_down,
    first_bqv,
    first_bup,
    first_vec,
    second_qkv,
    second_out,
    second_up,
    second_down,
    second_bqv,
    second_bup,
    second_vec,
):
    clips = frames.shape[0] // SEQ
    masters = (w_qkv, w_out, w_up, w_down, b_qv, b_up, vectors)
    firsts = (first_qkv, first_out, first_up, first_down, first_bqv, first_bup, first_vec)
    seconds = (second_qkv, second_out, second_up, second_down, second_bqv, second_bup, second_vec)
    resid = frames.astype(jnp.float32)
    kept_params = []
    saved_all = []
    for which_layer in range(LAYERS):
        params = fetch_forward(masters, which_layer)
        kept_params.append(params)
        resid, saved = layer_forward(resid, params, clips)
        saved_all.append(saved)
    output = resid.astype(jnp.bfloat16)
    upstream = cotangent.astype(jnp.float32)
    layer_grads = [None] * LAYERS
    for which_layer in reversed(range(LAYERS)):
        params = fetch_again(masters, which_layer)
        upstream, grads = layer_backward(upstream, saved_all[which_layer], params, clips)
        layer_grads[which_layer] = scatter_layer(grads)
    stacked = tuple(
        (
            jnp.stack([layer_grads[section][number] for section in range(LAYERS)])
            for number in range(7)
        )
    )
    rates = (rate_matrix,) * 4 + (rate_vector,) * 3
    decays = (decay_rate,) * 4 + (0.0,) * 3
    updated = [
        adamw(
            masters[number],
            stacked[number],
            firsts[number],
            seconds[number],
            rates[number],
            decays[number],
        )
        for number in range(7)
    ]
    return (
        output,
        upstream,
        stacked[0],
        stacked[1],
        stacked[2],
        stacked[3],
        stacked[4],
        stacked[5],
        stacked[6],
        updated[0][0],
        updated[1][0],
        updated[2][0],
        updated[3][0],
        updated[4][0],
        updated[5][0],
        updated[6][0],
        updated[0][1],
        updated[1][1],
        updated[2][1],
        updated[3][1],
        updated[4][1],
        updated[5][1],
        updated[6][1],
        updated[0][2],
        updated[1][2],
        updated[2][2],
        updated[3][2],
        updated[4][2],
        updated[5][2],
        updated[6][2],
    )


def solution(mesh):
    return jax.shard_map(
        on_device,
        mesh=mesh,
        in_specs=(
            P("fsdp", None),
            P("fsdp", None),
            P(None, "fsdp", None, "tp"),
            P(None, "tp", "fsdp"),
            P(None, "fsdp", "tp"),
            P(None, "tp", "fsdp"),
            P(None, None, "tp", "fsdp"),
            P(None, "tp", "fsdp"),
            P(None, None, "fsdp"),
            P(None, "fsdp", None, "tp"),
            P(None, "tp", "fsdp"),
            P(None, "fsdp", "tp"),
            P(None, "tp", "fsdp"),
            P(None, None, "tp", "fsdp"),
            P(None, "tp", "fsdp"),
            P(None, None, "fsdp"),
            P(None, "fsdp", None, "tp"),
            P(None, "tp", "fsdp"),
            P(None, "fsdp", "tp"),
            P(None, "tp", "fsdp"),
            P(None, None, "tp", "fsdp"),
            P(None, "tp", "fsdp"),
            P(None, None, "fsdp"),
        ),
        out_specs=(
            P("fsdp", None),
            P("fsdp", None),
            P(None, "fsdp", None, "tp"),
            P(None, "tp", "fsdp"),
            P(None, "fsdp", "tp"),
            P(None, "tp", "fsdp"),
            P(None, None, "tp", "fsdp"),
            P(None, "tp", "fsdp"),
            P(None, None, "fsdp"),
            P(None, "fsdp", None, "tp"),
            P(None, "tp", "fsdp"),
            P(None, "fsdp", "tp"),
            P(None, "tp", "fsdp"),
            P(None, None, "tp", "fsdp"),
            P(None, "tp", "fsdp"),
            P(None, None, "fsdp"),
            P(None, "fsdp", None, "tp"),
            P(None, "tp", "fsdp"),
            P(None, "fsdp", "tp"),
            P(None, "tp", "fsdp"),
            P(None, None, "tp", "fsdp"),
            P(None, "tp", "fsdp"),
            P(None, None, "fsdp"),
            P(None, "fsdp", None, "tp"),
            P(None, "tp", "fsdp"),
            P(None, "fsdp", "tp"),
            P(None, "tp", "fsdp"),
            P(None, None, "tp", "fsdp"),
            P(None, "tp", "fsdp"),
            P(None, None, "fsdp"),
        ),
        check_vma=False,
    )
```

profile of v0, /device:TPU:0, one launch (start us, length us, event | category | flops | bytes accessed | tf_op | source)
XLA Modules:
  0.0 1385.6 jit_solution(8959092495729330225)
XLA Ops:
  11.3 23.2 %all-gather.2 = bf16[1,2,6,64]{2,1,0,3:T(2,128)(2,1)S(1)} all-gather(bf16[1,2,6,4]{2,1,0,3:T(2,128)(2,1)S(1)} %get-tuple-element.666), channel_id=4, replica_groups=mesh['fsdp'=16,'tp'=2] {'fsdp'}, dimensions={3}, use_global_device_ids=true | all-gather | bytes 1632 | tf_op jit(solution)/shard_map/all_gather | solution.py:106
  37.3 19.6 %all-gather = bf16[1,6,768]{1,0,2:T(2,128)(2,1)S(1)} all-gather(bf16[1,6,48]{1,0,2:T(2,128)(2,1)S(1)} %get-tuple-element.662), channel_id=2, replica_groups=mesh['fsdp'=16,'tp'=2] {'fsdp'}, dimensions={2}, use_global_device_ids=true | all-gather | bytes 9792 | tf_op jit(solution)/shard_map/all_gather | solution.py:108
  57.9 20.2 %all-gather.3 = bf16[1,384,768]{1,2,0:T(8,128)(2,1)S(1)} all-gather(bf16[1,384,48]{1,2,0:T(8,128)(2,1)S(1)} %get-tuple-element.657), channel_id=5, replica_groups=mesh['fsdp'=16,'tp'=2] {'fsdp'}, dimensions={2}, use_global_device_ids=true | all-gather | bytes 626688 | tf_op jit(solution)/shard_map/all_gather | solution.py:103
  78.1 13.9 %fusion.184 = (f32[768]{0:T(1024)}, f32[768]{0:T(1024)S(1)}, f32[768]{0:T(1024)S(1)}, f32[768]{0:T(1024)S(1)}, f32[768]{0:T(1024)S(1)}, /*index=5*/f32[768]{0:T(1024)S(1)}) fusion(bf16[1,6,768]{1,0,2:T(2,128)(2,1)S(1)} %all-gather), kind=kLoop, calls=%fused_computation.257 | loop fusion | flops 4608 | bytes 27648 | tf_op jit(solution)/shard_map/add | solution.py:155
  92.1 2.6 copy.297
  98.1 11.0 while.52
  113.3 17.7 %all-gather.5 = bf16[1,24,64]{1,0,2:T(2,128)(2,1)S(1)} all-gather(bf16[1,24,4]{1,0,2:T(2,128)(2,1)S(1)} %get-tuple-element.668), channel_id=7, replica_groups=mesh['fsdp'=16,'tp'=2] {'fsdp'}, dimensions={2}, use_global_device_ids=true | all-gather | bytes 3264 | tf_op jit(solution)/shard_map/all_gather | solution.py:107
  131.2 18.7 %all-gather.9 = bf16[1,2,6,64]{2,1,0,3:T(2,128)(2,1)S(1)} all-gather(bf16[1,2,6,4]{2,1,0,3:T(2,128)(2,1)S(1)} %copy-done.101), channel_id=11, replica_groups=mesh['fsdp'=16,'tp'=2] {'fsdp'}, dimensions={3}, use_global_device_ids=true | all-gather | bytes 1632 | tf_op jit(solution)/shard_map/all_gather | solution.py:106
  149.8 20.5 %all-gather.10 = bf16[1,384,768]{1,2,0:T(8,128)(2,1)S(1)} all-gather(bf16[1,384,48]{1,2,0:T(8,128)(2,1)S(1)} %copy-done.59), channel_id=12, replica_groups=mesh['fsdp'=16,'tp'=2] {'fsdp'}, dimensions={2}, use_global_device_ids=true | all-gather | bytes 626688 | tf_op jit(solution)/shard_map/all_gather | solution.py:103
  173.1 6.0 all-gather.23.cloned.1.call-done
  179.2 3.7 multiply_convert_fusion.3
  182.9 40.4 %all-gather.25.cloned.1.call-done = bf16[1,1536,768]{1,2,0:T(8,128)(2,1)} async-done(((bf16[1,1536,48]{1,2,0:T(8,128)(2,1)}), bf16[1,1536,768]{1,2,0:T(8,128)(2,1)}) %all-gather.25.cloned.1.call-update) | async-done | bytes 2359312 | tf_op jit(solution)/shard_map/all_gather | solution.py:105
  223.3 3.2 fusion.117
  228.0 20.6 %all-gather.7 = bf16[1,6,768]{1,0,2:T(2,128)(2,1)S(1)} all-gather(bf16[1,6,48]{1,0,2:T(2,128)(2,1)S(1)} %copy-done.64), channel_id=9, replica_groups=mesh['fsdp'=16,'tp'=2] {'fsdp'}, dimensions={2}, use_global_device_ids=true | all-gather | bytes 9792 | tf_op jit(solution)/shard_map/all_gather | solution.py:108
  248.6 14.0 %fusion.178 = (f32[768]{0:T(1024)}, f32[768]{0:T(1024)}, f32[768]{0:T(1024)S(1)}, f32[768]{0:T(1024)}, f32[768]{0:T(1024)S(1)}, /*index=5*/f32[768]{0:T(1024)S(1)}) fusion(bf16[1,6,768]{1,0,2:T(2,128)(2,1)S(1)} %all-gather.7), kind=kLoop, calls=%fused_computation.244 | loop fusion | flops 4608 | bytes 27648 | tf_op jit(solution)/shard_map/add | solution.py:155
  262.6 2.9 all-gather.27.cloned.1.call-done
  265.5 3.8 copy.309
  269.3 23.4 %all-reduce.16.cloned.1.call-done = bf16[256,768]{1,0:T(8,128)(2,1)} async-done(((bf16[256,768]{1,0:T(8,128)(2,1)}), bf16[256,768]{1,0:T(8,128)(2,1)}) %all-reduce.16.cloned.1.call-update) | async-done | bytes 393232 | tf_op jit(solution)/shard_map/psum | solution.py:155
  302.8 13.5 while.53
  319.2 21.6 %all-gather.12 = bf16[1,24,64]{1,0,2:T(2,128)(2,1)S(1)} all-gather(bf16[1,24,4]{1,0,2:T(2,128)(2,1)S(1)} %copy-done.100), channel_id=14, replica_groups=mesh['fsdp'=16,'tp'=2] {'fsdp'}, dimensions={2}, use_global_device_ids=true | all-gather | bytes 3264 | tf_op jit(solution)/shard_map/all_gather | solution.py:107
  341.0 2.6 all-reduce.18.cloned.1.call-done
  345.0 43.7 %all-gather.29.cloned.1.call-done = bf16[1,768,1536]{2,1,0:T(8,128)(2,1)} async-done(((bf16[1,48,1536]{2,1,0:T(8,128)(2,1)}), bf16[1,768,1536]{2,1,0:T(8,128)(2,1)}) %all-gather.29.cloned.1.call-update) | async-done | bytes 2359312 | tf_op jit(solution)/shard_map/all_gather | solution.py:104
  388.8 4.0 multiply_convert_fusion.2
  392.8 39.9 %all-gather.31.cloned.1.call-done = bf16[1,1536,768]{1,2,0:T(8,128)(2,1)} async-done(((bf16[1,1536,48]{1,2,0:T(8,128)(2,1)}), bf16[1,1536,768]{1,2,0:T(8,128)(2,1)}) %all-gather.31.cloned.1.call-update) | async-done | bytes 2359312 | tf_op jit(solution)/shard_map/all_gather | solution.py:105
  432.7 3.9 fusion.248
  441.4 22.3 %all-reduce.20.cloned.1.call-done = bf16[256,768]{1,0:T(8,128)(2,1)} async-done(((bf16[256,768]{1,0:T(8,128)(2,1)}), bf16[256,768]{1,0:T(8,128)(2,1)}) %all-reduce.20.cloned.1.call-update) | async-done | bytes 393232 | tf_op jit(solution)/shard_map/psum | solution.py:199
  463.7 2.1 fusion.161
  465.8 2.1 fusion.233
  472.2 46.6 %while.54 = (s32[]{:T(128)}, f32[6,256,64]{1,2,0:T(8,128)}, bf16[6,256,64]{1,2,0:T(8,128)(2,1)}, f32[6,256,64]{1,2,0:T(8,128)}, bf16[6,256,64]{2,1,0:T(8,128)(2,...) while((s32[]{:T(128)}, f32[6,256,64]{1,2,0:T(8,128)}, ...), condition=%wide.region_25.26_spmd, body=%wide.region_23.25_spmd.sunk | while | flops 42532608 | bytes 2566249 | solution.py:209
  523.1 2.9 fusion.111
  526.2 25.9 %all-reduce.22.cloned.1.call-done = bf16[256,768]{1,0:T(8,128)(2,1)} async-done(((bf16[256,768]{1,0:T(8,128)(2,1)}), bf16[256,768]{1,0:T(8,128)(2,1)}) %all-reduce.22.cloned.1.call-update) | async-done | bytes 393232 | tf_op jit(solution)/shard_map/psum | solution.py:227
  552.0 2.0 fusion.162
  554.1 2.1 fusion.229
  556.1 3.4 fusion.249
  562.0 3.2 fusion.123
  565.2 22.6 %all-reduce.24.cloned.1.call-done = bf16[256,768]{1,0:T(8,128)(2,1)} async-done(((bf16[256,768]{1,0:T(8,128)(2,1)}), bf16[256,768]{1,0:T(8,128)(2,1)}) %all-reduce.24.cloned.1.call-update) | async-done | bytes 393232 | tf_op jit(solution)/shard_map/psum | solution.py:199
  587.9 2.2 fusion.163
  590.1 2.0 fusion.231
  596.5 41.4 %while.55 = (s32[]{:T(128)}, f32[6,256,64]{1,2,0:T(8,128)}, bf16[6,256,64]{1,2,0:T(8,128)(2,1)}, f32[6,256,64]{1,2,0:T(8,128)}, bf16[6,256,64]{2,1,0:T(8,128)(2,...) while((s32[]{:T(128)}, f32[6,256,64]{1,2,0:T(8,128)}, ...), condition=%wide.region_34.35_spmd, body=%wide.region_32.34_spmd.sunk | while | flops 42532608 | bytes 2566249 | solution.py:209
  642.1 3.1 fusion.108
  651.6 28.3 %all-reduce.26.cloned.1.call-done = (bf16[256,768]{1,0:T(8,128)(2,1)}, bf16[256,768]{1,0:T(8,128)(2,1)}) async-done(((bf16[256,768]{1,0:T(8,128)(2,1)}, bf16[256,768]{1,0:T(8,128)(2,1)}), (bf16[256,768]{1,0:T(8,128)(2,1)}, bf16[256,768]{1,0:T(8,128)(2,1)})) %all-reduce.26.cloned.1.call-update) | async-done | bytes 786448 | tf_op jit(solution)/shard_map/psum | solution.py:155
  679.8 2.0 fusion.164
  682.9 2.6 fusion.207
  687.1 1.9 maximum_convert_fusion
  689.1 2.1 copy.337
  691.2 3.7 fusion.167
  697.2 3.7 fusion.169
  702.2 3.0 fusion.250
  706.3 4.1 fusion.204
  711.6 3.2 fusion.193
  715.9 3.1 fusion.190
  725.4 14.4 %reduce-scatter.37.cloned.1.call-done = f32[48,6]{1,0:T(8,128)} async-done(((f32[768,6]{1,0:T(8,128)}), f32[48,6]{1,0:T(8,128)}) %reduce-scatter.37.cloned.1.call-update) | async-done | bytes 1168
  741.6 59.5 %all-reduce.4 = (f32[2,6,64]{1,2,0:T(8,128)S(1)}, f32[2,6,64]{1,2,0:T(8,128)S(1)}, f32[24,64]{1,0:T(8,128)S(1)}, f32[24,64]{1,0:T(8,128)S(1)}) all-reduce(f32[2,6,64]{1,2,0:T(8,128)} %copy.340, f32[2,6,64]{1,2,0:T(8,128)S(1)} %copy.339, f32[24,64]{1,0:T(8,128)S(1)} %reshape.503, ...), channel_id=25, replica_groups=mesh['fsdp'=16,'tp'=2] {'fsdp'}, use_global_device_ids=true, to_apply=%region_51.52.clone | all-reduce | flops 4608 | bytes 36864
  811.7 47.8 %reduce-scatter.25.cloned.1.call-done = f32[384,48]{0,1:T(8,128)} async-done(((f32[384,768]{0,1:T(8,128)}), f32[384,48]{0,1:T(8,128)}) %reduce-scatter.25.cloned.1.call-update) | async-done | bytes 73744 | tf_op jit(solution)/shard_map/reduce_scatter | solution.py:257
  859.5 60.6 %reduce-scatter.23.cloned.1.call-done = f32[384,48]{0,1:T(8,128)} async-done(((f32[384,768]{0,1:T(8,128)}), f32[384,48]{0,1:T(8,128)}) %reduce-scatter.23.cloned.1.call-update) | async-done | bytes 73744 | tf_op jit(solution)/shard_map/reduce_scatter | solution.py:257
  921.9 69.1 %reduce-scatter.21.cloned.1.call-done = f32[48,3,384]{2,0,1:T(8,128)} async-done(((f32[768,3,384]{2,0,1:T(8,128)}), f32[48,3,384]{2,0,1:T(8,128)}) %reduce-scatter.21.cloned.1.call-update) | async-done | bytes 221200 | tf_op jit(solution)/shard_map/reduce_scatter | solution.py:256
  991.0 70.8 %reduce-scatter.19.cloned.1.call-done = f32[48,3,384]{2,0,1:T(8,128)} async-done(((f32[768,3,384]{2,0,1:T(8,128)}), f32[48,3,384]{2,0,1:T(8,128)}) %reduce-scatter.19.cloned.1.call-update) | async-done | bytes 221200 | tf_op jit(solution)/shard_map/reduce_scatter | solution.py:256
  1061.8 2.5 multiply_subtract_fusion.2
  1064.3 75.7 %reduce-scatter.33.cloned.1.call-done = f32[1536,48]{0,1:T(8,128)} async-done(((f32[1536,768]{0,1:T(8,128)}), f32[1536,48]{0,1:T(8,128)}) %reduce-scatter.33.cloned.1.call-update) | async-done | bytes 294928 | tf_op jit(solution)/shard_map/reduce_scatter | solution.py:259
  1140.0 78.7 %reduce-scatter.31.cloned.1.call-done = f32[1536,48]{0,1:T(8,128)} async-done(((f32[1536,768]{0,1:T(8,128)}), f32[1536,48]{0,1:T(8,128)}) %reduce-scatter.31.cloned.1.call-update) | async-done | bytes 294928 | tf_op jit(solution)/shard_map/reduce_scatter | solution.py:259
  1218.7 2.8 multiply_subtract_fusion
  1221.5 75.9 %reduce-scatter.29.cloned.1.call-done = f32[48,1536]{1,0:T(8,128)} async-done(((f32[768,1536]{1,0:T(8,128)}), f32[48,1536]{1,0:T(8,128)}) %reduce-scatter.29.cloned.1.call-update) | async-done | bytes 294928 | tf_op jit(solution)/shard_map/reduce_scatter | solution.py:258
  1297.3 78.7 %reduce-scatter.27.cloned.1.call-done = f32[48,1536]{1,0:T(8,128)} async-done(((f32[768,1536]{1,0:T(8,128)}), f32[48,1536]{1,0:T(8,128)}) %reduce-scatter.27.cloned.1.call-update) | async-done | bytes 294928 | tf_op jit(solution)/shard_map/reduce_scatter | solution.py:258
  1376.0 2.6 multiply_subtract_fusion.1
  (550 shorter events, 205.8 us)
Async XLA Ops:
  7.2 28.6 %copy-start.52 = (f32[2,384,48]{1,2,0:T(8,128)S(1)}, f32[2,384,48]{1,2,0:T(8,128)}, u32[]{:S(2)}) copy-start(f32[2,384,48]{1,2,0:T(8,128)} %param.34) | copy-start | bytes 442372
  7.2 28.6 %copy-start.21 = (f32[2,48,1536]{2,1,0:T(8,128)S(1)}, f32[2,48,1536]{2,1,0:T(8,128)}, u32[]{:S(2)}) copy-start(f32[2,48,1536]{2,1,0:T(8,128)} %param.35) | copy-start | bytes 1769476
  7.2 49.6 %copy-start = (bf16[256,768]{1,0:T(8,128)(2,1)S(1)}, bf16[256,768]{1,0:T(8,128)(2,1)}, u32[]{:S(2)}) copy-start(bf16[256,768]{1,0:T(8,128)(2,1)} %param.31) | copy-start | bytes 1179652
  7.2 84.9 %all-gather.21.cloned.1.call-start = ((), (), s32[]{:S(2)}) async-start(), calls=%async_computation.24 | async-start | bytes 1880064 | tf_op jit(solution)/shard_map/all_gather | solution.py:102
  9.1 161.2 %all-reduce.14.cloned.1.call-start = ((), (), s32[]{:S(2)}) async-start(), calls=%async_computation.10 | async-start | bytes 786432 | tf_op jit(solution)/shard_map/psum | solution.py:148
  57.0 37.7 %copy-start.82 = (f32[256]{0:T(256)}, f32[256]{0:T(256)S(1)}, u32[]{:S(2)}) copy-start(f32[256]{0:T(256)S(1)} %broadcast_multiply_fusion.11) | copy-start | bytes 3076
  57.3 37.5 %copy-start.97 = (f32[256]{0:T(256)}, f32[256]{0:T(256)S(1)}, u32[]{:S(2)}) copy-start(f32[256]{0:T(256)S(1)} %add_rsqrt_fusion.3) | copy-start | bytes 3076
  78.1 31.1 %copy-start.8 = (bf16[1,384,768]{1,2,0:T(8,128)(2,1)}, bf16[1,384,768]{1,2,0:T(8,128)(2,1)S(1)}, u32[]{:S(2)}) copy-start(bf16[1,384,768]{1,2,0:T(8,128)(2,1)S(1)} %all-gather.3) | copy-start | bytes 1769476
  110.4 39.5 %copy-start.59 = (bf16[1,384,48]{1,2,0:T(8,128)(2,1)S(1)}, bf16[1,384,48]{1,2,0:T(8,128)(2,1)}, u32[]{:S(2)}) copy-start(bf16[1,384,48]{1,2,0:T(8,128)(2,1)} %get-tuple-element.656) | copy-start | bytes 110596
  110.4 68.8 %all-gather.23.cloned.1.call-start = ((), (), s32[]{:S(2)}) async-start(), calls=%async_computation.25 | async-start | bytes 2506752 | tf_op jit(solution)/shard_map/all_gather | solution.py:104
  111.2 112.1 %all-gather.25.cloned.1.call-start = ((), (), s32[]{:S(2)}) async-start(), calls=%async_computation.26 | async-start | bytes 2506752 | tf_op jit(solution)/shard_map/all_gather | solution.py:105
  112.1 153.4 %all-gather.27.cloned.1.call-start = ((), (), s32[]{:S(2)}) async-start(), calls=%async_computation.27 | async-start | bytes 1880064 | tf_op jit(solution)/shard_map/all_gather | solution.py:102
  112.7 180.0 %all-reduce.16.cloned.1.call-start = ((), (), s32[]{:S(2)}) async-start(), calls=%async_computation.11 | async-start | bytes 786432 | tf_op jit(solution)/shard_map/psum | solution.py:155
  170.4 146.1 %copy-start.10 = (bf16[1,384,768]{1,2,0:T(8,128)(2,1)}, bf16[1,384,768]{1,2,0:T(8,128)(2,1)S(1)}, u32[]{:S(2)}) copy-start(bf16[1,384,768]{1,2,0:T(8,128)(2,1)S(1)} %all-gather.10) | copy-start | bytes 1769476
  182.9 43.6 %copy-start.23 = (bf16[256,1536]{1,0:T(8,128)(2,1)}, bf16[256,1536]{1,0:T(8,128)(2,1)S(1)}, u32[]{:S(2)}) copy-start(bf16[256,1536]{1,0:T(8,128)(2,1)S(1)} %get-tuple-element.669) | copy-start | bytes 2359300
  226.6 117.0 %all-reduce.18.cloned.1.call-start = ((), (), s32[]{:S(2)}) async-start(), calls=%async_computation.12 | async-start | bytes 786432 | tf_op jit(solution)/shard_map/psum | solution.py:148
  262.6 31.8 %copy-start.62 = (f32[768]{0:T(1024)}, f32[768]{0:T(1024)S(1)}, u32[]{:S(2)}) copy-start(f32[768]{0:T(1024)S(1)} %get-tuple-element.525) | copy-start | bytes 9220
  262.6 31.8 %copy-start.68 = (f32[768]{0:T(1024)}, f32[768]{0:T(1024)S(1)}, u32[]{:S(2)}) copy-start(f32[768]{0:T(1024)S(1)} %get-tuple-element.524) | copy-start | bytes 9220
  262.6 30.1 %copy-start.87 = (f32[768]{0:T(1024)S(1)}, f32[768]{0:T(1024)}, u32[]{:S(2)}) copy-start(f32[768]{0:T(1024)} %get-tuple-element.526) | copy-start | bytes 9220
  316.4 27.2 %copy-start.26 = (bf16[6,256,64]{1,2,0:T(8,128)(2,1)}, bf16[6,256,64]{1,2,0:T(8,128)(2,1)S(1)}, u32[]{:S(2)}) copy-start(bf16[6,256,64]{1,2,0:T(8,128)(2,1)S(1)} %get-tuple-element.195) | copy-start | bytes 589828
  316.4 28.3 %copy-start.13 = (bf16[6,256,64]{2,1,0:T(8,128)(2,1)}, bf16[6,256,64]{2,1,0:T(8,128)(2,1)S(1)}, u32[]{:S(2)}) copy-start(bf16[6,256,64]{2,1,0:T(8,128)(2,1)S(1)} %get-tuple-element.1032) | copy-start | bytes 589828
  316.4 28.3 %copy-start.86 = (f32[6,256]{1,0:T(8,128)}, f32[6,256]{1,0:T(8,128)S(1)}, u32[]{:S(2)}) copy-start(f32[6,256]{1,0:T(8,128)S(1)} %get-tuple-element.937) | copy-start | bytes 18436
  317.6 71.1 %all-gather.29.cloned.1.call-start = ((), (), s32[]{:S(2)}) async-start(), calls=%async_computation.28 | async-start | bytes 2506752 | tf_op jit(solution)/shard_map/all_gather | solution.py:104
  317.7 71.1 %copy-start.60 = (f32[768]{0:T(1024)S(1)}, f32[768]{0:T(1024)}, u32[]{:S(2)}) copy-start(f32[768]{0:T(1024)} %get-tuple-element.521) | copy-start | bytes 9220
  318.4 114.3 %all-gather.31.cloned.1.call-start = ((), (), s32[]{:S(2)}) async-start(), calls=%async_computation.29 | async-start | bytes 2506752 | tf_op jit(solution)/shard_map/all_gather | solution.py:105
  319.1 144.6 %all-reduce.20.cloned.1.call-start = ((), (), s32[]{:S(2)}) async-start(), calls=%async_computation.13 | async-start | bytes 786432 | tf_op jit(solution)/shard_map/psum | solution.py:199
  344.8 118.9 %copy-start.74 = (f32[256]{0:T(256)}, f32[256]{0:T(256)S(1)}, u32[]{:S(2)}) copy-start(f32[256]{0:T(256)S(1)} %broadcast_multiply_fusion.8) | copy-start | bytes 3076
  345.0 118.7 %copy-start.80 = (f32[256]{0:T(256)}, f32[256]{0:T(256)S(1)}, u32[]{:S(2)}) copy-start(f32[256]{0:T(256)S(1)} %add_rsqrt_fusion) | copy-start | bytes 3076
  388.8 43.9 %copy-start.31 = (bf16[256,768]{1,0:T(8,128)(2,1)S(1)}, bf16[256,768]{1,0:T(8,128)(2,1)}, u32[]{:S(2)}) copy-start(bf16[256,768]{1,0:T(8,128)(2,1)} %param.32) | copy-start | bytes 1179652
  439.0 113.0 %all-reduce.22.cloned.1.call-start = ((), (), s32[]{:S(2)}) async-start(), calls=%async_computation.14 | async-start | bytes 786432 | tf_op jit(solution)/shard_map/psum | solution.py:227
  526.1 28.0 %copy-start.3 = (f32[256,768]{1,0:T(8,128)S(1)}, f32[256,768]{1,0:T(8,128)}, u32[]{:S(2)}) copy-start(f32[256,768]{1,0:T(8,128)} %copy-done.2) | copy-start | bytes 2359300
  526.1 61.8 %all-reduce.24.cloned.1.call-start = ((), (), s32[]{:S(2)}) async-start(), calls=%async_computation.15 | async-start | bytes 786432 | tf_op jit(solution)/shard_map/psum | solution.py:199
  562.0 117.9 %all-reduce.26.cloned.1.call-start = ((), (), s32[]{:S(2)}) async-start(), calls=%async_computation.32 | async-start | bytes 1572864 | tf_op jit(solution)/shard_map/psum | solution.py:155
  645.2 34.6 %copy-start.66 = (f32[768]{0:T(1024)S(1)}, f32[768]{0:T(1024)}, u32[]{:S(2)}) copy-start(f32[768]{0:T(1024)} %copy-done.65) | copy-start | bytes 9220
  645.2 34.6 %copy-start.83 = (f32[256]{0:T(256)S(1)}, f32[256]{0:T(256)}, u32[]{:S(2)}) copy-start(f32[256]{0:T(256)} %copy-done.82) | copy-start | bytes 3076
  645.3 34.6 %copy-start.98 = (f32[256]{0:T(256)S(1)}, f32[256]{0:T(256)}, u32[]{:S(2)}) copy-start(f32[256]{0:T(256)} %copy-done.97) | copy-start | bytes 3076
  645.3 37.7 %copy-start.27 = (bf16[6,256,64]{1,2,0:T(8,128)(2,1)S(1)}, bf16[6,256,64]{1,2,0:T(8,128)(2,1)}, u32[]{:S(2)}) copy-start(bf16[6,256,64]{1,2,0:T(8,128)(2,1)} %copy-done.26) | copy-start | bytes 589828
  645.3 94.5 %reduce-scatter.37.cloned.1.call-start = ((), (), s32[]{:S(2)}) async-start(), calls=%async_computation.31 | async-start | bytes 417792
  651.2 157.1 %reduce-scatter.35.cloned.1.call-start = ((), (), s32[]{:S(2)}) async-start(), calls=%async_computation.30 | async-start | bytes 417792
  682.9 176.6 %reduce-scatter.25.cloned.1.call-start = ((), (), s32[]{:S(2)}) async-start(), calls=%async_computation.19 | async-start | bytes 1253376 | tf_op jit(solution)/shard_map/reduce_scatter | solution.py:257
  685.5 234.6 %reduce-scatter.23.cloned.1.call-start = ((), (), s32[]{:S(2)}) async-start(), calls=%async_computation.18 | async-start | bytes 1253376 | tf_op jit(solution)/shard_map/reduce_scatter | solution.py:257
  687.1 303.9 %reduce-scatter.21.cloned.1.call-start = ((), (), s32[]{:S(2)}) async-start(), calls=%async_computation.17 | async-start | bytes 3760128 | tf_op jit(solution)/shard_map/reduce_scatter | solution.py:256
  695.0 366.8 %reduce-scatter.19.cloned.1.call-start = ((), (), s32[]{:S(2)}) async-start(), calls=%async_computation.16 | async-start | bytes 3760128 | tf_op jit(solution)/shard_map/reduce_scatter | solution.py:256
  701.0 439.0 %reduce-scatter.33.cloned.1.call-start = ((), (), s32[]{:S(2)}) async-start(), calls=%async_computation.23 | async-start | bytes 5013504 | tf_op jit(solution)/shard_map/reduce_scatter | solution.py:259
  705.2 513.5 %reduce-scatter.31.cloned.1.call-start = ((), (), s32[]{:S(2)}) async-start(), calls=%async_computation.22 | async-start | bytes 5013504 | tf_op jit(solution)/shard_map/reduce_scatter | solution.py:259
  710.5 586.9 %reduce-scatter.29.cloned.1.call-start = ((), (), s32[]{:S(2)}) async-start(), calls=%async_computation.21 | async-start | bytes 5013504 | tf_op jit(solution)/shard_map/reduce_scatter | solution.py:258
  714.8 661.2 %reduce-scatter.27.cloned.1.call-start = ((), (), s32[]{:S(2)}) async-start(), calls=%async_computation.20 | async-start | bytes 5013504 | tf_op jit(solution)/shard_map/reduce_scatter | solution.py:258
  721.9 83.6 %copy-start.56 = (bf16[256,768]{1,0:T(8,128)(2,1)S(1)}, bf16[256,768]{1,0:T(8,128)(2,1)}, u32[]{:S(2)}) copy-start(bf16[256,768]{1,0:T(8,128)(2,1)} %get-tuple-element.596) | copy-start | bytes 1179652
  721.9 85.1 %copy-start.33 = (bf16[256,768]{1,0:T(8,128)(2,1)S(1)}, bf16[256,768]{1,0:T(8,128)(2,1)}, u32[]{:S(2)}) copy-start(bf16[256,768]{1,0:T(8,128)(2,1)} %get-tuple-element.597) | copy-start | bytes 1179652
  722.0 85.1 %copy-start.67 = (f32[768]{0:T(1024)S(1)}, f32[768]{0:T(1024)}, u32[]{:S(2)}) copy-start(f32[768]{0:T(1024)} %copy-done.65) | copy-start | bytes 9220
  741.3 65.7 %copy-start.84 = (f32[256]{0:T(256)S(1)}, f32[256]{0:T(256)}, u32[]{:S(2)}) copy-start(f32[256]{0:T(256)} %copy-done.82) | copy-start | bytes 3076
  741.4 65.7 %copy-start.99 = (f32[256]{0:T(256)S(1)}, f32[256]{0:T(256)}, u32[]{:S(2)}) copy-start(f32[256]{0:T(256)} %copy-done.97) | copy-start | bytes 3076
  807.1 113.0 %copy-start.53 = (f32[2,384,48]{1,2,0:T(8,128)S(1)}, f32[2,384,48]{1,2,0:T(8,128)}, u32[]{:S(2)}) copy-start(f32[2,384,48]{1,2,0:T(8,128)} %param.34) | copy-start | bytes 442372
  807.1 113.0 %copy-start.57 = (f32[2,384,48]{1,2,0:T(8,128)S(1)}, f32[2,384,48]{1,2,0:T(8,128)}, u32[]{:S(2)}) copy-start(f32[2,384,48]{1,2,0:T(8,128)} %param.41) | copy-start | bytes 442372
  807.1 113.0 %copy-start.58 = (f32[2,384,48]{1,2,0:T(8,128)S(1)}, f32[2,384,48]{1,2,0:T(8,128)}, u32[]{:S(2)}) copy-start(f32[2,384,48]{1,2,0:T(8,128)} %param.48) | copy-start | bytes 442372
  807.2 254.6 %copy-start.30 = (f32[2,48,3,384]{3,1,2,0:T(8,128)S(1)}, f32[2,48,3,384]{3,1,2,0:T(8,128)}, u32[]{:S(2)}) copy-start(f32[2,48,3,384]{3,1,2,0:T(8,128)} %param.33) | copy-start | bytes 1327108
  808.4 253.4 %copy-start.54 = (f32[2,48,3,384]{3,1,2,0:T(8,128)S(1)}, f32[2,48,3,384]{3,1,2,0:T(8,128)}, u32[]{:S(2)}) copy-start(f32[2,48,3,384]{3,1,2,0:T(8,128)} %param.40) | copy-start | bytes 1327108
  808.4 253.4 %copy-start.55 = (f32[2,48,3,384]{3,1,2,0:T(8,128)S(1)}, f32[2,48,3,384]{3,1,2,0:T(8,128)}, u32[]{:S(2)}) copy-start(f32[2,48,3,384]{3,1,2,0:T(8,128)} %param.47) | copy-start | bytes 1327108
  1061.8 156.9 %copy-start.20 = (f32[2,1536,48]{1,2,0:T(8,128)S(1)}, f32[2,1536,48]{1,2,0:T(8,128)}, u32[]{:S(2)}) copy-start(f32[2,1536,48]{1,2,0:T(8,128)} %param.36) | copy-start | bytes 1769476
  1061.8 156.9 %copy-start.48 = (f32[2,1536,48]{1,2,0:T(8,128)S(1)}, f32[2,1536,48]{1,2,0:T(8,128)}, u32[]{:S(2)}) copy-start(f32[2,1536,48]{1,2,0:T(8,128)} %param.43) | copy-start | bytes 1769476
  1061.8 156.9 %copy-start.49 = (f32[2,1536,48]{1,2,0:T(8,128)S(1)}, f32[2,1536,48]{1,2,0:T(8,128)}, u32[]{:S(2)}) copy-start(f32[2,1536,48]{1,2,0:T(8,128)} %param.50) | copy-start | bytes 1769476
  1218.7 157.3 %copy-start.22 = (f32[2,48,1536]{2,1,0:T(8,128)S(1)}, f32[2,48,1536]{2,1,0:T(8,128)}, u32[]{:S(2)}) copy-start(f32[2,48,1536]{2,1,0:T(8,128)} %param.35) | copy-start | bytes 1769476
  1218.7 157.3 %copy-start.50 = (f32[2,48,1536]{2,1,0:T(8,128)S(1)}, f32[2,48,1536]{2,1,0:T(8,128)}, u32[]{:S(2)}) copy-start(f32[2,48,1536]{2,1,0:T(8,128)} %param.42) | copy-start | bytes 1769476
  1218.7 157.3 %copy-start.51 = (f32[2,48,1536]{2,1,0:T(8,128)S(1)}, f32[2,48,1536]{2,1,0:T(8,128)}, u32[]{:S(2)}) copy-start(f32[2,48,1536]{2,1,0:T(8,128)} %param.49) | copy-start | bytes 1769476
  (67 other events, 267.8 us)
Sparse Core Ops, SparseCore 0:
  10.9 44.3 all-gather.20
  110.5 23.0 all-reduce.13
  136.5 42.6 all-gather.22
  181.9 41.3 all-gather.24
  226.1 39.3 all-gather.26
  268.2 24.4 all-reduce.15
  317.8 25.7 all-reduce.17
  346.4 42.3 all-gather.28
  391.6 41.0 all-gather.30
  439.2 24.4 all-reduce.19
  526.2 25.7 all-reduce.21
  562.1 25.7 all-reduce.23
  645.4 34.3 all-reduce.25
  683.8 55.9 reduce-scatter.36
  743.7 54.9 reduce-scatter.34
  802.2 57.1 reduce-scatter.24
  862.9 57.1 reduce-scatter.22
  923.8 67.1 reduce-scatter.20
  994.8 66.8 reduce-scatter.18
  1065.5 74.4 reduce-scatter.32
  1143.9 74.7 reduce-scatter.30
  1222.5 74.7 reduce-scatter.28
  1301.2 74.7 reduce-scatter.26
where the time goes:
time: 1400 us; the launch traced here: 1390 us
  waiting for transfers between devices  832 us (59%)
  blocking collectives  222 us (16%)
  matrix products  155 us (11%)
  local copies, waits for them, and re-layouts  83.9 us (6%)
  other arithmetic  74.8 us (5%)
  between operations  16.4 us (1%)
    reduce_scatter x2, waiting for transfers between devices, scatter_layer(): lax.psum_scatter(grad_up, 'fsdp', scatter_dimension=0, tiled=True)  155 us
    reduce_scatter x2, waiting for transfers between devices, scatter_layer(): lax.psum_scatter(grad_down, 'fsdp', scatter_dimension=1, tiled=True)  154 us
    reduce_scatter x2, waiting for transfers between devices, scatter_layer(): lax.psum_scatter(grad_qkv, 'fsdp', scatter_dimension=0, tiled=True)  140 us
    reduce_scatter x2, waiting for transfers between devices, scatter_layer(): lax.psum_scatter(grad_wout, 'fsdp', scatter_dimension=1, tiled=True)  108 us
    all_gather x2, waiting for transfers between devices, fetch_forward(): lax.all_gather(piece_down, 'fsdp', axis=1, tiled=True)  80.3 us
    unnamed x1, blocking collectives  59.5 us
    psum x2, waiting for transfers between devices, layer_forward(): lax.psum(column_terms.astype(jnp.bfloat16), 'tp').astype(jnp.float32)  51.6 us
    all_gather x2, waiting for transfers between devices, fetch_forward(): lax.all_gather(piece_up, 'fsdp', axis=0, tiled=True)  49.8 us
  transfers between devices with their start and end apart: 23, of which 20 were waited for; matrix products, arithmetic and copies ran while one was open for 9% of the time, Pallas kernels for 0%

commit v1 on v0

v1 whole, which is shorter than its diff:
```python
import functools
import jax
import jax.numpy as jnp
from jax import lax
from jax.experimental import pallas as pl
from jax.experimental.pallas import tpu as pltpu
from jax.sharding import PartitionSpec as P

HD = 64
SEQ = 256
STEP = 3

norm_eps = 1e-05
beta_one = 0.9
beta_two = 0.999
adam_eps = 1e-08
decay_rate = 0.1
rate_matrix = 0.01
rate_vector = 0.2
root_half = 0.7071067811865476
inv_root_two_pi = 0.3989422804014327

BF = jnp.bfloat16
F32 = jnp.float32
NN = (((1,), (0,)), ((), ()))
NT = (((1,), (1,)), ((), ()))
TN = (((0,), (0,)), ((), ()))
MESH = pl.DeviceIdType.MESH
LANES = 128
BIAS_ROWS = 16
VEC_ROWS = 8


def mm(left, right, dims):
    return lax.dot_general(left, right, dims, preferred_element_type=F32)


def factor_axes(count):
    chips = count // 2
    sizes = []
    while chips > 1:
        step = 4 if chips % 4 == 0 else 2 if chips % 2 == 0 else chips
        sizes.append(step)
        chips //= step
    return tuple(sizes) + (2,)


class Plan:
    def __init__(self, count, rows, width, half, hidden, layers):
        self.count = count
        self.axes = factor_axes(count)
        strides = []
        stride = count
        for size in self.axes:
            stride //= size
            strides.append(stride)
        self.strides = tuple(strides)
        self.rows = rows
        self.width = width
        self.own = width // count
        self.block = -(-self.own // 16) * 16
        self.padded = self.block * count
        self.half = half
        self.pairs = half // LANES
        self.layers = layers
        self.piece = 2 * half
        self.up_pieces = hidden // self.piece
        self.pieces = 2 + 2 * self.up_pieces
        self.quarter = HD // count
        self.heads = half // HD
        self.bias_cols = 2 * half + hidden
        self.slots = sum(size - 1 for size in self.axes)
        self.chunk = rows // 2


def train_kernel(
    plan,
    frames_ref,
    cot_ref,
    shard_ref,
    small_ref,
    out_ref,
    gin_ref,
    gout_ref,
    smallg_ref,
    W,
    SB,
    VEC,
    BIAS,
    XS,
    XR,
    MID,
    ACC,
    LAST,
    HAT,
    INV,
    ACT,
    Q,
    K,
    V,
    LSE,
    CTX,
    SLOPE,
    HIDDEN,
    DX,
    LOW,
    FL,
    DCTX,
    RQK,
    RV,
    VG,
    BG,
    TURN,
    SG,
    RBs,
    RSs,
    ag_send,
    ag_recv,
    rs_send,
    rs_recv,
    x_send,
    x_recv,
):
    axes = plan.axes
    depth = len(axes)
    rp = plan.block
    Dp = plan.padded
    L = plan.layers
    NP = plan.pieces
    UP = plan.up_pieces
    half = plan.half
    rows = plan.rows
    chunk = plan.chunk

    me = lax.axis_index("fsdp")
    side = lax.axis_index("tp")
    digit = [lax.rem(me // stride, size) for stride, size in zip(plan.strides, axes)]
    offsets = []
    total = 0
    for size in axes:
        offsets.append(total)
        total += size - 1

    def peer(k, j):
        value = lax.rem(digit[k] + j, axes[k])
        return value, (me + (value - digit[k]) * plan.strides[k], side)

    def source(k, j):
        return lax.rem(digit[k] - j + axes[k], axes[k])

    def place(k, value):
        return (slice(None),) * k + (value,) + tuple(digit[k + 1 :])

    other = (me, 1 - side)

    barrier = pltpu.get_barrier_semaphore()
    greeted = 1
    pl.semaphore_signal(barrier, inc=1, device_id=other, device_id_type=MESH)
    for k in range(depth):
        for j in range(1, axes[k]):
            pl.semaphore_signal(barrier, inc=1, device_id=peer(k, j)[1], device_id_type=MESH)
            greeted += 1
    pl.semaphore_wait(barrier, greeted)

    def remote(src, dst, send, recv, device):
        return pltpu.make_async_remote_copy(
            src_ref=src,
            dst_ref=dst,
            send_sem=send,
            recv_sem=recv,
            device_id=device,
            device_id_type=MESH,
        )

    small_index = L * NP

    def gather_copy(k, j, piece, small, sending):
        slot = offsets[k] + j - 1
        value, device = peer(k, j)
        spot = place(k, digit[k]) if sending else place(k, source(k, j))
        if small:
            dst = SB.at[spot]
            src = small_ref if (k == 0 and sending) else dst
        else:
            dst = W.at[(piece,) + spot]
            src = shard_ref.at[piece] if (k == 0 and sending) else dst
        return remote(src, dst, ag_send.at[piece, slot], ag_recv.at[piece, slot], device)

    def gather_start(k, piece, small=False):
        for j in range(1, axes[k]):
            gather_copy(k, j, piece, small, True).start()

    def gather_wait(k, piece, small=False):
        for j in range(1, axes[k]):
            gather_copy(k, j, piece, small, False).wait_recv()

    def gather_drain(piece, small=False):
        for k in range(depth):
            for j in range(1, axes[k]):
                gather_copy(k, j, piece, small, True).wait_send()

    def ready(piece):
        @pl.when(piece + 1 < L * NP)
        def _():
            gather_wait(0, piece + 1)
            gather_start(1, piece + 1)

        for k in range(1, depth):
            gather_wait(k, piece)
            if k + 1 < depth:
                gather_start(k + 1, piece)

    here = tuple(digit)
    SB[here] = small_ref[...]
    gather_start(0, small_index, True)
    for piece in range(L * NP):
        gather_start(0, piece)
    for piece in range(L * NP):
        W[(piece,) + here] = shard_ref[piece]

    gather_wait(0, small_index, True)
    for k in range(1, depth):
        gather_start(k, small_index, True)
        gather_wait(k, small_index, True)
    gather_wait(0, 0)
    gather_start(1, 0)

    vec_all = SB[(slice(None),) * depth + (slice(0, rp), slice(None))]
    vec_rows = vec_all.reshape(Dp, LANES).astype(F32).T
    for layer in range(L):
        VEC[layer] = vec_rows[layer * VEC_ROWS : (layer + 1) * VEC_ROWS]
    every = L * plan.bias_cols
    shift = HD.bit_length() - 1

    def static_place(owner):
        return tuple((owner // stride) % size for stride, size in zip(plan.strides, axes))

    def column_ids(lines):
        return lax.broadcasted_iota(jnp.int32, (lines, every), 1)

    def line_ids(lines):
        return lax.broadcasted_iota(jnp.int32, (lines, every), 0)

    def group_match():
        return lax.shift_right_logical(column_ids(LANES), shift) == line_ids(LANES)

    def feature_match(lines):
        return (column_ids(lines) & (HD - 1)) == line_ids(lines)

    for owner in range(plan.count):
        held = SB[static_place(owner) + (slice(rp, rp + BIAS_ROWS), slice(None))].astype(F32)
        low = owner * plan.quarter
        TURN[low : low + plan.quarter] = held[0 : plan.quarter]
    spread = mm(TURN[0:HD].astype(BF), group_match().astype(F32).astype(BF), NN)
    bias_row = jnp.sum(jnp.where(feature_match(HD), spread, 0.0), axis=0, keepdims=True)
    for layer in range(L):
        BIAS[layer] = bias_row[:, layer * plan.bias_cols : (layer + 1) * plan.bias_cols]

    if plan.block != plan.own:
        column = lax.broadcasted_iota(jnp.int32, (1, Dp), 1)
        valid = (lax.rem(column, rp) < plan.own).astype(F32)
    else:
        valid = None

    def average(values):
        return jnp.sum(values, axis=-1, keepdims=True) * (1.0 / plan.width)

    def masked(values):
        return values if valid is None else values * valid

    def piece_of(index, low=0, high=None):
        high = plan.piece if high is None else high
        tail = (slice(None), slice(low, high))
        return W[(index,) + (slice(None),) * depth + tail].reshape(Dp, high - low)

    def norm_forward(values, layer, which, region):
        centred = masked(values - average(values))
        inverse = lax.rsqrt(average(centred * centred) + norm_eps)
        hat = centred * inverse
        HAT[layer, which, region] = hat
        INV[layer, which, region] = inverse
        gain = VEC[layer, 2 * which : 2 * which + 1]
        shift = VEC[layer, 2 * which + 1 : 2 * which + 2]
        ACT[layer, which, region] = (hat * gain + shift).astype(BF)

    def exchange_copy(number, slot, part):
        region = pl.ds(part * chunk, chunk)
        return remote(
            XS.at[slot, region],
            XR.at[slot, region],
            x_send.at[number, part],
            x_recv.at[number, part],
            other,
        )

    def exchange_send(number, slot, part, values):
        XS[slot, pl.ds(part * chunk, chunk)] = values.astype(BF)
        exchange_copy(number, slot, part).start()

    def exchange_sum(number, slot, part):
        exchange_copy(number, slot, part).wait_recv()
        region = pl.ds(part * chunk, chunk)
        result = XS[slot, region].astype(F32) + XR[slot, region].astype(F32)
        return result

    def exchange_done(number, slot):
        for part in range(2):
            exchange_copy(number, slot, part).wait_send()

    lane = lax.broadcasted_iota(jnp.int32, (1, LANES), 1)
    head_mask = [((lane // HD) == h).astype(F32).astype(BF) for h in range(LANES // HD)]
    scale = HD ** (-0.5)
    clips = rows // SEQ

    def attend(layer):
        def one(item, _):
            pair = item // clips
            clip = lax.rem(item, clips)
            span = pl.ds(clip * SEQ, SEQ)
            query = Q[layer, pair, span]
            key = K[layer, pair, span]
            value = V[layer, pair, span]
            total = None
            for h, mask in enumerate(head_mask):
                scores = mm(query * mask, key, NT) * scale
                highest = jnp.max(scores, axis=1, keepdims=True)
                logsum = highest + jnp.log(jnp.sum(jnp.exp(scores - highest), axis=1, keepdims=True))
                LSE[layer, pair, h, span] = logsum
                weights = jnp.exp(scores - logsum).astype(BF)
                part = mm(weights, value * mask, NN)
                total = part if total is None else total + part
            CTX[layer, pair, span] = total.astype(BF)
            return 0

        lax.fori_loop(0, plan.pairs * clips, one, 0)

    def context_of(layer, region=slice(None)):
        return jnp.concatenate([CTX[layer, pair, region] for pair in range(plan.pairs)], axis=1)

    def forward_layer(layer, carry):
        first = layer * NP

        @pl.when(layer == 0)
        def _():
            value = frames_ref[...].astype(F32)
            DX[...] = value
            norm_forward(value, layer, 0, slice(None))

        @pl.when(layer > 0)
        def _():
            for part in range(2):
                region = pl.ds(part * chunk, chunk)
                value = MID[region] + exchange_sum(2 * layer - 1, 1, part) + VEC[layer - 1, 5:6]
                DX[region] = value
                norm_forward(value, layer, 0, region)
            exchange_done(2 * layer - 1, 1)

        ready(first)
        both = mm(ACT[layer, 0], piece_of(first), NN)
        for pair in range(plan.pairs):
            low = pair * LANES
            query = both[:, low : low + LANES] + BIAS[layer, :, low : low + LANES]
            Q[layer, pair] = query.astype(BF)
            K[layer, pair] = both[:, half + low : half + low + LANES].astype(BF)
        ready(first + 1)
        values = mm(ACT[layer, 0], piece_of(first + 1, 0, half), NN)
        for pair in range(plan.pairs):
            low = pair * LANES
            bias = BIAS[layer, :, half + low : half + low + LANES]
            V[layer, pair] = (values[:, low : low + LANES] + bias).astype(BF)
        attend(layer)
        for part in range(2):
            region = pl.ds(part * chunk, chunk)
            heads = context_of(layer, region)
            exchange_send(2 * layer, 0, part, mm(heads, piece_of(first + 1, half), NT))
        for number in range(UP):
            ready(first + 2 + number)
        for part in range(2):
            region = pl.ds(part * chunk, chunk)
            value = DX[region] + exchange_sum(2 * layer, 0, part) + VEC[layer, 4:5]
            MID[region] = value
            norm_forward(value, layer, 1, region)
        exchange_done(2 * layer, 0)
        for number in range(UP):
            before = mm(ACT[layer, 1], piece_of(first + 2 + number), NN)
            low = 2 * half + number * plan.piece
            before = before + BIAS[layer, :, low : low + plan.piece]
            bell = 0.5 * (1.0 + lax.erf(before * root_half))
            HIDDEN[layer, number] = (before * bell).astype(BF)
            slope = bell + before * jnp.exp(-0.5 * before * before) * inv_root_two_pi
            SLOPE[layer, number] = slope.astype(BF)
        for number in range(UP):
            ready(first + 2 + UP + number)
            term = mm(HIDDEN[layer, number], piece_of(first + 2 + UP + number), NT)
            if number + 1 < UP:
                ACC[...] = term if number == 0 else ACC[...] + term
            else:
                whole = term + ACC[...] if UP > 1 else term

                @pl.when(layer + 1 < L)
                def _():
                    for part in range(2):
                        exchange_send(2 * layer + 1, 1, part, whole[part * chunk : (part + 1) * chunk])

                @pl.when(layer + 1 == L)
                def _():
                    LAST[...] = whole.astype(BF)

        return carry

    lax.fori_loop(0, L, forward_layer, 0)

    def landing(k, piece):
        return lax.rem(piece, NP) if k == depth - 1 else piece

    def scatter_copy(k, j, piece, small):
        slot = offsets[k] + j - 1
        value, device = peer(k, j)
        spot = place(k, value)
        if small:
            src = SG.at[spot]
            dst = RSs[k].at[j - 1]
        else:
            src = W.at[(piece,) + spot]
            dst = RBs[k].at[landing(k, piece), j - 1]
        return remote(src, dst, rs_send.at[piece, slot], rs_recv.at[piece, slot], device)

    def scatter_start(k, piece, small=False):
        for j in range(1, axes[k]):
            scatter_copy(k, j, piece, small).start()

    def scatter_wait(k, piece, small=False):
        for j in range(1, axes[k]):
            scatter_copy(k, j, piece, small).wait_recv()

    def scatter_step(k, piece, small=False):
        scatter_wait(k, piece, small)
        spot = place(k, digit[k])
        if small:
            value = SG[spot]
            for j in range(1, axes[k]):
                value = value + RSs[k][j - 1]
            if k == 0:
                smallg_ref[...] = value
            else:
                SG[spot] = value
                scatter_start(k - 1, piece, True)
        else:
            value = W[(piece,) + spot].astype(F32)
            for j in range(1, axes[k]):
                value = value + RBs[k][landing(k, piece), j - 1].astype(F32)
            if k == 0:
                gout_ref[piece] = value
            else:
                W[(piece,) + spot] = value.astype(BF)
                scatter_start(k - 1, piece)

    def scatter_drain(piece, small=False):
        for k in range(depth):
            for j in range(1, axes[k]):
                scatter_copy(k, j, piece, small).wait_send()

    block_shape = axes + (rp,)

    def put_gradient(index, value, low=0, high=None):
        high = plan.piece if high is None else high
        tail = (slice(None), slice(low, high))
        W[(index,) + (slice(None),) * depth + tail] = value.astype(BF).reshape(block_shape + (high - low,))

    for piece in range(L * NP):
        gather_drain(piece)
    gather_drain(small_index, True)

    def attend_back(layer):
        def one(item, _):
            pair = item // clips
            clip = lax.rem(item, clips)
            span = pl.ds(clip * SEQ, SEQ)
            query = Q[layer, pair, span]
            key = K[layer, pair, span]
            value = V[layer, pair, span]
            upper = DCTX[pair, span]
            grad_q = grad_k = grad_v = None
            for h, mask in enumerate(head_mask):
                scores = mm(query * mask, key, NT) * scale
                probs = jnp.exp(scores - LSE[layer, pair, h, span])
                weights = probs.astype(BF)
                up_head = upper * mask
                part_v = mm(weights, up_head, TN)
                grad_p = mm(up_head, value, NT)
                inner = jnp.sum(probs * grad_p, axis=1, keepdims=True)
                grad_s = (probs * (grad_p - inner) * scale).astype(BF)
                part_q = mm(grad_s, key * mask, NN)
                part_k = mm(grad_s, query * mask, TN)
                grad_q = part_q if grad_q is None else grad_q + part_q
                grad_k = part_k if grad_k is None else grad_k + part_k
                grad_v = part_v if grad_v is None else grad_v + part_v
            low = pl.ds(pl.multiple_of(pair * LANES, LANES), LANES)
            next_low = pl.ds(pl.multiple_of(half + pair * LANES, LANES), LANES)
            RQK[span, low] = grad_q.astype(BF)
            RQK[span, next_low] = grad_k.astype(BF)
            RV[span, low] = grad_v.astype(BF)
            sum_q = jnp.sum(grad_q, axis=0, keepdims=True)
            sum_v = jnp.sum(grad_v, axis=0, keepdims=True)

            @pl.when(clip == 0)
            def _():
                BG[layer, :, low] = sum_q
                BG[layer, :, next_low] = sum_v

            @pl.when(clip > 0)
            def _():
                BG[layer, :, low] += sum_q
                BG[layer, :, next_low] += sum_v

            return 0

        lax.fori_loop(0, plan.pairs * clips, one, 0)

    def column_sum(values):
        return jnp.sum(values, axis=0, keepdims=True)

    def norm_backward(upper, layer, which, region):
        hat = HAT[layer, which, region]
        scaled = upper * VEC[layer, 2 * which : 2 * which + 1]
        return INV[layer, which, region] * (
            masked(scaled - average(scaled)) - hat * average(scaled * hat)
        )

    def keep_rows(layer, line, part, value):
        if part == 0:
            VG[layer, line : line + 1] = value
        else:
            VG[layer, line : line + 1] += value

    DX[...] = cot_ref[...].astype(F32)
    DMID = ACC

    def produced(m):
        step = m // NP
        turn = lax.rem(m, NP)
        name = jnp.where(
            turn < UP,
            2 + UP + turn,
            jnp.where(turn < 2 * UP, 2 + turn - UP, NP - 1 - turn),
        )
        return (L - 1 - step) * NP + name

    def pump(m, carry):
        for k in range(depth - 2, -1, -1):
            earlier = m - (depth - 2 - k)

            @pl.when((earlier >= 0) & (earlier < L * NP))
            def _():
                scatter_step(k, produced(earlier))

        return carry

    def pumped(step, place_in_layer):
        counts = PUMPS[place_in_layer]
        value = counts[0]
        for s in range(1, L):
            value = jnp.where(step == s, counts[min(s, len(counts) - 1)], value)
        return jnp.minimum(value, L * NP)

    def pump_to(step, place_in_layer):
        if place_in_layer == 0:
            low = jnp.where(step == 0, 0, pumped(step - 1, len(PUMPS) - 1))
        else:
            low = pumped(step, place_in_layer - 1)
        lax.fori_loop(low, pumped(step, place_in_layer), pump, 0)

    def backward_layer(step, carry):
        layer = L - 1 - step
        first = layer * NP
        up = first + 2
        down = first + 2 + UP
        number_up = 2 * L + 2 * step
        VG[layer] = jnp.zeros((VEC_ROWS, Dp), F32)
        upper = DX[...]
        VG[layer, 5:6] = column_sum(upper)
        LOW[...] = upper.astype(BF)
        for number in range(UP):
            grad = mm(LOW[...], piece_of(down + number), NN) * SLOPE[layer, number].astype(F32)
            low = 2 * half + number * plan.piece
            BG[layer, :, low : low + plan.piece] = column_sum(grad)
            FL[number] = grad.astype(BF)
            put_gradient(down + number, mm(LOW[...], HIDDEN[layer, number], TN))
            scatter_start(depth - 1, down + number)
        for part in range(2):
            region = pl.ds(part * chunk, chunk)
            whole = None
            for number in range(UP):
                term = mm(FL[number, region], piece_of(up + number), NT)
                whole = term if whole is None else whole + term
            exchange_send(number_up, 1, part, whole)
        for number in range(UP):
            scatter_step(depth - 1, down + number)
        for number in range(UP):
            put_gradient(up + number, mm(ACT[layer, 1], FL[number], TN))
            scatter_start(depth - 1, up + number)
        for number in range(UP):
            scatter_step(depth - 1, up + number)
        pump_to(step, 0)
        for part in range(2):
            region = pl.ds(part * chunk, chunk)
            grad = exchange_sum(number_up, 1, part)
            keep_rows(layer, 2, part, column_sum(grad * HAT[layer, 1, region]))
            keep_rows(layer, 3, part, column_sum(grad))
            grad_mid = DX[region] + norm_backward(grad, layer, 1, region)
            DMID[region] = grad_mid
            keep_rows(layer, 4, part, column_sum(grad_mid))
            LOW[region] = grad_mid.astype(BF)
        exchange_done(number_up, 1)
        heads = mm(LOW[...], piece_of(first + 1, half), NN)
        for pair in range(plan.pairs):
            DCTX[pair] = heads[:, pair * LANES : (pair + 1) * LANES].astype(BF)
        put_gradient(first + 1, mm(LOW[...], context_of(layer), TN), half)
        attend_back(layer)
        for part in range(2):
            region = pl.ds(part * chunk, chunk)
            whole = mm(RQK[region], piece_of(first), NT)
            whole = whole + mm(RV[region], piece_of(first + 1, 0, half), NT)
            exchange_send(number_up + 1, 0, part, whole)
        put_gradient(first + 1, mm(ACT[layer, 0], RV[...], TN), 0, half)
        scatter_start(depth - 1, first + 1)
        put_gradient(first, mm(ACT[layer, 0], RQK[...], TN))
        scatter_start(depth - 1, first)
        pump_to(step, 1)
        scatter_step(depth - 1, first + 1)
        scatter_step(depth - 1, first)
        pump_to(step, 2)

        @pl.when(step + 1 == L)
        def _():
            pack_biases()

        for part in range(2):
            region = pl.ds(part * chunk, chunk)
            grad = exchange_sum(number_up + 1, 0, part)
            keep_rows(layer, 0, part, column_sum(grad * HAT[layer, 0, region]))
            keep_rows(layer, 1, part, column_sum(grad))
            DX[region] = DMID[region] + norm_backward(grad, layer, 0, region)
        exchange_done(number_up + 1, 0)
        return carry

    def pack_biases():
        row = jnp.concatenate([BG[layer] for layer in range(L)], axis=1)
        wide = jnp.where(group_match(), row, 0.0)
        high = wide.astype(BF)
        low = (wide - high.astype(F32)).astype(BF)
        select = feature_match(LANES).astype(F32).astype(BF)
        table = (mm(high, select, NT) + mm(low, select, NT)).T
        for owner in range(plan.count):
            start = owner * plan.quarter
            spot = static_place(owner) + (slice(rp, rp + plan.quarter), slice(None))
            SG[spot] = table[start : start + plan.quarter]

    SG[...] = jnp.zeros(SG.shape, F32)
    lax.fori_loop(0, L, backward_layer, 0)

    lines = [VG[layer] for layer in range(L)]
    lines.append(jnp.zeros((LANES - L * VEC_ROWS, Dp), F32))
    turned = jnp.concatenate(lines, axis=0).T.reshape(axes + (rp, LANES))
    SG[(slice(None),) * depth + (slice(0, rp), slice(None))] = turned
    scatter_start(depth - 1, small_index, True)
    for part in range(2):
        exchange_send(2 * L - 1, 1, part, LAST[pl.ds(part * chunk, chunk)])
    gin_ref[...] = DX[...]
    scatter_step(depth - 1, small_index, True)
    for part in range(2):
        region = pl.ds(part * chunk, chunk)
        value = MID[region] + exchange_sum(2 * L - 1, 1, part) + VEC[L - 1, 5:6]
        out_ref[region] = value.astype(BF)
    exchange_done(2 * L - 1, 1)
    lax.fori_loop(pumped(L - 1, len(PUMPS) - 1), L * NP + depth - 2, pump, 0)
    for k in range(depth - 2, -1, -1):
        scatter_step(k, small_index, True)
    for piece in range(L * NP):
        scatter_drain(piece)
    scatter_drain(small_index, True)


PUMPS = ((1, 5), (2, 7), (3, 8))


def run_kernel(plan, frames, cotangent, shards, small):
    L, NP, Dp, rp, rows = plan.layers, plan.pieces, plan.padded, plan.block, plan.rows
    axes = plan.axes
    depth = len(axes)
    UP = plan.up_pieces
    piece = plan.piece
    landings = []
    small_landings = []
    for k, size in enumerate(axes):
        number = NP if k == depth - 1 else L * NP
        landings.append(pltpu.VMEM((number, size - 1) + axes[:k] + (rp, piece), BF))
        small_landings.append(pltpu.VMEM((size - 1,) + axes[:k] + (rp + BIAS_ROWS, LANES), F32))
    scratch = [
        pltpu.VMEM((L * NP,) + axes + (rp, piece), BF),
        pltpu.VMEM(axes + (rp + BIAS_ROWS, LANES), BF),
        pltpu.VMEM((L, VEC_ROWS, Dp), F32),
        pltpu.VMEM((L, 1, plan.bias_cols), F32),
        pltpu.VMEM((2, rows, Dp), BF),
        pltpu.VMEM((2, rows, Dp), BF),
        pltpu.VMEM((rows, Dp), F32),
        pltpu.VMEM((rows, Dp), F32),
        pltpu.VMEM((rows, Dp), BF),
        pltpu.VMEM((L, 2, rows, Dp), F32),
        pltpu.VMEM((L, 2, rows, 1), F32),
        pltpu.VMEM((L, 2, rows, Dp), BF),
        pltpu.VMEM((L, plan.pairs, rows, LANES), BF),
        pltpu.VMEM((L, plan.pairs, rows, LANES), BF),
        pltpu.VMEM((L, plan.pairs, rows, LANES), BF),
        pltpu.VMEM((L, plan.pairs, LANES // HD, rows, 1), F32),
        pltpu.VMEM((L, plan.pairs, rows, LANES), BF),
        pltpu.VMEM((L, UP, rows, piece), BF),
        pltpu.VMEM((L, UP, rows, piece), BF),
        pltpu.VMEM((rows, Dp), F32),
        pltpu.VMEM((rows, Dp), BF),
        pltpu.VMEM((UP, rows, piece), BF),
        pltpu.VMEM((plan.pairs, rows, LANES), BF),
        pltpu.VMEM((rows, piece), BF),
        pltpu.VMEM((rows, plan.half), BF),
        pltpu.VMEM((L, VEC_ROWS, Dp), F32),
        pltpu.VMEM((L, 1, plan.bias_cols), F32),
        pltpu.VMEM((HD, LANES), F32),
        pltpu.VMEM(axes + (rp + BIAS_ROWS, LANES), F32),
        landings,
        small_landings,
        pltpu.SemaphoreType.DMA((L * NP + 1, plan.slots)),
        pltpu.SemaphoreType.DMA((L * NP + 1, plan.slots)),
        pltpu.SemaphoreType.DMA((L * NP + 1, plan.slots)),
        pltpu.SemaphoreType.DMA((L * NP + 1, plan.slots)),
        pltpu.SemaphoreType.DMA((4 * L, 2)),
        pltpu.SemaphoreType.DMA((4 * L, 2)),
    ]
    return pl.pallas_call(
        functools.partial(train_kernel, plan),
        out_shape=(
            jax.ShapeDtypeStruct((rows, Dp), BF),
            jax.ShapeDtypeStruct((rows, Dp), F32),
            jax.ShapeDtypeStruct((L * NP, rp, piece), F32),
            jax.ShapeDtypeStruct((rp + BIAS_ROWS, LANES), F32),
        ),
        in_specs=[pl.BlockSpec(memory_space=pltpu.VMEM)] * 4,
        out_specs=tuple([pl.BlockSpec(memory_space=pltpu.VMEM)] * 4),
        scratch_shapes=scratch,
        compiler_params=pltpu.CompilerParams(
            collective_id=0, has_side_effects=True, vmem_limit_bytes=67043328
        ),
        name="train_step",
    )(frames, cotangent, shards, small)


def adamw(weight, gradient, first, second, rate, decay):
    first_new = beta_one * first + (1.0 - beta_one) * gradient
    second_new = beta_two * second + (1.0 - beta_two) * gradient * gradient
    first_hat = first_new / (1.0 - beta_one**STEP)
    second_hat = second_new / (1.0 - beta_two**STEP)
    weight_new = weight - rate * (first_hat / (jnp.sqrt(second_hat) + adam_eps) + decay * weight)
    return (weight_new, first_new, second_new)


def pad_axis(values, axis, size):
    widths = [(0, 0)] * values.ndim
    widths[axis] = (0, size - values.shape[axis])
    return jnp.pad(values, widths)


def on_device(count, frames, cotangent, *tensors):
    masters, firsts, seconds = tensors[:7], tensors[7:14], tensors[14:21]
    w_qkv, w_out, w_up, w_down, b_qv, b_up, vectors = masters
    L = w_qkv.shape[0]
    rows, width = frames.shape
    half = w_qkv.shape[3]
    hidden = w_up.shape[2]
    plan = Plan(count, rows, width, half, hidden, L)
    own, rp, piece, UP = plan.own, plan.block, plan.piece, plan.up_pieces

    def spread_features(values):
        if rp == own:
            return values
        return pad_axis(values.reshape(rows, count, own), 2, rp).reshape(rows, plan.padded)

    def gather_features(values):
        if rp == own:
            return values
        return values.reshape(rows, count, rp)[:, :, :own].reshape(rows, width)

    low_qkv = w_qkv.astype(BF).reshape(L, own, 3 * half)
    low_out = w_out.astype(BF).transpose(0, 2, 1)
    low_up = w_up.astype(BF)
    low_down = w_down.astype(BF).transpose(0, 2, 1)
    parts = [low_qkv[:, :, :piece], jnp.concatenate([low_qkv[:, :, piece:], low_out], axis=2)]
    parts += [low_up[:, :, n * piece : (n + 1) * piece] for n in range(UP)]
    parts += [low_down[:, :, n * piece : (n + 1) * piece] for n in range(UP)]
    shards = jnp.stack(parts, axis=1).reshape(L * plan.pieces, own, piece)
    shards = pad_axis(shards, 1, rp)

    quarter = plan.quarter
    vec_part = pad_axis(vectors.astype(BF).transpose(2, 0, 1), 2, VEC_ROWS).reshape(own, L * VEC_ROWS)
    bias_part = jnp.concatenate(
        [b_qv.astype(BF).reshape(L, -1, quarter), b_up.astype(BF).reshape(L, -1, quarter)], axis=1
    )
    groups = bias_part.shape[1]
    bias_part = bias_part.transpose(2, 0, 1).reshape(quarter, L * groups)
    small = jnp.concatenate(
        [
            pad_axis(pad_axis(vec_part, 1, LANES), 0, rp),
            pad_axis(pad_axis(bias_part, 1, LANES), 0, BIAS_ROWS),
        ],
        axis=0,
    )

    output, grad_input, wide, small_grad = run_kernel(
        plan, spread_features(frames), spread_features(cotangent), shards, small
    )

    wide = wide.reshape(L, plan.pieces, rp, piece)[:, :, :own]
    grad_qkv = jnp.concatenate([wide[:, 0], wide[:, 1, :, :half]], axis=2).reshape(w_qkv.shape)
    grad_out = wide[:, 1, :, half:].transpose(0, 2, 1)
    grad_up = jnp.concatenate([wide[:, 2 + n] for n in range(UP)], axis=2)
    grad_down = jnp.concatenate([wide[:, 2 + UP + n] for n in range(UP)], axis=2).transpose(0, 2, 1)
    vec_grad = small_grad[:own, : L * VEC_ROWS].reshape(own, L, VEC_ROWS)[:, :, : vectors.shape[1]]
    grad_vec = vec_grad.transpose(1, 2, 0)
    bias_grad = small_grad[rp : rp + quarter, : L * groups].reshape(quarter, L, groups)
    bias_grad = bias_grad.transpose(1, 2, 0)
    split = b_qv.shape[1] * b_qv.shape[2]
    grad_bqv = bias_grad[:, :split].reshape(b_qv.shape)
    grad_bup = bias_grad[:, split:]
    grads = (grad_qkv, grad_out, grad_up, grad_down, grad_bqv, grad_bup, grad_vec)
    rates = (rate_matrix,) * 4 + (rate_vector,) * 3
    decays = (decay_rate,) * 4 + (0.0,) * 3
    updated = [
        adamw(masters[n], grads[n], firsts[n], seconds[n], rates[n], decays[n]) for n in range(7)
    ]
    return (
        (gather_features(output), gather_features(grad_input))
        + grads
        + tuple(updated[n][0] for n in range(7))
        + tuple(updated[n][1] for n in range(7))
        + tuple(updated[n][2] for n in range(7))
    )


def solution(mesh):
    tensors = (
        P(None, "fsdp", None, "tp"),
        P(None, "tp", "fsdp"),
        P(None, "fsdp", "tp"),
        P(None, "tp", "fsdp"),
        P(None, None, "tp", "fsdp"),
        P(None, "tp", "fsdp"),
        P(None, None, "fsdp"),
    )
    rows = (P("fsdp", None), P("fsdp", None))
    return jax.shard_map(
        functools.partial(on_device, mesh.shape["fsdp"]),
        mesh=mesh,
        in_specs=rows + tensors * 3,
        out_specs=rows + tensors * 4,
        check_vma=False,
    )
```

time: 1400 us -> 259 us (0.18)
  waiting for transfers between devices: 832 us -> 0 us
  Pallas kernels: 0 us -> 238 us
  blocking collectives: 222 us -> 0 us
  matrix products: 155 us -> 0 us
  local copies, waits for them, and re-layouts: 83.9 us -> 8.96 us
  other arithmetic: 74.8 us -> 10.4 us
  between operations: 16.4 us -> 1.06 us
    reduce_scatter x8 -> x0, waiting for transfers between devices: 557 us -> none  [the longest x2 155 us: scatter_layer(): lax.psum_scatter(grad_up, 'fsdp', scatter_dimension=0, tiled=True)]
    pallas_call x0 -> x1, Pallas kernels: none -> 238 us  [run_kernel(): pl.pallas_call(functools.partial(train_kernel, plan), out_shape=(jax.Shap...]
    all_gather x8 -> x0, blocking collectives: 162 us -> none  [the longest x2 41.9 us: fetch_forward(): lax.all_gather(piece_bqv, 'fsdp', axis=2, tiled=True)]
    dot_general x108 -> x0, matrix products: 155 us -> none  [the longest x12 20.1 us: head_backward(): jnp.dot(grad_scores, key_head, preferred_element_type=jnp.float32)]
    all_gather x6 -> x0, waiting for transfers between devices: 133 us -> none  [the longest x2 80.3 us: fetch_forward(): lax.all_gather(piece_down, 'fsdp', axis=1, tiled=True)]
    psum x7 -> x0, waiting for transfers between devices: 125 us -> none  [the longest x2 51.6 us: layer_forward(): lax.psum(column_terms.astype(jnp.bfloat16), 'tp').astype(jnp.float32)]
    unnamed x1 -> x0, blocking collectives: 59.5 us -> none
    add x15 -> x0, other arithmetic: 29.2 us -> none  [the longest x2 27.9 us: layer_forward(): middle + lax.psum(column_terms.astype(jnp.bfloat16), 'tp').astype(jnp.flo...]
  transfers between devices with their start and end apart: 23 -> 0, of which waited for: 20 -> 0; matrix products, arithmetic and copies ran while one was open for 9% -> 0% of each run, Pallas kernels for 0% -> 0%
where the time goes in v1:
time: 259 us; the launch traced here: 258 us
  Pallas kernels  238 us (92%)
  other arithmetic  10.4 us (4%)
  local copies, waits for them, and re-layouts  8.96 us (3%)
    pallas_call x1, Pallas kernels, run_kernel(): pl.pallas_call(functools.partial(train_kernel, plan), out_shape=(jax.Shap...  238 us
    sub x7, other arithmetic, adamw(): weight - rate * (first_hat / (jnp.sqrt(second_hat) + adam_eps) + decay *...  7.57 us

profile of v1, /device:TPU:0, one launch (start us, length us, event | category | flops | bytes accessed | tf_op | source)
XLA Modules:
  0.0 258.3 jit_solution(13996659052852848902)
XLA Ops:
  0.7 0.0 copy-start
  0.7 0.0 copy-start.2
  0.7 1.1 convert_bitcast_fusion.1
  1.9 0.9 convert_bitcast_fusion.2
  2.8 0.0 copy-done
  2.9 0.0 copy-start.21
  2.9 0.0 copy-start.16
  2.9 0.0 copy-start.18
  3.0 0.0 copy-done.2
  3.1 1.0 copy.113
  4.0 0.0 copy-done.21
  4.1 0.0 copy-done.16
  4.1 0.1 reshape.93
  4.2 0.1 maximum_bitcast_fusion.2
  4.3 0.1 reshape.94
  4.3 0.0 copy-done.18
  4.4 0.1 copy.115
  4.5 0.6 fusion.12.small_ref
  5.1 237.8 %train_step.1 = (bf16[256,768]{1,0:T(8,128)(2,1)}, f32[256,768]{1,0:T(8,128)}, f32[12,48,768]{2,1,0:T(8,128)}, f32[64,128]{1,0:T(8,128)}) custom-call(bf16[256,768]{1,0:T(8,128)(2,1)} %frames_ref.1, bf16[256,768]{1,0:T(8,128)(2,1)} %cot_ref.1, bf16[12,48,768]{2,1,0:T(8,128)(2,1)} %bitcast.94, bf16[64,128]{1,0:T(8,128)(2,1)} %fusion.12.small_ref), custom_call_target="tpu_custom_call" | custom-call | tf_op jit(solution)/shard_map/train_step/pallas_call | solution.py:738
  242.9 0.9 slice_bitcast_fusion.6
  243.9 0.0 copy-start.4
  243.9 0.0 copy-start.11
  243.9 0.0 copy-start.12
  243.9 1.6 slice_bitcast_fusion.1
  245.5 0.0 copy-done.4
  245.5 0.0 copy-done.11
  245.5 0.1 copy-done.12
  245.6 0.0 copy-start.6
  245.6 0.0 copy-start.7
  245.6 1.3 multiply_subtract_fusion.2
  246.9 0.0 copy-done.10
  246.9 0.0 copy-done.14
  246.9 0.0 copy-done.15
  246.9 1.8 multiply_subtract_fusion.3
  248.7 0.0 copy-done.1
  248.7 0.0 copy-done.6
  248.7 0.0 copy-done.7
  248.7 0.0 copy-start.3
  248.8 0.0 copy-start.8
  248.8 0.0 copy-start.9
  248.8 1.6 multiply_subtract_fusion.1
  250.3 0.0 copy-done.3
  250.3 0.0 copy-done.8
  250.4 0.6 copy-done.9
  251.0 0.0 copy-start.22
  251.0 0.0 copy-start.27
  251.0 0.0 copy-start.28
  251.0 0.0 copy-start.19
  251.0 0.0 copy-start.25
  251.0 0.0 copy-start.26
  251.1 1.6 multiply_subtract_fusion
  252.6 0.1 reshape.97
  252.7 0.1 reshape.98
  252.8 0.6 multiply_subtract_fusion.4
  253.5 0.0 copy-done.28
  253.5 0.7 multiply_subtract_fusion.5
  254.2 0.1 copy.126
  254.2 0.6 copy.139
  254.8 0.0 copy-done.26
  254.9 0.6 copy.140
  255.5 0.6 copy.141
  256.1 0.6 copy.142
  256.7 0.7 copy.181
  257.4 0.9 copy.182
  (43 shorter events, 0.3 us)
Async XLA Ops:
  0.7 2.2 copy-start
  0.7 2.3 copy-start.2
  2.9 1.1 copy-start.21
  2.9 1.1 copy-start.16
  2.9 1.4 copy-start.18
  243.9 1.6 copy-start.4
  243.9 1.6 copy-start.11
  243.9 1.7 copy-start.12
  245.6 1.3 copy-start.10
  245.6 1.3 copy-start.14
  245.6 1.3 copy-start.15
  245.6 3.1 %copy-start.1 = (f32[2,48,1536]{2,1,0:T(8,128)S(1)}, f32[2,48,1536]{2,1,0:T(8,128)}, u32[]{:S(2)}) copy-start(f32[2,48,1536]{2,1,0:T(8,128)} %param.27) | copy-start | bytes 1769476
  245.6 3.1 %copy-start.6 = (f32[2,48,1536]{2,1,0:T(8,128)S(1)}, f32[2,48,1536]{2,1,0:T(8,128)}, u32[]{:S(2)}) copy-start(f32[2,48,1536]{2,1,0:T(8,128)} %param.34) | copy-start | bytes 1769476
  245.6 3.1 %copy-start.7 = (f32[2,48,1536]{2,1,0:T(8,128)S(1)}, f32[2,48,1536]{2,1,0:T(8,128)}, u32[]{:S(2)}) copy-start(f32[2,48,1536]{2,1,0:T(8,128)} %param.41) | copy-start | bytes 1769476
  248.7 1.6 copy-start.3
  248.8 1.6 copy-start.8
  248.8 2.2 copy-start.9
  251.0 1.7 copy-start.20
  251.0 1.9 copy-start.17
  251.0 1.9 copy-start.23
  251.0 1.9 copy-start.24
  251.0 2.5 copy-start.22
  251.0 2.5 copy-start.27
  251.0 2.5 copy-start.28
  251.0 3.8 %copy-start.19 = (f32[2,6,48]{2,0,1:T(2,128)S(1)}, f32[2,6,48]{2,0,1:T(2,128)}, u32[]{:S(2)}) copy-start(f32[2,6,48]{2,0,1:T(2,128)} %param.31) | copy-start | bytes 6916
  251.0 3.8 %copy-start.25 = (f32[2,6,48]{2,0,1:T(2,128)S(1)}, f32[2,6,48]{2,0,1:T(2,128)}, u32[]{:S(2)}) copy-start(f32[2,6,48]{2,0,1:T(2,128)} %param.38) | copy-start | bytes 6916
  251.0 3.8 %copy-start.26 = (f32[2,6,48]{2,0,1:T(2,128)S(1)}, f32[2,6,48]{2,0,1:T(2,128)}, u32[]{:S(2)}) copy-start(f32[2,6,48]{2,0,1:T(2,128)} %param.45) | copy-start | bytes 6916
  251.0 5.6 %copy-start.13 = (bf16[256,768]{1,0:T(8,128)(2,1)S(1)}, bf16[256,768]{1,0:T(8,128)(2,1)}, u32[]{:S(2)}) copy-start(bf16[256,768]{1,0:T(8,128)(2,1)} %get-tuple-element.190) | copy-start | bytes 1179652
  251.0 6.4 %copy-start.5 = (f32[256,768]{1,0:T(8,128)S(1)}, f32[256,768]{1,0:T(8,128)}, u32[]{:S(2)}) copy-start(f32[256,768]{1,0:T(8,128)} %get-tuple-element.191) | copy-start | bytes 2359300

commit v2 on v1

--- a/solution.py
+++ b/solution.py
@@ -63,13 +63,12 @@
         self.half = half
         self.pairs = half // LANES
         self.layers = layers
-        self.piece = 2 * half
-        self.up_pieces = hidden // self.piece
-        self.pieces = 2 + 2 * self.up_pieces
+        self.ups = hidden // half
+        self.units = 4 + 2 * self.ups
         self.quarter = HD // count
-        self.heads = half // HD
         self.bias_cols = 2 * half + hidden
-        self.slots = sum(size - 1 for size in self.axes)
+        self.hops = tuple(1 if size == 2 else 3 for size in self.axes)
+        self.slots = sum(self.hops)
         self.chunk = rows // 2
 
 
@@ -105,9 +104,6 @@
     DX,
     LOW,
     FL,
-    DCTX,
-    RQK,
-    RV,
     VG,
     BG,
     TURN,
@@ -126,8 +122,8 @@
     rp = plan.block
     Dp = plan.padded
     L = plan.layers
-    NP = plan.pieces
-    UP = plan.up_pieces
+    NP = plan.units
+    UP = plan.ups
     half = plan.half
     rows = plan.rows
     chunk = plan.chunk
@@ -135,95 +131,156 @@
     me = lax.axis_index("fsdp")
     side = lax.axis_index("tp")
     digit = [lax.rem(me // stride, size) for stride, size in zip(plan.strides, axes)]
-    offsets = []
-    total = 0
-    for size in axes:
-        offsets.append(total)
-        total += size - 1
-
-    def peer(k, j):
-        value = lax.rem(digit[k] + j, axes[k])
-        return value, (me + (value - digit[k]) * plan.strides[k], side)
-
-    def source(k, j):
-        return lax.rem(digit[k] - j + axes[k], axes[k])
-
-    def place(k, value):
-        return (slice(None),) * k + (value,) + tuple(digit[k + 1 :])
-
+    slot_of = [sum(plan.hops[:k]) for k in range(depth)]
     other = (me, 1 - side)
 
+    def device(k, value):
+        return (me + (value - digit[k]) * plan.strides[k], side)
+
+    half_side = [d // 2 for d in digit]
+    outer = [(d == 0) | (d == 3) for d in digit]
+    inner = [jnp.logical_not(flag) for flag in outer]
+    mine_in = [1 + s for s in half_side]
+    mine_out = [3 * s for s in half_side]
+    far_in = [2 - s for s in half_side]
+    near = [pl.ds(2 * s, 2) for s in half_side]
+    far = [pl.ds(2 * (1 - s), 2) for s in half_side]
+    three = [pl.ds(1 - s, 3) for s in half_side]
+
     barrier = pltpu.get_barrier_semaphore()
+
+    def greet(target):
+        pl.semaphore_signal(barrier, inc=1, device_id=target, device_id_type=MESH)
+
+    greet(other)
     greeted = 1
-    pl.semaphore_signal(barrier, inc=1, device_id=other, device_id_type=MESH)
     for k in range(depth):
-        for j in range(1, axes[k]):
-            pl.semaphore_signal(barrier, inc=1, device_id=peer(k, j)[1], device_id_type=MESH)
-            greeted += 1
+        if axes[k] == 2:
+            greet(device(k, 1 - digit[k]))
+        else:
+            greet(device(k, jnp.where(outer[k], mine_in[k], mine_out[k])))
+        greeted += 1
+    for k in range(depth):
+        if axes[k] == 4:
+
+            @pl.when(inner[k])
+            def _():
+                greet(device(k, far_in[k]))
+
+            greeted = greeted + jnp.where(inner[k], 1, 0)
     pl.semaphore_wait(barrier, greeted)
 
-    def remote(src, dst, send, recv, device):
+    def remote(src, dst, send, recv, target):
         return pltpu.make_async_remote_copy(
             src_ref=src,
             dst_ref=dst,
             send_sem=send,
             recv_sem=recv,
-            device_id=device,
+            device_id=target,
             device_id_type=MESH,
         )
 
     small_index = L * NP
-
-    def gather_copy(k, j, piece, small, sending):
-        slot = offsets[k] + j - 1
-        value, device = peer(k, j)
-        spot = place(k, digit[k]) if sending else place(k, source(k, j))
-        if small:
-            dst = SB.at[spot]
-            src = small_ref if (k == 0 and sending) else dst
+    straight = tuple(range(depth))
+
+    def gather_copy(k, hop, unit, order, small, sending):
+        done = order[: order.index(k)]
+
+        def spot(value):
+            return tuple(
+                slice(None) if a in done else value if a == k else digit[a] for a in range(depth)
+            )
+
+        if axes[k] == 2:
+            value = digit[k] if sending else 1 - digit[k]
+            target = 1 - digit[k]
+        elif hop == 0:
+            value = digit[k] if sending else mine_out[k]
+            target = mine_in[k]
+        elif hop == 1:
+            value = near[k] if sending else far[k]
+            target = far_in[k]
         else:
-            dst = W.at[(piece,) + spot]
-            src = shard_ref.at[piece] if (k == 0 and sending) else dst
-        return remote(src, dst, ag_send.at[piece, slot], ag_recv.at[piece, slot], device)
-
-    def gather_start(k, piece, small=False):
-        for j in range(1, axes[k]):
-            gather_copy(k, j, piece, small, True).start()
-
-    def gather_wait(k, piece, small=False):
-        for j in range(1, axes[k]):
-            gather_copy(k, j, piece, small, False).wait_recv()
-
-    def gather_drain(piece, small=False):
+            value = three[k]
+            target = mine_out[k]
+        dst = SB.at[spot(value)] if small else W.at[(unit,) + spot(value)]
+        src = dst
+        if sending and not done and hop == 0:
+            src = small_ref if small else shard_ref.at[unit]
+        slot = slot_of[k] + hop
+        return remote(src, dst, ag_send.at[unit, slot], ag_recv.at[unit, slot], device(k, target))
+
+    def gather_begin(k, unit, order, small):
+        if axes[k] == 2:
+            gather_copy(k, 0, unit, order, small, True).start()
+        else:
+
+            @pl.when(outer[k])
+            def _():
+                gather_copy(k, 0, unit, order, small, True).start()
+
+    def gather_next(k, unit, order, small):
+        position = order.index(k) + 1
+        if position < depth:
+            gather_begin(order[position], unit, order, small)
+
+    def gather_hop(index, unit, order, small):
+        for k in order:
+            if index < plan.hops[k]:
+                break
+            index -= plan.hops[k]
+        if axes[k] == 2:
+            gather_copy(k, 0, unit, order, small, False).wait_recv()
+            gather_next(k, unit, order, small)
+            return
+
+        @pl.when(outer[k] if index == 2 else inner[k])
+        def _():
+            gather_copy(k, index, unit, order, small, False).wait_recv()
+            if index < 2:
+                gather_copy(k, index + 1, unit, order, small, True).start()
+            if index > 0:
+                gather_next(k, unit, order, small)
+
+    def gather_drain(unit, small=False):
         for k in range(depth):
-            for j in range(1, axes[k]):
-                gather_copy(k, j, piece, small, True).wait_send()
-
-    def ready(piece):
-        @pl.when(piece + 1 < L * NP)
-        def _():
-            gather_wait(0, piece + 1)
-            gather_start(1, piece + 1)
-
-        for k in range(1, depth):
-            gather_wait(k, piece)
-            if k + 1 < depth:
-                gather_start(k + 1, piece)
-
+            for hop in range(plan.hops[k]):
+                if axes[k] == 2:
+                    gather_copy(k, hop, unit, straight, small, True).wait_send()
+                else:
+
+                    @pl.when(outer[k] if hop == 0 else inner[k])
+                    def _():
+                        gather_copy(k, hop, unit, straight, small, True).wait_send()
+
+    hops = plan.slots
+
+    def gather_ahead(n, low, high):
+        for index in range(low, high):
+            unit = n + (hops - 1 - index if index < hops - 2 else 0)
+
+            @pl.when((unit >= 0) & (unit < L * NP))
+            def _():
+                gather_hop(index, unit, straight, False)
+
+    def gather_tick(n, carry=0):
+        gather_ahead(n, 0, hops)
+        return carry
+
+    def ready(low, high):
+        lax.fori_loop(low, high, gather_tick, 0)
+
+    gather_begin(0, small_index, straight, True)
+    for unit in range(L * NP):
+        gather_begin(0, unit, straight, False)
     here = tuple(digit)
     SB[here] = small_ref[...]
-    gather_start(0, small_index, True)
-    for piece in range(L * NP):
-        gather_start(0, piece)
-    for piece in range(L * NP):
-        W[(piece,) + here] = shard_ref[piece]
-
-    gather_wait(0, small_index, True)
-    for k in range(1, depth):
-        gather_start(k, small_index, True)
-        gather_wait(k, small_index, True)
-    gather_wait(0, 0)
-    gather_start(1, 0)
+    for unit in range(L * NP):
+        W[(unit,) + here] = shard_ref[unit]
+    for index in range(hops):
+        gather_hop(index, small_index, straight, True)
+        if index < hops - 1:
+            gather_ahead(index - (hops - 1), 0, hops)
 
     vec_all = SB[(slice(None),) * depth + (slice(0, rp), slice(None))]
     vec_rows = vec_all.reshape(Dp, LANES).astype(F32).T
@@ -268,10 +325,11 @@
     def masked(values):
         return values if valid is None else values * valid
 
-    def piece_of(index, low=0, high=None):
-        high = plan.piece if high is None else high
-        tail = (slice(None), slice(low, high))
-        return W[(index,) + (slice(None),) * depth + tail].reshape(Dp, high - low)
+    def unit_of(index):
+        return W[index].reshape(Dp, half)
+
+    def pair_of(index):
+        return jnp.concatenate([unit_of(index), unit_of(index + 1)], axis=1)
 
     def norm_forward(values, layer, which, region):
         centred = masked(values - average(values))
@@ -325,10 +383,11 @@
                 scores = mm(query * mask, key, NT) * scale
                 highest = jnp.max(scores, axis=1, keepdims=True)
                 logsum = highest + jnp.log(jnp.sum(jnp.exp(scores - highest), axis=1, keepdims=True))
-                LSE[layer, pair, h, span] = logsum
+                kept = logsum if h == 0 else jnp.where(lane < h * HD, kept, logsum)
                 weights = jnp.exp(scores - logsum).astype(BF)
                 part = mm(weights, value * mask, NN)
                 total = part if total is None else total + part
+            LSE[layer, pair, span] = jnp.broadcast_to(kept, (SEQ, LANES))
             CTX[layer, pair, span] = total.astype(BF)
             return 0
 
@@ -339,12 +398,16 @@
 
     def forward_layer(layer, carry):
         first = layer * NP
+        up = first + 4
+        down = up + UP
 
         @pl.when(layer == 0)
         def _():
             value = frames_ref[...].astype(F32)
             DX[...] = value
             norm_forward(value, layer, 0, slice(None))
+
+        ready(first, first + 2)
 
         @pl.when(layer > 0)
         def _():
@@ -355,47 +418,46 @@
                 norm_forward(value, layer, 0, region)
             exchange_done(2 * layer - 1, 1)
 
-        ready(first)
-        both = mm(ACT[layer, 0], piece_of(first), NN)
+        both = mm(ACT[layer, 0], pair_of(first), NN)
         for pair in range(plan.pairs):
             low = pair * LANES
             query = both[:, low : low + LANES] + BIAS[layer, :, low : low + LANES]
             Q[layer, pair] = query.astype(BF)
             K[layer, pair] = both[:, half + low : half + low + LANES].astype(BF)
-        ready(first + 1)
-        values = mm(ACT[layer, 0], piece_of(first + 1, 0, half), NN)
+        ready(first + 2, first + 3)
+        values = mm(ACT[layer, 0], unit_of(first + 2), NN)
         for pair in range(plan.pairs):
             low = pair * LANES
             bias = BIAS[layer, :, half + low : half + low + LANES]
             V[layer, pair] = (values[:, low : low + LANES] + bias).astype(BF)
         attend(layer)
+        ready(first + 3, first + 4)
         for part in range(2):
             region = pl.ds(part * chunk, chunk)
             heads = context_of(layer, region)
-            exchange_send(2 * layer, 0, part, mm(heads, piece_of(first + 1, half), NT))
-        for number in range(UP):
-            ready(first + 2 + number)
+            exchange_send(2 * layer, 0, part, mm(heads, unit_of(first + 3), NT))
+        ready(up, up + UP)
         for part in range(2):
             region = pl.ds(part * chunk, chunk)
             value = DX[region] + exchange_sum(2 * layer, 0, part) + VEC[layer, 4:5]
             MID[region] = value
             norm_forward(value, layer, 1, region)
         exchange_done(2 * layer, 0)
-        for number in range(UP):
-            before = mm(ACT[layer, 1], piece_of(first + 2 + number), NN)
-            low = 2 * half + number * plan.piece
-            before = before + BIAS[layer, :, low : low + plan.piece]
+        for number in range(0, UP, 2):
+            before = mm(ACT[layer, 1], pair_of(up + number), NN)
+            low = (2 + number) * half
+            before = before + BIAS[layer, :, low : low + 2 * half]
             bell = 0.5 * (1.0 + lax.erf(before * root_half))
-            HIDDEN[layer, number] = (before * bell).astype(BF)
+            HIDDEN[layer, number // 2] = (before * bell).astype(BF)
             slope = bell + before * jnp.exp(-0.5 * before * before) * inv_root_two_pi
-            SLOPE[layer, number] = slope.astype(BF)
-        for number in range(UP):
-            ready(first + 2 + UP + number)
-            term = mm(HIDDEN[layer, number], piece_of(first + 2 + UP + number), NT)
-            if number + 1 < UP:
+            SLOPE[layer, number // 2] = slope.astype(BF)
+        for number in range(0, UP, 2):
+            ready(down + number, down + number + 2)
+            term = mm(HIDDEN[layer, number // 2], pair_of(down + number), NT)
+            if number + 2 < UP:
                 ACC[...] = term if number == 0 else ACC[...] + term
             else:
-                whole = term + ACC[...] if UP > 1 else term
+                whole = term + ACC[...] if UP > 2 else term
 
                 @pl.when(layer + 1 < L)
                 def _():
@@ -410,65 +472,120 @@
 
     lax.fori_loop(0, L, forward_layer, 0)
 
-    def landing(k, piece):
-        return lax.rem(piece, NP) if k == depth - 1 else piece
-
-    def scatter_copy(k, j, piece, small):
-        slot = offsets[k] + j - 1
-        value, device = peer(k, j)
-        spot = place(k, value)
+    def landing(k, unit):
+        return lax.rem(unit, NP) if k == depth - 1 else unit
+
+    def land(k, slots):
+        return (slice(None),) * k + (slots,)
+
+    def scatter_spot(k, order, value):
+        done = order[order.index(k) + 1 :]
+        return tuple(
+            digit[a] if a in done else value if a == k else slice(None) for a in range(depth)
+        )
+
+    def scatter_copy(k, hop, unit, order, small):
+        if axes[k] == 2:
+            value, target, slots = 1 - digit[k], 1 - digit[k], 0
+        elif hop == 0:
+            value, target, slots = three[k], mine_in[k], pl.ds(0, 3)
+        elif hop == 1:
+            value, target, slots = far[k], far_in[k], pl.ds(3, 2)
+        else:
+            value, target, slots = mine_out[k], mine_out[k], 0
+        spot = scatter_spot(k, order, value)
         if small:
-            src = SG.at[spot]
-            dst = RSs[k].at[j - 1]
+            src, dst = SG.at[spot], RSs[k].at[land(k, slots)]
         else:
-            src = W.at[(piece,) + spot]
-            dst = RBs[k].at[landing(k, piece), j - 1]
-        return remote(src, dst, rs_send.at[piece, slot], rs_recv.at[piece, slot], device)
-
-    def scatter_start(k, piece, small=False):
-        for j in range(1, axes[k]):
-            scatter_copy(k, j, piece, small).start()
-
-    def scatter_wait(k, piece, small=False):
-        for j in range(1, axes[k]):
-            scatter_copy(k, j, piece, small).wait_recv()
-
-    def scatter_step(k, piece, small=False):
-        scatter_wait(k, piece, small)
-        spot = place(k, digit[k])
+            src, dst = W.at[(unit,) + spot], RBs[k].at[(landing(k, unit),) + land(k, slots)]
+        slot = slot_of[k] + hop
+        return remote(src, dst, rs_send.at[unit, slot], rs_recv.at[unit, slot], device(k, target))
+
+    def scatter_begin(k, unit, order, small=False):
+        if axes[k] == 2:
+            scatter_copy(k, 0, unit, order, small).start()
+        else:
+
+            @pl.when(outer[k])
+            def _():
+                scatter_copy(k, 0, unit, order, small).start()
+
+    def held(small, unit, spot):
+        return SG[spot] if small else W[(unit,) + spot].astype(F32)
+
+    def arrived(k, small, unit, slots):
         if small:
-            value = SG[spot]
-            for j in range(1, axes[k]):
-                value = value + RSs[k][j - 1]
-            if k == 0:
-                smallg_ref[...] = value
+            return RSs[k][land(k, slots)]
+        return RBs[k][(landing(k, unit),) + land(k, slots)].astype(F32)
+
+    def keep(small, unit, spot, value):
+        if small:
+            SG[spot] = value
+        else:
+            W[(unit,) + spot] = value.astype(BF)
+
+    def finish(k, unit, order, small, slots):
+        spot = scatter_spot(k, order, digit[k])
+        value = held(small, unit, spot) + arrived(k, small, unit, slots)
+        position = order.index(k)
+        if position > 0:
+            keep(small, unit, spot, value)
+            scatter_begin(order[position - 1], unit, order, small)
+        elif small:
+            smallg_ref[...] = value
+        else:
+            gout_ref[unit] = value
+
+    def add_in(k, unit, order, small, value, slots):
+        spot = scatter_spot(k, order, value)
+        keep(small, unit, spot, held(small, unit, spot) + arrived(k, small, unit, slots))
+
+    def scatter_hop(index, unit, order, small=False):
+        for k in reversed(order):
+            if index < plan.hops[k]:
+                break
+            index -= plan.hops[k]
+        if axes[k] == 2:
+            scatter_copy(k, 0, unit, order, small).wait_recv()
+            finish(k, unit, order, small, 0)
+            return
+
+        @pl.when(outer[k] if index == 2 else inner[k])
+        def _():
+            scatter_copy(k, index, unit, order, small).wait_recv()
+            if index == 0:
+                add_in(k, unit, order, small, three[k], pl.ds(0, 3))
+                scatter_copy(k, 1, unit, order, small).start()
+            elif index == 1:
+                add_in(k, unit, order, small, mine_out[k], 3 + mine_out[k] - 2 * half_side[k])
+                scatter_copy(k, 2, unit, order, small).start()
+                finish(k, unit, order, small, 3 + digit[k] - 2 * half_side[k])
             else:
-                SG[spot] = value
-                scatter_start(k - 1, piece, True)
-        else:
-            value = W[(piece,) + spot].astype(F32)
-            for j in range(1, axes[k]):
-                value = value + RBs[k][landing(k, piece), j - 1].astype(F32)
-            if k == 0:
-                gout_ref[piece] = value
-            else:
-                W[(piece,) + spot] = value.astype(BF)
-                scatter_start(k - 1, piece)
-
-    def scatter_drain(piece, small=False):
+                finish(k, unit, order, small, 0)
+
+    def scatter_drain(unit, small=False):
         for k in range(depth):
-            for j in range(1, axes[k]):
-                scatter_copy(k, j, piece, small).wait_send()
+            for hop in range(plan.hops[k]):
+                if axes[k] == 2:
+                    scatter_copy(k, hop, unit, straight, small).wait_send()
+                else:
+
+                    @pl.when(outer[k] if hop == 0 else inner[k])
+                    def _():
+                        scatter_copy(k, hop, unit, straight, small).wait_send()
 
     block_shape = axes + (rp,)
 
-    def put_gradient(index, value, low=0, high=None):
-        high = plan.piece if high is None else high
-        tail = (slice(None), slice(low, high))
-        W[(index,) + (slice(None),) * depth + tail] = value.astype(BF).reshape(block_shape + (high - low,))
-
-    for piece in range(L * NP):
-        gather_drain(piece)
+    def put_gradient(index, value):
+        W[index] = value.astype(BF).reshape(block_shape + (half,))
+        scatter_begin(depth - 1, index, straight)
+
+    def put_pair(index, value):
+        put_gradient(index, value[:, :half])
+        put_gradient(index + 1, value[:, half:])
+
+    for unit in range(L * NP):
+        gather_drain(unit)
     gather_drain(small_index, True)
 
     def attend_back(layer):
@@ -479,11 +596,12 @@
             query = Q[layer, pair, span]
             key = K[layer, pair, span]
             value = V[layer, pair, span]
-            upper = DCTX[pair, span]
+            upper = FL[1, span, pl.ds(pl.multiple_of(half + pair * LANES, LANES), LANES)]
+            logsums = LSE[layer, pair, span]
             grad_q = grad_k = grad_v = None
             for h, mask in enumerate(head_mask):
                 scores = mm(query * mask, key, NT) * scale
-                probs = jnp.exp(scores - LSE[layer, pair, h, span])
+                probs = jnp.exp(scores - logsums[:, h * HD : h * HD + 1])
                 weights = probs.astype(BF)
                 up_head = upper * mask
                 part_v = mm(weights, up_head, TN)
@@ -497,9 +615,9 @@
                 grad_v = part_v if grad_v is None else grad_v + part_v
             low = pl.ds(pl.multiple_of(pair * LANES, LANES), LANES)
             next_low = pl.ds(pl.multiple_of(half + pair * LANES, LANES), LANES)
-            RQK[span, low] = grad_q.astype(BF)
-            RQK[span, next_low] = grad_k.astype(BF)
-            RV[span, low] = grad_v.astype(BF)
+            FL[0, span, low] = grad_q.astype(BF)
+            FL[0, span, next_low] = grad_k.astype(BF)
+            FL[1, span, low] = grad_v.astype(BF)
             sum_q = jnp.sum(grad_q, axis=0, keepdims=True)
             sum_v = jnp.sum(grad_v, axis=0, keepdims=True)
 
@@ -537,71 +655,93 @@
     DMID = ACC
 
     def produced(m):
-        step = m // NP
         turn = lax.rem(m, NP)
         name = jnp.where(
             turn < UP,
-            2 + UP + turn,
-            jnp.where(turn < 2 * UP, 2 + turn - UP, NP - 1 - turn),
+            4 + UP + turn,
+            jnp.where(turn < 2 * UP, 4 + turn - UP, NP - 1 - turn),
         )
-        return (L - 1 - step) * NP + name
-
-    def pump(m, carry):
-        for k in range(depth - 2, -1, -1):
-            earlier = m - (depth - 2 - k)
-
-            @pl.when((earlier >= 0) & (earlier < L * NP))
-            def _():
-                scatter_step(k, produced(earlier))
-
-        return carry
-
-    def pumped(step, place_in_layer):
-        counts = PUMPS[place_in_layer]
+        return (L - 1 - m // NP) * NP + name
+
+    def pumped(step, place, index):
+        counts = [row[min(index - 1, len(row) - 1)] - max(0, index - len(row)) for row in PUMPS[place]]
         value = counts[0]
         for s in range(1, L):
             value = jnp.where(step == s, counts[min(s, len(counts) - 1)], value)
-        return jnp.minimum(value, L * NP)
-
-    def pump_to(step, place_in_layer):
-        if place_in_layer == 0:
-            low = jnp.where(step == 0, 0, pumped(step - 1, len(PUMPS) - 1))
-        else:
-            low = pumped(step, place_in_layer - 1)
-        lax.fori_loop(low, pumped(step, place_in_layer), pump, 0)
+        return jnp.clip(value, 0, L * NP)
+
+    def pump_range(index, low, high):
+        def one(m, carry):
+            scatter_hop(index, produced(m), straight)
+            return carry
+
+        lax.fori_loop(low, high, one, 0)
+
+    def pump_to(step, place):
+        for index in range(1, hops):
+            if place == 0:
+                low = jnp.where(step == 0, 0, pumped(step - 1, len(PUMPS) - 1, index))
+            else:
+                low = pumped(step, place - 1, index)
+            pump_range(index, low, pumped(step, place, index))
+
+    def pump_rest():
+        last = len(PUMPS) - 1
+        start = PUMPS[last][-1][0]
+        delays = [0 if index == 1 else index for index in range(1, hops)]
+        for index in range(1, hops):
+            pump_range(index, pumped(L - 1, last, index), max(0, min(start - delays[index - 1], L * NP)))
+
+        def one(m, carry):
+            for index in range(1, hops):
+                earlier = m - delays[index - 1]
+
+                @pl.when((earlier >= 0) & (earlier < L * NP))
+                def _():
+                    scatter_hop(index, produced(earlier), straight)
+
+                @pl.when(earlier == L * NP)
+                def _():
+                    scatter_hop(index, small_index, straight, True)
+
+            return carry
+
+        lax.fori_loop(start, L * NP + 1 + max(delays), one, 0)
 
     def backward_layer(step, carry):
         layer = L - 1 - step
         first = layer * NP
-        up = first + 2
-        down = first + 2 + UP
+        up = first + 4
+        down = up + UP
         number_up = 2 * L + 2 * step
+
+        def from_core(low, high):
+            for n in range(low, high):
+                scatter_hop(0, first + n, straight)
+
         VG[layer] = jnp.zeros((VEC_ROWS, Dp), F32)
         upper = DX[...]
         VG[layer, 5:6] = column_sum(upper)
         LOW[...] = upper.astype(BF)
-        for number in range(UP):
-            grad = mm(LOW[...], piece_of(down + number), NN) * SLOPE[layer, number].astype(F32)
-            low = 2 * half + number * plan.piece
-            BG[layer, :, low : low + plan.piece] = column_sum(grad)
-            FL[number] = grad.astype(BF)
-            put_gradient(down + number, mm(LOW[...], HIDDEN[layer, number], TN))
-            scatter_start(depth - 1, down + number)
+        for number in range(0, UP, 2):
+            grad = mm(LOW[...], pair_of(down + number), NN) * SLOPE[layer, number // 2].astype(F32)
+            low = (2 + number) * half
+            BG[layer, :, low : low + 2 * half] = column_sum(grad)
+            FL[number // 2] = grad.astype(BF)
+            put_pair(down + number, mm(LOW[...], HIDDEN[layer, number // 2], TN))
         for part in range(2):
             region = pl.ds(part * chunk, chunk)
             whole = None
-            for number in range(UP):
-                term = mm(FL[number, region], piece_of(up + number), NT)
+            for number in range(0, UP, 2):
+                term = mm(FL[number // 2, region], pair_of(up + number), NT)
                 whole = term if whole is None else whole + term
             exchange_send(number_up, 1, part, whole)
-        for number in range(UP):
-            scatter_step(depth - 1, down + number)
-        for number in range(UP):
-            put_gradient(up + number, mm(ACT[layer, 1], FL[number], TN))
-            scatter_start(depth - 1, up + number)
-        for number in range(UP):
-            scatter_step(depth - 1, up + number)
+        from_core(4 + UP, 4 + 2 * UP)
         pump_to(step, 0)
+        for number in range(0, UP, 2):
+            put_pair(up + number, mm(ACT[layer, 1], FL[number // 2], TN))
+        from_core(4, 4 + UP)
+        pump_to(step, 1)
         for part in range(2):
             region = pl.ds(part * chunk, chunk)
             grad = exchange_sum(number_up, 1, part)
@@ -612,24 +752,25 @@
             keep_rows(layer, 4, part, column_sum(grad_mid))
             LOW[region] = grad_mid.astype(BF)
         exchange_done(number_up, 1)
-        heads = mm(LOW[...], piece_of(first + 1, half), NN)
-        for pair in range(plan.pairs):
-            DCTX[pair] = heads[:, pair * LANES : (pair + 1) * LANES].astype(BF)
-        put_gradient(first + 1, mm(LOW[...], context_of(layer), TN), half)
+        heads = mm(LOW[...], unit_of(first + 3), NN)
+        FL[1, :, half : 2 * half] = heads.astype(BF)
+        put_gradient(first + 3, mm(LOW[...], context_of(layer), TN))
+        pump_to(step, 2)
         attend_back(layer)
         for part in range(2):
             region = pl.ds(part * chunk, chunk)
-            whole = mm(RQK[region], piece_of(first), NT)
-            whole = whole + mm(RV[region], piece_of(first + 1, 0, half), NT)
+            whole = mm(FL[0, region], pair_of(first), NT)
+            whole = whole + mm(FL[1, region, 0:half], unit_of(first + 2), NT)
             exchange_send(number_up + 1, 0, part, whole)
-        put_gradient(first + 1, mm(ACT[layer, 0], RV[...], TN), 0, half)
-        scatter_start(depth - 1, first + 1)
-        put_gradient(first, mm(ACT[layer, 0], RQK[...], TN))
-        scatter_start(depth - 1, first)
-        pump_to(step, 1)
-        scatter_step(depth - 1, first + 1)
-        scatter_step(depth - 1, first)
-        pump_to(step, 2)
+        from_core(3, 4)
+        pump_to(step, 3)
+        put_gradient(first + 2, mm(ACT[layer, 0], FL[1, :, 0:half], TN))
+        grad_qk = mm(ACT[layer, 0], FL[0], TN)
+        put_gradient(first + 1, grad_qk[:, half:])
+        put_gradient(first, grad_qk[:, :half])
+        for n in (2, 1, 0):
+            from_core(n, n + 1)
+        pump_to(step, 4)
 
         @pl.when(step + 1 == L)
         def _():
@@ -663,41 +804,47 @@
     lines.append(jnp.zeros((LANES - L * VEC_ROWS, Dp), F32))
     turned = jnp.concatenate(lines, axis=0).T.reshape(axes + (rp, LANES))
     SG[(slice(None),) * depth + (slice(0, rp), slice(None))] = turned
-    scatter_start(depth - 1, small_index, True)
+    scatter_begin(depth - 1, small_index, straight, True)
     for part in range(2):
         exchange_send(2 * L - 1, 1, part, LAST[pl.ds(part * chunk, chunk)])
     gin_ref[...] = DX[...]
-    scatter_step(depth - 1, small_index, True)
+    scatter_hop(0, small_index, straight, True)
+    pump_rest()
     for part in range(2):
         region = pl.ds(part * chunk, chunk)
         value = MID[region] + exchange_sum(2 * L - 1, 1, part) + VEC[L - 1, 5:6]
         out_ref[region] = value.astype(BF)
     exchange_done(2 * L - 1, 1)
-    lax.fori_loop(pumped(L - 1, len(PUMPS) - 1), L * NP + depth - 2, pump, 0)
-    for k in range(depth - 2, -1, -1):
-        scatter_step(k, small_index, True)
-    for piece in range(L * NP):
-        scatter_drain(piece)
+    for unit in range(L * NP):
+        scatter_drain(unit)
     scatter_drain(small_index, True)
 
 
-PUMPS = ((1, 5), (2, 7), (3, 8))
+PUMPS = (
+    ((0, 0, 0, 0), (9, 7, 5, 3)),
+    ((2, 1, 0, 0), (12, 9, 7, 5)),
+    ((3, 2, 1, 0), (13, 11, 9, 7)),
+    ((5, 2, 1, 0), (15, 13, 11, 9)),
+    ((7, 5, 3, 2), (18, 15, 13, 11)),
+)
 
 
 def run_kernel(plan, frames, cotangent, shards, small):
-    L, NP, Dp, rp, rows = plan.layers, plan.pieces, plan.padded, plan.block, plan.rows
+    L, NP, Dp, rp, rows = plan.layers, plan.units, plan.padded, plan.block, plan.rows
     axes = plan.axes
     depth = len(axes)
-    UP = plan.up_pieces
-    piece = plan.piece
+    half = plan.half
+    UP = plan.ups // 2
+    piece = 2 * half
     landings = []
     small_landings = []
     for k, size in enumerate(axes):
         number = NP if k == depth - 1 else L * NP
-        landings.append(pltpu.VMEM((number, size - 1) + axes[:k] + (rp, piece), BF))
-        small_landings.append(pltpu.VMEM((size - 1,) + axes[:k] + (rp + BIAS_ROWS, LANES), F32))
+        slots = 1 if size == 2 else 5
+        landings.append(pltpu.VMEM((number,) + axes[:k] + (slots, rp, half), BF))
+        small_landings.append(pltpu.VMEM(axes[:k] + (slots, rp + BIAS_ROWS, LANES), F32))
     scratch = [
-        pltpu.VMEM((L * NP,) + axes + (rp, piece), BF),
+        pltpu.VMEM((L * NP,) + axes + (rp, half), BF),
         pltpu.VMEM(axes + (rp + BIAS_ROWS, LANES), BF),
         pltpu.VMEM((L, VEC_ROWS, Dp), F32),
         pltpu.VMEM((L, 1, plan.bias_cols), F32),
@@ -712,16 +859,13 @@
         pltpu.VMEM((L, plan.pairs, rows, LANES), BF),
         pltpu.VMEM((L, plan.pairs, rows, LANES), BF),
         pltpu.VMEM((L, plan.pairs, rows, LANES), BF),
-        pltpu.VMEM((L, plan.pairs, LANES // HD, rows, 1), F32),
+        pltpu.VMEM((L, plan.pairs, rows, LANES), F32),
         pltpu.VMEM((L, plan.pairs, rows, LANES), BF),
         pltpu.VMEM((L, UP, rows, piece), BF),
         pltpu.VMEM((L, UP, rows, piece), BF),
         pltpu.VMEM((rows, Dp), F32),
         pltpu.VMEM((rows, Dp), BF),
         pltpu.VMEM((UP, rows, piece), BF),
-        pltpu.VMEM((plan.pairs, rows, LANES), BF),
-        pltpu.VMEM((rows, piece), BF),
-        pltpu.VMEM((rows, plan.half), BF),
         pltpu.VMEM((L, VEC_ROWS, Dp), F32),
         pltpu.VMEM((L, 1, plan.bias_cols), F32),
         pltpu.VMEM((HD, LANES), F32),
@@ -740,7 +884,7 @@
         out_shape=(
             jax.ShapeDtypeStruct((rows, Dp), BF),
             jax.ShapeDtypeStruct((rows, Dp), F32),
-            jax.ShapeDtypeStruct((L * NP, rp, piece), F32),
+            jax.ShapeDtypeStruct((L * NP, rp, half), F32),
             jax.ShapeDtypeStruct((rp + BIAS_ROWS, LANES), F32),
         ),
         in_specs=[pl.BlockSpec(memory_space=pltpu.VMEM)] * 4,
@@ -776,7 +920,7 @@
     half = w_qkv.shape[3]
     hidden = w_up.shape[2]
     plan = Plan(count, rows, width, half, hidden, L)
-    own, rp, piece, UP = plan.own, plan.block, plan.piece, plan.up_pieces
+    own, rp, UP = plan.own, plan.block, plan.ups
 
     def spread_features(values):
         if rp == own:
@@ -792,10 +936,10 @@
     low_out = w_out.astype(BF).transpose(0, 2, 1)
     low_up = w_up.astype(BF)
     low_down = w_down.astype(BF).transpose(0, 2, 1)
-    parts = [low_qkv[:, :, :piece], jnp.concatenate([low_qkv[:, :, piece:], low_out], axis=2)]
-    parts += [low_up[:, :, n * piece : (n + 1) * piece] for n in range(UP)]
-    parts += [low_down[:, :, n * piece : (n + 1) * piece] for n in range(UP)]
-    shards = jnp.stack(parts, axis=1).reshape(L * plan.pieces, own, piece)
+    parts = [low_qkv[:, :, n * half : (n + 1) * half] for n in range(3)] + [low_out]
+    parts += [low_up[:, :, n * half : (n + 1) * half] for n in range(UP)]
+    parts += [low_down[:, :, n * half : (n + 1) * half] for n in range(UP)]
+    shards = jnp.stack(parts, axis=1).reshape(L * plan.units, own, half)
     shards = pad_axis(shards, 1, rp)
 
     quarter = plan.quarter
@@ -817,11 +961,11 @@
         plan, spread_features(frames), spread_features(cotangent), shards, small
     )
 
-    wide = wide.reshape(L, plan.pieces, rp, piece)[:, :, :own]
-    grad_qkv = jnp.concatenate([wide[:, 0], wide[:, 1, :, :half]], axis=2).reshape(w_qkv.shape)
-    grad_out = wide[:, 1, :, half:].transpose(0, 2, 1)
-    grad_up = jnp.concatenate([wide[:, 2 + n] for n in range(UP)], axis=2)
-    grad_down = jnp.concatenate([wide[:, 2 + UP + n] for n in range(UP)], axis=2).transpose(0, 2, 1)
+    wide = wide.reshape(L, plan.units, rp, half)[:, :, :own]
+    grad_qkv = jnp.stack([wide[:, n] for n in range(3)], axis=2)
+    grad_out = wide[:, 3].transpose(0, 2, 1)
+    grad_up = jnp.concatenate([wide[:, 4 + n] for n in range(UP)], axis=2)
+    grad_down = jnp.concatenate([wide[:, 4 + UP + n] for n in range(UP)], axis=2).transpose(0, 2, 1)
     vec_grad = small_grad[:own, : L * VEC_ROWS].reshape(own, L, VEC_ROWS)[:, :, : vectors.shape[1]]
     grad_vec = vec_grad.transpose(1, 2, 0)
     bias_grad = small_grad[rp : rp + quarter, : L * groups].reshape(quarter, L, groups)

time: 259 us -> 220 us (0.85)
  Pallas kernels: 238 us -> 200 us
    pallas_call x1, Pallas kernels: 238 us -> 200 us  [run_kernel(): pl.pallas_call(functools.partial(train_kernel, plan), out_shape=(jax.Shap...]
where the time goes in v2:
time: 220 us
  Pallas kernels  200 us (91%)
  other arithmetic  10.4 us (5%)
  local copies, waits for them, and re-layouts  8.37 us (4%)
    pallas_call x1, Pallas kernels, run_kernel(): pl.pallas_call(functools.partial(train_kernel, plan), out_shape=(jax.Shap...  200 us
    sub x7, other arithmetic, adamw(): weight - rate * (first_hat / (jnp.sqrt(second_hat) + adam_eps) + decay *...  7.57 us
    unnamed x75, local copies, waits for them, and re-layouts  5.09 us

profile of v2, /device:TPU:0, one launch (start us, length us, event | category | flops | bytes accessed | tf_op | source)
XLA Modules:
  0.0 220.1 jit_solution(8087117272745323193)
XLA Ops:
  0.7 0.0 copy-start
  0.7 0.0 copy-start.2
  0.7 1.1 convert_bitcast_fusion.1
  1.9 0.9 bitcast_dynamic-update-slice_fusion
  2.9 0.0 copy-done
  2.9 0.0 copy-start.21
  3.0 0.0 copy-start.16
  3.0 0.0 copy-start.18
  3.0 0.0 copy-done.2
  3.2 1.0 copy.117
  4.2 0.0 copy-done.21
  4.2 0.0 copy-done.16
  4.2 0.1 reshape.90
  4.3 0.1 maximum_bitcast_fusion.1
  4.4 0.1 reshape.91
  4.5 0.0 copy-done.18
  4.5 0.1 copy.119
  4.6 0.6 fusion.17.small_ref
  5.2 200.3 %train_step.1 = (bf16[256,768]{1,0:T(8,128)(2,1)}, f32[256,768]{1,0:T(8,128)}, f32[24,48,384]{2,1,0:T(8,128)}, f32[64,128]{1,0:T(8,128)}) custom-call(bf16[256,768]{1,0:T(8,128)(2,1)} %frames_ref.1, bf16[256,768]{1,0:T(8,128)(2,1)} %cot_ref.1, bf16[24,48,384]{2,1,0:T(8,128)(2,1)} %bitcast.132, bf16[64,128]{1,0:T(8,128)(2,1)} %fusion.17.small_ref), custom_call_target="tpu_custom_call" | custom-call | tf_op jit(solution)/shard_map/train_step/pallas_call | solution.py:882
  205.5 0.0 copy-start.4
  205.5 0.0 copy-start.11
  205.5 0.0 copy-start.12
  205.5 1.7 slice_bitcast_fusion.3
  207.2 0.0 copy-done.4
  207.2 0.0 copy-done.11
  207.2 0.1 copy-done.12
  207.4 0.0 copy-start.6
  207.4 0.0 copy-start.7
  207.4 1.3 multiply_subtract_fusion.2
  208.7 0.0 copy-done.10
  208.7 0.0 copy-done.14
  208.7 0.0 copy-done.15
  208.7 1.8 multiply_subtract_fusion.3
  210.5 0.0 copy-done.1
  210.5 0.0 copy-done.6
  210.5 0.0 copy-done.7
  210.5 0.0 copy-start.3
  210.5 0.0 copy-start.8
  210.5 0.0 copy-start.9
  210.6 1.6 multiply_subtract_fusion.1
  212.1 0.0 copy-done.8
  212.1 0.6 copy-done.9
  212.7 0.0 copy-start.22
  212.8 0.0 copy-start.27
  212.8 0.0 copy-start.28
  212.8 0.0 copy-start.19
  212.8 0.0 copy-start.25
  212.8 0.0 copy-start.26
  212.8 1.6 multiply_subtract_fusion
  214.4 0.0 copy-done.20
  214.4 0.1 reshape.93
  214.5 0.1 reshape.94
  214.6 0.0 copy-done.17
  214.6 0.6 multiply_subtract_fusion.4
  215.2 0.0 copy-done.27
  215.2 0.7 multiply_subtract_fusion.5
  215.9 0.1 copy.135
  216.0 0.6 copy.144
  216.6 0.6 copy.145
  217.3 0.6 copy.146
  217.8 0.6 copy.147
  218.4 0.7 copy.194
  219.2 0.0 copy-done.5
  219.2 0.9 copy.195
  (45 shorter events, 0.4 us)
Async XLA Ops:
  0.7 2.2 copy-start
  0.7 2.4 %copy-start.2 = (f32[2,1536,48]{1,2,0:T(8,128)S(1)}, f32[2,1536,48]{1,2,0:T(8,128)}, u32[]{:S(2)}) copy-start(f32[2,1536,48]{1,2,0:T(8,128)} %param.28) | copy-start | bytes 1769476
  2.9 1.2 copy-start.21
  3.0 1.2 copy-start.16
  3.0 1.5 copy-start.18
  205.5 1.7 copy-start.4
  205.5 1.7 copy-start.11
  205.5 1.9 copy-start.12
  207.4 1.3 copy-start.10
  207.4 1.3 copy-start.14
  207.4 1.3 copy-start.15
  207.4 3.1 %copy-start.1 = (f32[2,48,1536]{2,1,0:T(8,128)S(1)}, f32[2,48,1536]{2,1,0:T(8,128)}, u32[]{:S(2)}) copy-start(f32[2,48,1536]{2,1,0:T(8,128)} %param.27) | copy-start | bytes 1769476
  207.4 3.1 %copy-start.6 = (f32[2,48,1536]{2,1,0:T(8,128)S(1)}, f32[2,48,1536]{2,1,0:T(8,128)}, u32[]{:S(2)}) copy-start(f32[2,48,1536]{2,1,0:T(8,128)} %param.34) | copy-start | bytes 1769476
  207.4 3.1 %copy-start.7 = (f32[2,48,1536]{2,1,0:T(8,128)S(1)}, f32[2,48,1536]{2,1,0:T(8,128)}, u32[]{:S(2)}) copy-start(f32[2,48,1536]{2,1,0:T(8,128)} %param.41) | copy-start | bytes 1769476
  210.5 1.6 copy-start.3
  210.5 1.6 copy-start.8
  210.5 2.2 copy-start.9
  212.7 1.7 copy-start.20
  212.7 1.9 copy-start.17
  212.7 1.9 copy-start.23
  212.7 1.9 copy-start.24
  212.7 2.5 %copy-start.22 = (f32[2,24,4]{1,2,0:T(4,128)S(1)}, f32[2,24,4]{1,2,0:T(4,128)}, u32[]{:S(2)}) copy-start(f32[2,24,4]{1,2,0:T(4,128)} %param.30) | copy-start | bytes 2308
  212.8 2.5 %copy-start.27 = (f32[2,24,4]{1,2,0:T(4,128)S(1)}, f32[2,24,4]{1,2,0:T(4,128)}, u32[]{:S(2)}) copy-start(f32[2,24,4]{1,2,0:T(4,128)} %param.37) | copy-start | bytes 2308
  212.8 2.5 %copy-start.28 = (f32[2,24,4]{1,2,0:T(4,128)S(1)}, f32[2,24,4]{1,2,0:T(4,128)}, u32[]{:S(2)}) copy-start(f32[2,24,4]{1,2,0:T(4,128)} %param.44) | copy-start | bytes 2308
  212.8 3.8 %copy-start.19 = (f32[2,6,48]{2,0,1:T(2,128)S(1)}, f32[2,6,48]{2,0,1:T(2,128)}, u32[]{:S(2)}) copy-start(f32[2,6,48]{2,0,1:T(2,128)} %param.31) | copy-start | bytes 6916
  212.8 3.8 %copy-start.25 = (f32[2,6,48]{2,0,1:T(2,128)S(1)}, f32[2,6,48]{2,0,1:T(2,128)}, u32[]{:S(2)}) copy-start(f32[2,6,48]{2,0,1:T(2,128)} %param.38) | copy-start | bytes 6916
  212.8 3.8 %copy-start.26 = (f32[2,6,48]{2,0,1:T(2,128)S(1)}, f32[2,6,48]{2,0,1:T(2,128)}, u32[]{:S(2)}) copy-start(f32[2,6,48]{2,0,1:T(2,128)} %param.45) | copy-start | bytes 6916
  212.8 5.6 %copy-start.13 = (bf16[256,768]{1,0:T(8,128)(2,1)S(1)}, bf16[256,768]{1,0:T(8,128)(2,1)}, u32[]{:S(2)}) copy-start(bf16[256,768]{1,0:T(8,128)(2,1)} %get-tuple-element.196) | copy-start | bytes 1179652
  212.8 6.4 %copy-start.5 = (f32[256,768]{1,0:T(8,128)S(1)}, f32[256,768]{1,0:T(8,128)}, u32[]{:S(2)}) copy-start(f32[256,768]{1,0:T(8,128)} %get-tuple-element.197) | copy-start | bytes 2359300

commit v3 on v2

--- a/solution.py
+++ b/solution.py
@@ -28,6 +28,7 @@
 MESH = pl.DeviceIdType.MESH
 LANES = 128
 BIAS_ROWS = 16
+TURN_EVERY = 6
 VEC_ROWS = 8
 
 
@@ -43,6 +44,15 @@
         sizes.append(step)
         chips //= step
     return tuple(sizes) + (2,)
+
+
+LEADS = (6, 5, 3, 1, 0)
+TURNED_LEADS = (8, 7, 5, 1, 0)
+
+
+def spread_leads(leads, hops):
+    extra = hops - len(leads)
+    return [leads[0] + extra - n for n in range(extra)] + list(leads)
 
 
 class Plan:
@@ -70,6 +80,7 @@
         self.hops = tuple(1 if size == 2 else 3 for size in self.axes)
         self.slots = sum(self.hops)
         self.chunk = rows // 2
+        self.early = TURN_EVERY - 1 if self.axes[:2] == (4, 2) else 0
 
 
 def train_kernel(
@@ -109,6 +120,7 @@
     TURN,
     SG,
     RBs,
+    RBt,
     RSs,
     ag_send,
     ag_recv,
@@ -182,6 +194,14 @@
 
     small_index = L * NP
     straight = tuple(range(depth))
+    turned = (1, 0) + straight[2:]
+    early = plan.early
+
+    def gather_turned(unit):
+        return lax.rem(unit, TURN_EVERY) == TURN_EVERY - 1
+
+    def gather_order(unit):
+        return turned if unit % TURN_EVERY == TURN_EVERY - 1 else straight
 
     def gather_copy(k, hop, unit, order, small, sending):
         done = order[: order.index(k)]
@@ -210,8 +230,42 @@
         slot = slot_of[k] + hop
         return remote(src, dst, ag_send.at[unit, slot], ag_recv.at[unit, slot], device(k, target))
 
+    def early_copy(value, slot, unit, sending):
+        own = value is digit[0]
+        spot = (value, digit[1] if sending else 1 - digit[1]) + tuple(digit[2:])
+        dst = W.at[(unit,) + spot]
+        src = shard_ref.at[unit] if own and sending else dst
+        target = device(1, 1 - digit[1])
+        return remote(src, dst, ag_send.at[unit, slot], ag_recv.at[unit, slot], target)
+
+    def early_own(unit, sending):
+        return early_copy(digit[0], plan.slots, unit, sending)
+
+    def early_rest(unit, sending, act):
+        @pl.when(outer[0])
+        def _():
+            act(early_copy(three[0], slot_of[1], unit, sending))
+
+        @pl.when(inner[0])
+        def _():
+            act(early_copy(mine_out[0], slot_of[1], unit, sending))
+            act(early_copy(far[0], plan.slots + 1, unit, sending))
+
+    def is_early(k, order, small):
+        return bool(early) and k == 1 and order == straight and not small
+
     def gather_begin(k, unit, order, small):
-        if axes[k] == 2:
+        if is_early(k, order, small):
+
+            @pl.when(unit < early)
+            def _():
+                early_rest(unit, True, lambda copy: copy.start())
+
+            @pl.when(unit >= early)
+            def _():
+                gather_copy(k, 0, unit, order, small, True).start()
+
+        elif axes[k] == 2:
             gather_copy(k, 0, unit, order, small, True).start()
         else:
 
@@ -230,7 +284,19 @@
                 break
             index -= plan.hops[k]
         if axes[k] == 2:
-            gather_copy(k, 0, unit, order, small, False).wait_recv()
+            if is_early(k, order, small):
+
+                @pl.when(unit < early)
+                def _():
+                    early_own(unit, False).wait_recv()
+                    early_rest(unit, False, lambda copy: copy.wait_recv())
+
+                @pl.when(unit >= early)
+                def _():
+                    gather_copy(k, 0, unit, order, small, False).wait_recv()
+
+            else:
+                gather_copy(k, 0, unit, order, small, False).wait_recv()
             gather_next(k, unit, order, small)
             return
 
@@ -242,29 +308,48 @@
             if index > 0:
                 gather_next(k, unit, order, small)
 
-    def gather_drain(unit, small=False):
+    def gather_drain(unit, order, small=False):
         for k in range(depth):
             for hop in range(plan.hops[k]):
-                if axes[k] == 2:
-                    gather_copy(k, hop, unit, straight, small, True).wait_send()
+                if is_early(k, order, small):
+
+                    @pl.when(unit < early)
+                    def _():
+                        early_own(unit, True).wait_send()
+                        early_rest(unit, True, lambda copy: copy.wait_send())
+
+                    @pl.when(unit >= early)
+                    def _():
+                        gather_copy(k, hop, unit, order, small, True).wait_send()
+
+                elif axes[k] == 2:
+                    gather_copy(k, hop, unit, order, small, True).wait_send()
                 else:
 
                     @pl.when(outer[k] if hop == 0 else inner[k])
                     def _():
-                        gather_copy(k, hop, unit, straight, small, True).wait_send()
+                        gather_copy(k, hop, unit, order, small, True).wait_send()
 
     hops = plan.slots
-
-    def gather_ahead(n, low, high):
-        for index in range(low, high):
-            unit = n + (hops - 1 - index if index < hops - 2 else 0)
-
-            @pl.when((unit >= 0) & (unit < L * NP))
+    leads = spread_leads(LEADS, hops)
+    turned_leads = spread_leads(TURNED_LEADS, hops)
+
+    def gather_tick(n, carry=0):
+        for index in range(hops):
+            ahead = n + leads[index]
+            inside = (ahead >= 0) & (ahead < L * NP)
+
+            @pl.when(inside & jnp.logical_not(gather_turned(ahead)))
             def _():
-                gather_hop(index, unit, straight, False)
-
-    def gather_tick(n, carry=0):
-        gather_ahead(n, 0, hops)
+                gather_hop(index, ahead, straight, False)
+
+            further = n + turned_leads[index]
+            inside = (further >= 0) & (further < L * NP)
+
+            @pl.when(inside & gather_turned(further))
+            def _():
+                gather_hop(index, further, turned, False)
+
         return carry
 
     def ready(low, high):
@@ -272,15 +357,20 @@
 
     gather_begin(0, small_index, straight, True)
     for unit in range(L * NP):
-        gather_begin(0, unit, straight, False)
+        order = gather_order(unit)
+        gather_begin(order[0], unit, order, False)
+        if unit < early:
+            early_own(unit, True).start()
     here = tuple(digit)
     SB[here] = small_ref[...]
     for unit in range(L * NP):
         W[(unit,) + here] = shard_ref[unit]
-    for index in range(hops):
-        gather_hop(index, small_index, straight, True)
-        if index < hops - 1:
-            gather_ahead(index - (hops - 1), 0, hops)
+    before = max(max(leads), hops)
+    for n in range(-before, 0):
+        gather_tick(n)
+        index = n + before
+        if index < hops:
+            gather_hop(index, small_index, straight, True)
 
     vec_all = SB[(slice(None),) * depth + (slice(0, rp), slice(None))]
     vec_rows = vec_all.reshape(Dp, LANES).astype(F32).T
@@ -369,6 +459,159 @@
     head_mask = [((lane // HD) == h).astype(F32).astype(BF) for h in range(LANES // HD)]
     scale = HD ** (-0.5)
     clips = rows // SEQ
+
+    def landing(k, order, unit):
+        if k == depth - 1:
+            return lax.rem(unit, NP)
+        if k > 1:
+            return unit
+        m = production(unit)
+        return m // TURN_EVERY if order == turned else m - m // TURN_EVERY - 1
+
+    def production(unit):
+        name = lax.rem(unit, NP)
+        turn = jnp.where(
+            name >= 4 + UP,
+            name - 4 - UP,
+            jnp.where(name >= 4, name - 4 + UP, NP - 1 - name),
+        )
+        return (L - 1 - unit // NP) * NP + turn
+
+    def land(k, order, slots):
+        done = order[order.index(k) + 1 :]
+        return tuple(slots if a == k else slice(None) for a in range(depth) if a not in done)
+
+    def landing_ref(k, order):
+        return RBt[k] if order == turned and k < 2 else RBs[k]
+
+    def scatter_spot(k, order, value):
+        done = order[order.index(k) + 1 :]
+        return tuple(
+            digit[a] if a in done else value if a == k else slice(None) for a in range(depth)
+        )
+
+    def scatter_copy(k, hop, unit, order, small):
+        if axes[k] == 2:
+            value, target, slots = 1 - digit[k], 1 - digit[k], 0
+        elif hop == 0:
+            value, target, slots = three[k], mine_in[k], pl.ds(0, 3)
+        elif hop == 1:
+            value, target, slots = far[k], far_in[k], pl.ds(3, 2)
+        else:
+            value, target, slots = mine_out[k], mine_out[k], 0
+        spot = scatter_spot(k, order, value)
+        if small:
+            src, dst = SG.at[spot], RSs[k].at[land(k, order, slots)]
+        else:
+            src, dst = W.at[(unit,) + spot], landing_ref(k, order).at[(landing(k, order, unit),) + land(k, order, slots)]
+        slot = slot_of[k] + hop
+        return remote(src, dst, rs_send.at[unit, slot], rs_recv.at[unit, slot], device(k, target))
+
+    def scatter_begin(k, unit, order, small=False):
+        if axes[k] == 2:
+            scatter_copy(k, 0, unit, order, small).start()
+        else:
+
+            @pl.when(outer[k])
+            def _():
+                scatter_copy(k, 0, unit, order, small).start()
+
+    def held(small, unit, spot):
+        return SG[spot] if small else W[(unit,) + spot].astype(F32)
+
+    def arrived(k, order, small, unit, slots):
+        if small:
+            return RSs[k][land(k, order, slots)]
+        spot = (landing(k, order, unit),) + land(k, order, slots)
+        return landing_ref(k, order)[spot].astype(F32)
+
+    def keep(small, unit, spot, value):
+        if small:
+            SG[spot] = value
+        else:
+            W[(unit,) + spot] = value.astype(BF)
+
+    def finish(k, unit, order, small, slots):
+        spot = scatter_spot(k, order, digit[k])
+        value = held(small, unit, spot) + arrived(k, order, small, unit, slots)
+        position = order.index(k)
+        if position > 0:
+            keep(small, unit, spot, value)
+            scatter_begin(order[position - 1], unit, order, small)
+        elif small:
+            smallg_ref[...] = value
+        else:
+            gout_ref[unit] = value
+
+    def add_in(k, unit, order, small, value, slots):
+        spot = scatter_spot(k, order, value)
+        keep(small, unit, spot, held(small, unit, spot) + arrived(k, order, small, unit, slots))
+
+    def scatter_hop(index, unit, order, small=False):
+        for k in reversed(order):
+            if index < plan.hops[k]:
+                break
+            index -= plan.hops[k]
+        if axes[k] == 2:
+            scatter_copy(k, 0, unit, order, small).wait_recv()
+            finish(k, unit, order, small, 0)
+            return
+
+        @pl.when(outer[k] if index == 2 else inner[k])
+        def _():
+            scatter_copy(k, index, unit, order, small).wait_recv()
+            if index == 0:
+                add_in(k, unit, order, small, three[k], pl.ds(0, 3))
+                scatter_copy(k, 1, unit, order, small).start()
+            elif index == 1:
+                add_in(k, unit, order, small, mine_out[k], 3 + mine_out[k] - 2 * half_side[k])
+                scatter_copy(k, 2, unit, order, small).start()
+                finish(k, unit, order, small, 3 + digit[k] - 2 * half_side[k])
+            else:
+                finish(k, unit, order, small, 0)
+
+    def scatter_drain(unit, order, small=False):
+        for k in range(depth):
+            for hop in range(plan.hops[k]):
+                if axes[k] == 2:
+                    scatter_copy(k, hop, unit, order, small).wait_send()
+                else:
+
+                    @pl.when(outer[k] if hop == 0 else inner[k])
+                    def _():
+                        scatter_copy(k, hop, unit, order, small).wait_send()
+
+    block_shape = axes + (rp,)
+
+    def put_gradient(index, value):
+        W[index] = value.astype(BF).reshape(block_shape + (half,))
+        scatter_begin(depth - 1, index, straight)
+
+    def put_pair(index, value):
+        put_gradient(index, value[:, :half])
+        put_gradient(index + 1, value[:, half:])
+
+    def column_sum(values):
+        return jnp.sum(values, axis=0, keepdims=True)
+
+    def drain_down(unit):
+        for order in (straight, turned):
+
+            @pl.when(gather_turned(unit) == (order == turned))
+            def _():
+                gather_drain(unit, order)
+
+    def down_gradient(layer, number):
+        down = layer * NP + 4 + UP
+        grad = mm(LOW[...], pair_of(down + number), NN) * SLOPE[layer, number // 2].astype(F32)
+        low = (2 + number) * half
+        BG[layer, :, low : low + 2 * half] = column_sum(grad)
+        FL[number // 2] = grad.astype(BF)
+        put_pair(down + number, mm(LOW[...], HIDDEN[layer, number // 2], TN))
+
+    LOW[...] = cot_ref[...]
+    VG[...] = jnp.zeros(VG.shape, F32)
+    SG[...] = jnp.zeros(SG.shape, F32)
 
     def attend(layer):
         def one(item, _):
@@ -468,125 +711,15 @@
                 def _():
                     LAST[...] = whole.astype(BF)
 
+            @pl.when(layer + 1 == L)
+            def _():
+                for unit in (down + number, down + number + 1):
+                    drain_down(unit)
+                down_gradient(layer, number)
+
         return carry
 
     lax.fori_loop(0, L, forward_layer, 0)
-
-    def landing(k, unit):
-        return lax.rem(unit, NP) if k == depth - 1 else unit
-
-    def land(k, slots):
-        return (slice(None),) * k + (slots,)
-
-    def scatter_spot(k, order, value):
-        done = order[order.index(k) + 1 :]
-        return tuple(
-            digit[a] if a in done else value if a == k else slice(None) for a in range(depth)
-        )
-
-    def scatter_copy(k, hop, unit, order, small):
-        if axes[k] == 2:
-            value, target, slots = 1 - digit[k], 1 - digit[k], 0
-        elif hop == 0:
-            value, target, slots = three[k], mine_in[k], pl.ds(0, 3)
-        elif hop == 1:
-            value, target, slots = far[k], far_in[k], pl.ds(3, 2)
-        else:
-            value, target, slots = mine_out[k], mine_out[k], 0
-        spot = scatter_spot(k, order, value)
-        if small:
-            src, dst = SG.at[spot], RSs[k].at[land(k, slots)]
-        else:
-            src, dst = W.at[(unit,) + spot], RBs[k].at[(landing(k, unit),) + land(k, slots)]
-        slot = slot_of[k] + hop
-        return remote(src, dst, rs_send.at[unit, slot], rs_recv.at[unit, slot], device(k, target))
-
-    def scatter_begin(k, unit, order, small=False):
-        if axes[k] == 2:
-            scatter_copy(k, 0, unit, order, small).start()
-        else:
-
-            @pl.when(outer[k])
-            def _():
-                scatter_copy(k, 0, unit, order, small).start()
-
-    def held(small, unit, spot):
-        return SG[spot] if small else W[(unit,) + spot].astype(F32)
-
-    def arrived(k, small, unit, slots):
-        if small:
-            return RSs[k][land(k, slots)]
-        return RBs[k][(landing(k, unit),) + land(k, slots)].astype(F32)
-
-    def keep(small, unit, spot, value):
-        if small:
-            SG[spot] = value
-        else:
-            W[(unit,) + spot] = value.astype(BF)
-
-    def finish(k, unit, order, small, slots):
-        spot = scatter_spot(k, order, digit[k])
-        value = held(small, unit, spot) + arrived(k, small, unit, slots)
-        position = order.index(k)
-        if position > 0:
-            keep(small, unit, spot, value)
-            scatter_begin(order[position - 1], unit, order, small)
-        elif small:
-            smallg_ref[...] = value
-        else:
-            gout_ref[unit] = value
-
-    def add_in(k, unit, order, small, value, slots):
-        spot = scatter_spot(k, order, value)
-        keep(small, unit, spot, held(small, unit, spot) + arrived(k, small, unit, slots))
-
-    def scatter_hop(index, unit, order, small=False):
-        for k in reversed(order):
-            if index < plan.hops[k]:
-                break
-            index -= plan.hops[k]
-        if axes[k] == 2:
-            scatter_copy(k, 0, unit, order, small).wait_recv()
-            finish(k, unit, order, small, 0)
-            return
-
-        @pl.when(outer[k] if index == 2 else inner[k])
-        def _():
-            scatter_copy(k, index, unit, order, small).wait_recv()
-            if index == 0:
-                add_in(k, unit, order, small, three[k], pl.ds(0, 3))
-                scatter_copy(k, 1, unit, order, small).start()
-            elif index == 1:
-                add_in(k, unit, order, small, mine_out[k], 3 + mine_out[k] - 2 * half_side[k])
-                scatter_copy(k, 2, unit, order, small).start()
-                finish(k, unit, order, small, 3 + digit[k] - 2 * half_side[k])
-            else:
-                finish(k, unit, order, small, 0)
-
-    def scatter_drain(unit, small=False):
-        for k in range(depth):
-            for hop in range(plan.hops[k]):
-                if axes[k] == 2:
-                    scatter_copy(k, hop, unit, straight, small).wait_send()
-                else:
-
-                    @pl.when(outer[k] if hop == 0 else inner[k])
-                    def _():
-                        scatter_copy(k, hop, unit, straight, small).wait_send()
-
-    block_shape = axes + (rp,)
-
-    def put_gradient(index, value):
-        W[index] = value.astype(BF).reshape(block_shape + (half,))
-        scatter_begin(depth - 1, index, straight)
-
-    def put_pair(index, value):
-        put_gradient(index, value[:, :half])
-        put_gradient(index + 1, value[:, half:])
-
-    for unit in range(L * NP):
-        gather_drain(unit)
-    gather_drain(small_index, True)
 
     def attend_back(layer):
         def one(item, _):
@@ -635,9 +768,6 @@
 
         lax.fori_loop(0, plan.pairs * clips, one, 0)
 
-    def column_sum(values):
-        return jnp.sum(values, axis=0, keepdims=True)
-
     def norm_backward(upper, layer, which, region):
         hat = HAT[layer, which, region]
         scaled = upper * VEC[layer, 2 * which : 2 * which + 1]
@@ -652,7 +782,11 @@
             VG[layer, line : line + 1] += value
 
     DX[...] = cot_ref[...].astype(F32)
+    VG[L - 1, 5:6] = column_sum(DX[...])
     DMID = ACC
+    for unit in range((L - 1) * NP + 4 + UP):
+        gather_drain(unit, gather_order(unit))
+    gather_drain(small_index, straight, True)
 
     def produced(m):
         turn = lax.rem(m, NP)
@@ -670,43 +804,65 @@
             value = jnp.where(step == s, counts[min(s, len(counts) - 1)], value)
         return jnp.clip(value, 0, L * NP)
 
-    def pump_range(index, low, high):
-        def one(m, carry):
-            scatter_hop(index, produced(m), straight)
+    def scatter_either(index, m):
+        unit = produced(m)
+
+        @pl.when(lax.rem(m, TURN_EVERY) != 0)
+        def _():
+            scatter_hop(index, unit, straight)
+
+        @pl.when(lax.rem(m, TURN_EVERY) == 0)
+        def _():
+            scatter_hop(index, unit, turned)
+
+    def pump_between(lows, highs):
+        length = functools.reduce(jnp.maximum, [high - low for low, high in zip(lows, highs)])
+
+        def one(t, carry):
+            for index in range(1, hops):
+                m = lows[index - 1] + t
+
+                @pl.when(m < highs[index - 1])
+                def _():
+                    scatter_either(index, m)
+
             return carry
 
-        lax.fori_loop(low, high, one, 0)
+        lax.fori_loop(0, length, one, 0)
 
     def pump_to(step, place):
-        for index in range(1, hops):
-            if place == 0:
-                low = jnp.where(step == 0, 0, pumped(step - 1, len(PUMPS) - 1, index))
-            else:
-                low = pumped(step, place - 1, index)
-            pump_range(index, low, pumped(step, place, index))
+        if place == 0:
+            before = [
+                jnp.where(step == 0, 0, pumped(step - 1, len(PUMPS) - 1, index)) for index in range(1, hops)
+            ]
+        else:
+            before = [pumped(step, place - 1, index) for index in range(1, hops)]
+        pump_between(before, [pumped(step, place, index) for index in range(1, hops)])
+
+    def rest_order():
+        last = [row[-1] for row in PUMPS][-1]
+        done = [min(last[min(index, 4) - 1], L * NP) for index in range(1, 5)]
+        done += [0] * (hops - 5)
+        if hops == 5 and sum(done) + len(REST) == 4 * L * NP:
+            given = list(REST)
+        else:
+            done = [max(0, min(done[min(index, 4) - 1] - max(0, index - 4), L * NP)) for index in range(1, hops)]
+            left = [(m + 2 * index, index) for index in range(1, hops) for m in range(done[index - 1], L * NP)]
+            given = [index for _, index in sorted(left)]
+        events = []
+        for index in given:
+            events.append((index, done[index - 1]))
+            done[index - 1] += 1
+        return events
 
     def pump_rest():
-        last = len(PUMPS) - 1
-        start = PUMPS[last][-1][0]
-        delays = [0 if index == 1 else index for index in range(1, hops)]
-        for index in range(1, hops):
-            pump_range(index, pumped(L - 1, last, index), max(0, min(start - delays[index - 1], L * NP)))
-
-        def one(m, carry):
-            for index in range(1, hops):
-                earlier = m - delays[index - 1]
-
-                @pl.when((earlier >= 0) & (earlier < L * NP))
-                def _():
-                    scatter_hop(index, produced(earlier), straight)
-
-                @pl.when(earlier == L * NP)
-                def _():
-                    scatter_hop(index, small_index, straight, True)
-
-            return carry
-
-        lax.fori_loop(start, L * NP + 1 + max(delays), one, 0)
+        for index, m in rest_order():
+            name = m % NP
+            name = 4 + UP + name if name < UP else 4 + name - UP if name < 2 * UP else NP - 1 - name
+            unit = (L - 1 - m // NP) * NP + name
+            scatter_hop(index, unit, turned if m % TURN_EVERY == 0 else straight)
+            if m == L * NP - 1:
+                scatter_hop(index, small_index, straight, True)
 
     def backward_layer(step, carry):
         layer = L - 1 - step
@@ -717,26 +873,17 @@
 
         def from_core(low, high):
             for n in range(low, high):
-                scatter_hop(0, first + n, straight)
-
-        VG[layer] = jnp.zeros((VEC_ROWS, Dp), F32)
-        upper = DX[...]
-        VG[layer, 5:6] = column_sum(upper)
-        LOW[...] = upper.astype(BF)
-        for number in range(0, UP, 2):
-            grad = mm(LOW[...], pair_of(down + number), NN) * SLOPE[layer, number // 2].astype(F32)
-            low = (2 + number) * half
-            BG[layer, :, low : low + 2 * half] = column_sum(grad)
-            FL[number // 2] = grad.astype(BF)
-            put_pair(down + number, mm(LOW[...], HIDDEN[layer, number // 2], TN))
+                turn = n - 4 - UP if n >= 4 + UP else n - 4 + UP if n >= 4 else NP - 1 - n
+                scatter_hop(0, first + n, turned if turn % TURN_EVERY == 0 else straight)
+
         for part in range(2):
+            from_core(4 + UP + part * UP // 2, 4 + UP + (part + 1) * UP // 2)
             region = pl.ds(part * chunk, chunk)
             whole = None
             for number in range(0, UP, 2):
                 term = mm(FL[number // 2, region], pair_of(up + number), NT)
                 whole = term if whole is None else whole + term
             exchange_send(number_up, 1, part, whole)
-        from_core(4 + UP, 4 + 2 * UP)
         pump_to(step, 0)
         for number in range(0, UP, 2):
             put_pair(up + number, mm(ACT[layer, 1], FL[number // 2], TN))
@@ -781,8 +928,17 @@
             grad = exchange_sum(number_up + 1, 0, part)
             keep_rows(layer, 0, part, column_sum(grad * HAT[layer, 0, region]))
             keep_rows(layer, 1, part, column_sum(grad))
-            DX[region] = DMID[region] + norm_backward(grad, layer, 0, region)
+            upper = DMID[region] + norm_backward(grad, layer, 0, region)
+            DX[region] = upper
+            LOW[region] = upper.astype(BF)
         exchange_done(number_up + 1, 0)
+
+        @pl.when(step + 1 < L)
+        def _():
+            VG[layer - 1, 5:6] = column_sum(DX[...])
+            for number in range(0, UP, 2):
+                down_gradient(layer - 1, number)
+
         return carry
 
     def pack_biases():
@@ -797,13 +953,12 @@
             spot = static_place(owner) + (slice(rp, rp + plan.quarter), slice(None))
             SG[spot] = table[start : start + plan.quarter]
 
-    SG[...] = jnp.zeros(SG.shape, F32)
     lax.fori_loop(0, L, backward_layer, 0)
 
     lines = [VG[layer] for layer in range(L)]
     lines.append(jnp.zeros((LANES - L * VEC_ROWS, Dp), F32))
-    turned = jnp.concatenate(lines, axis=0).T.reshape(axes + (rp, LANES))
-    SG[(slice(None),) * depth + (slice(0, rp), slice(None))] = turned
+    columns = jnp.concatenate(lines, axis=0).T.reshape(axes + (rp, LANES))
+    SG[(slice(None),) * depth + (slice(0, rp), slice(None))] = columns
     scatter_begin(depth - 1, small_index, straight, True)
     for part in range(2):
         exchange_send(2 * L - 1, 1, part, LAST[pl.ds(part * chunk, chunk)])
@@ -816,16 +971,22 @@
         out_ref[region] = value.astype(BF)
     exchange_done(2 * L - 1, 1)
     for unit in range(L * NP):
-        scatter_drain(unit)
-    scatter_drain(small_index, True)
+        name = unit % NP
+        turn = name - 4 - UP if name >= 4 + UP else name - 4 + UP if name >= 4 else NP - 1 - name
+        scatter_drain(unit, turned if turn % TURN_EVERY == 0 else straight)
+    scatter_drain(small_index, straight, True)
 
 
 PUMPS = (
-    ((0, 0, 0, 0), (9, 7, 5, 3)),
-    ((2, 1, 0, 0), (12, 9, 7, 5)),
-    ((3, 2, 1, 0), (13, 11, 9, 7)),
-    ((5, 2, 1, 0), (15, 13, 11, 9)),
-    ((7, 5, 3, 2), (18, 15, 13, 11)),
+    ((0, 0, 0, 0), (12, 8, 5, 1)),
+    ((2, 0, 0, 0), (14, 9, 8, 1)),
+    ((4, 1, 0, 0), (16, 11, 8, 6)),
+    ((7, 3, 1, 0), (18, 13, 11, 6)),
+    ((8, 5, 1, 0), (20, 14, 13, 9)),
+)
+REST = (
+    1, 1, 2, 2, 2, 3, 4, 4, 4, 1, 2, 2, 2, 3, 3, 2, 3, 2, 3, 2, 1, 4, 4, 3,
+    3, 3, 2, 3, 4, 3, 4, 4, 4, 4, 3, 4, 4, 4, 4, 4,
 )
 
 
@@ -839,10 +1000,15 @@
     landings = []
     small_landings = []
     for k, size in enumerate(axes):
-        number = NP if k == depth - 1 else L * NP
+        turned_number = -(-L * NP // TURN_EVERY)
+        number = NP if k == depth - 1 else L * NP - turned_number if k < 2 else L * NP
         slots = 1 if size == 2 else 5
         landings.append(pltpu.VMEM((number,) + axes[:k] + (slots, rp, half), BF))
         small_landings.append(pltpu.VMEM(axes[:k] + (slots, rp + BIAS_ROWS, LANES), F32))
+    turned_landings = [
+        pltpu.VMEM((-(-L * NP // TURN_EVERY), 1 if axes[0] == 2 else 5, axes[1], rp, half), BF),
+        pltpu.VMEM((-(-L * NP // TURN_EVERY), 1 if axes[1] == 2 else 5, rp, half), BF),
+    ]
     scratch = [
         pltpu.VMEM((L * NP,) + axes + (rp, half), BF),
         pltpu.VMEM(axes + (rp + BIAS_ROWS, LANES), BF),
@@ -871,9 +1037,10 @@
         pltpu.VMEM((HD, LANES), F32),
         pltpu.VMEM(axes + (rp + BIAS_ROWS, LANES), F32),
         landings,
+        turned_landings,
         small_landings,
-        pltpu.SemaphoreType.DMA((L * NP + 1, plan.slots)),
-        pltpu.SemaphoreType.DMA((L * NP + 1, plan.slots)),
+        pltpu.SemaphoreType.DMA((L * NP + 1, plan.slots + (2 if plan.early else 0))),
+        pltpu.SemaphoreType.DMA((L * NP + 1, plan.slots + (2 if plan.early else 0))),
         pltpu.SemaphoreType.DMA((L * NP + 1, plan.slots)),
         pltpu.SemaphoreType.DMA((L * NP + 1, plan.slots)),
         pltpu.SemaphoreType.DMA((4 * L, 2)),

time: 220 us -> 205 us (0.932)
  Pallas kernels: 200 us -> 185 us
    pallas_call x1, Pallas kernels: 200 us -> 185 us  [run_kernel(): pl.pallas_call(functools.partial(train_kernel, plan), out_shape=(jax.Shap...]
where the time goes in v3:
time: 205 us
  Pallas kernels  185 us (90%)
  other arithmetic  10.4 us (5%)
  local copies, waits for them, and re-layouts  8.37 us (4%)
    pallas_call x1, Pallas kernels, run_kernel(): pl.pallas_call(functools.partial(train_kernel, plan), out_shape=(jax.Shap...  185 us
    sub x7, other arithmetic, adamw(): weight - rate * (first_hat / (jnp.sqrt(second_hat) + adam_eps) + decay *...  7.57 us
    unnamed x75, local copies, waits for them, and re-layouts  5.09 us

profile of v3, /device:TPU:0, one launch (start us, length us, event | category | flops | bytes accessed | tf_op | source)
XLA Modules:
  0.0 205.1 jit_solution(13215936934019290639)
XLA Ops:
  0.7 0.0 copy-start
  0.7 0.0 copy-start.2
  0.7 1.1 convert_bitcast_fusion.1
  1.9 0.9 bitcast_dynamic-update-slice_fusion
  2.9 0.0 copy-done
  2.9 0.0 copy-start.21
  3.0 0.0 copy-start.16
  3.0 0.0 copy-start.18
  3.0 0.0 copy-done.2
  3.2 1.0 copy.117
  4.2 0.0 copy-done.21
  4.2 0.0 copy-done.16
  4.2 0.1 reshape.90
  4.3 0.1 maximum_bitcast_fusion.1
  4.4 0.1 reshape.91
  4.5 0.0 copy-done.18
  4.5 0.1 copy.119
  4.6 0.6 fusion.17.small_ref
  5.2 185.2 %train_step.1 = (bf16[256,768]{1,0:T(8,128)(2,1)}, f32[256,768]{1,0:T(8,128)}, f32[24,48,384]{2,1,0:T(8,128)}, f32[64,128]{1,0:T(8,128)}) custom-call(bf16[256,768]{1,0:T(8,128)(2,1)} %frames_ref.1, bf16[256,768]{1,0:T(8,128)(2,1)} %cot_ref.1, bf16[24,48,384]{2,1,0:T(8,128)(2,1)} %bitcast.132, bf16[64,128]{1,0:T(8,128)(2,1)} %fusion.17.small_ref), custom_call_target="tpu_custom_call" | custom-call | tf_op jit(solution)/shard_map/train_step/pallas_call | solution.py:1049
  190.5 0.0 copy-start.4
  190.5 0.0 copy-start.11
  190.5 0.0 copy-start.12
  190.5 1.7 slice_bitcast_fusion.3
  192.2 0.0 copy-done.4
  192.2 0.0 copy-done.11
  192.2 0.1 copy-done.12
  192.4 0.0 copy-start.6
  192.4 0.0 copy-start.7
  192.4 1.3 multiply_subtract_fusion.2
  193.7 0.0 copy-done.10
  193.7 0.0 copy-done.14
  193.7 0.0 copy-done.15
  193.7 1.8 multiply_subtract_fusion.3
  195.5 0.0 copy-done.1
  195.5 0.0 copy-done.6
  195.5 0.0 copy-done.7
  195.5 0.0 copy-start.3
  195.5 0.0 copy-start.8
  195.5 0.0 copy-start.9
  195.5 1.6 multiply_subtract_fusion.1
  197.1 0.0 copy-done.3
  197.1 0.0 copy-done.8
  197.1 0.6 copy-done.9
  197.7 0.0 copy-start.22
  197.7 0.0 copy-start.27
  197.7 0.0 copy-start.28
  197.8 0.0 copy-start.19
  197.8 0.0 copy-start.25
  197.8 0.0 copy-start.26
  197.8 0.0 copy-start.13
  197.8 0.0 copy-start.5
  197.8 1.6 multiply_subtract_fusion
  199.4 0.0 copy-done.20
  199.4 0.1 reshape.93
  199.5 0.1 reshape.94
  199.6 0.6 multiply_subtract_fusion.4
  200.2 0.7 multiply_subtract_fusion.5
  200.9 0.1 copy.135
  201.0 0.6 copy.144
  201.6 0.6 copy.145
  202.2 0.6 copy.146
  202.8 0.6 copy.147
  203.4 0.7 copy.194
  204.2 0.9 copy.195
  (45 shorter events, 0.4 us)
Async XLA Ops:
  0.7 2.2 %copy-start = (f32[2,48,1536]{2,1,0:T(8,128)S(1)}, f32[2,48,1536]{2,1,0:T(8,128)}, u32[]{:S(2)}) copy-start(f32[2,48,1536]{2,1,0:T(8,128)} %param.27) | copy-start | bytes 1769476
  0.7 2.4 %copy-start.2 = (f32[2,1536,48]{1,2,0:T(8,128)S(1)}, f32[2,1536,48]{1,2,0:T(8,128)}, u32[]{:S(2)}) copy-start(f32[2,1536,48]{1,2,0:T(8,128)} %param.28) | copy-start | bytes 1769476
  2.9 1.2 copy-start.21
  3.0 1.2 copy-start.16
  3.0 1.5 copy-start.18
  190.5 1.7 copy-start.4
  190.5 1.7 copy-start.11
  190.5 1.9 copy-start.12
  192.3 1.3 copy-start.10
  192.3 1.3 copy-start.14
  192.4 1.3 copy-start.15
  192.4 3.1 %copy-start.1 = (f32[2,48,1536]{2,1,0:T(8,128)S(1)}, f32[2,48,1536]{2,1,0:T(8,128)}, u32[]{:S(2)}) copy-start(f32[2,48,1536]{2,1,0:T(8,128)} %param.27) | copy-start | bytes 1769476
  192.4 3.1 %copy-start.6 = (f32[2,48,1536]{2,1,0:T(8,128)S(1)}, f32[2,48,1536]{2,1,0:T(8,128)}, u32[]{:S(2)}) copy-start(f32[2,48,1536]{2,1,0:T(8,128)} %param.34) | copy-start | bytes 1769476
  192.4 3.1 %copy-start.7 = (f32[2,48,1536]{2,1,0:T(8,128)S(1)}, f32[2,48,1536]{2,1,0:T(8,128)}, u32[]{:S(2)}) copy-start(f32[2,48,1536]{2,1,0:T(8,128)} %param.41) | copy-start | bytes 1769476
  195.5 1.6 copy-start.3
  195.5 1.6 copy-start.8
  195.5 2.2 %copy-start.9 = (f32[2,1536,48]{1,2,0:T(8,128)S(1)}, f32[2,1536,48]{1,2,0:T(8,128)}, u32[]{:S(2)}) copy-start(f32[2,1536,48]{1,2,0:T(8,128)} %param.42) | copy-start | bytes 1769476
  197.7 1.7 copy-start.20
  197.7 1.9 copy-start.17
  197.7 1.9 copy-start.23
  197.7 1.9 copy-start.24
  197.7 2.5 %copy-start.22 = (f32[2,24,4]{1,2,0:T(4,128)S(1)}, f32[2,24,4]{1,2,0:T(4,128)}, u32[]{:S(2)}) copy-start(f32[2,24,4]{1,2,0:T(4,128)} %param.30) | copy-start | bytes 2308
  197.7 2.5 %copy-start.27 = (f32[2,24,4]{1,2,0:T(4,128)S(1)}, f32[2,24,4]{1,2,0:T(4,128)}, u32[]{:S(2)}) copy-start(f32[2,24,4]{1,2,0:T(4,128)} %param.37) | copy-start | bytes 2308
  197.7 2.5 %copy-start.28 = (f32[2,24,4]{1,2,0:T(4,128)S(1)}, f32[2,24,4]{1,2,0:T(4,128)}, u32[]{:S(2)}) copy-start(f32[2,24,4]{1,2,0:T(4,128)} %param.44) | copy-start | bytes 2308
  197.8 3.8 %copy-start.19 = (f32[2,6,48]{2,0,1:T(2,128)S(1)}, f32[2,6,48]{2,0,1:T(2,128)}, u32[]{:S(2)}) copy-start(f32[2,6,48]{2,0,1:T(2,128)} %param.31) | copy-start | bytes 6916
  197.8 3.8 %copy-start.25 = (f32[2,6,48]{2,0,1:T(2,128)S(1)}, f32[2,6,48]{2,0,1:T(2,128)}, u32[]{:S(2)}) copy-start(f32[2,6,48]{2,0,1:T(2,128)} %param.38) | copy-start | bytes 6916
  197.8 3.8 %copy-start.26 = (f32[2,6,48]{2,0,1:T(2,128)S(1)}, f32[2,6,48]{2,0,1:T(2,128)}, u32[]{:S(2)}) copy-start(f32[2,6,48]{2,0,1:T(2,128)} %param.45) | copy-start | bytes 6916
  197.8 5.6 %copy-start.13 = (bf16[256,768]{1,0:T(8,128)(2,1)S(1)}, bf16[256,768]{1,0:T(8,128)(2,1)}, u32[]{:S(2)}) copy-start(bf16[256,768]{1,0:T(8,128)(2,1)} %get-tuple-element.196) | copy-start | bytes 1179652
  197.8 6.4 %copy-start.5 = (f32[256,768]{1,0:T(8,128)S(1)}, f32[256,768]{1,0:T(8,128)}, u32[]{:S(2)}) copy-start(f32[256,768]{1,0:T(8,128)} %get-tuple-element.197) | copy-start | bytes 2359300

commit v4 on v3

--- a/solution.py
+++ b/solution.py
@@ -46,8 +46,8 @@
     return tuple(sizes) + (2,)
 
 
-LEADS = (6, 5, 3, 1, 0)
-TURNED_LEADS = (8, 7, 5, 1, 0)
+LEADS = (7, 5, 4, 2, 0)
+EARLY = 12
 
 
 def spread_leads(leads, hops):
@@ -80,7 +80,7 @@
         self.hops = tuple(1 if size == 2 else 3 for size in self.axes)
         self.slots = sum(self.hops)
         self.chunk = rows // 2
-        self.early = TURN_EVERY - 1 if self.axes[:2] == (4, 2) else 0
+        self.early = EARLY if self.axes[:2] == (4, 2) else 0
 
 
 def train_kernel(
@@ -128,6 +128,9 @@
     rs_recv,
     x_send,
     x_recv,
+    GO,
+    OUT,
+    go_sem,
 ):
     axes = plan.axes
     depth = len(axes)
@@ -196,12 +199,6 @@
     straight = tuple(range(depth))
     turned = (1, 0) + straight[2:]
     early = plan.early
-
-    def gather_turned(unit):
-        return lax.rem(unit, TURN_EVERY) == TURN_EVERY - 1
-
-    def gather_order(unit):
-        return turned if unit % TURN_EVERY == TURN_EVERY - 1 else straight
 
     def gather_copy(k, hop, unit, order, small, sending):
         done = order[: order.index(k)]
@@ -332,24 +329,15 @@
 
     hops = plan.slots
     leads = spread_leads(LEADS, hops)
-    turned_leads = spread_leads(TURNED_LEADS, hops)
 
     def gather_tick(n, carry=0):
         for index in range(hops):
             ahead = n + leads[index]
-            inside = (ahead >= 0) & (ahead < L * NP)
-
-            @pl.when(inside & jnp.logical_not(gather_turned(ahead)))
+
+            @pl.when((ahead >= 0) & (ahead < L * NP))
             def _():
                 gather_hop(index, ahead, straight, False)
 
-            further = n + turned_leads[index]
-            inside = (further >= 0) & (further < L * NP)
-
-            @pl.when(inside & gather_turned(further))
-            def _():
-                gather_hop(index, further, turned, False)
-
         return carry
 
     def ready(low, high):
@@ -357,8 +345,7 @@
 
     gather_begin(0, small_index, straight, True)
     for unit in range(L * NP):
-        order = gather_order(unit)
-        gather_begin(order[0], unit, order, False)
+        gather_begin(0, unit, straight, False)
         if unit < early:
             early_own(unit, True).start()
     here = tuple(digit)
@@ -531,6 +518,9 @@
         else:
             W[(unit,) + spot] = value.astype(BF)
 
+    def keep_copy(unit):
+        return pltpu.make_async_copy(GO.at[unit], gout_ref.at[unit], go_sem.at[unit])
+
     def finish(k, unit, order, small, slots):
         spot = scatter_spot(k, order, digit[k])
         value = held(small, unit, spot) + arrived(k, order, small, unit, slots)
@@ -541,7 +531,8 @@
         elif small:
             smallg_ref[...] = value
         else:
-            gout_ref[unit] = value
+            GO[unit] = value
+            keep_copy(unit).start()
 
     def add_in(k, unit, order, small, value, slots):
         spot = scatter_spot(k, order, value)
@@ -593,13 +584,6 @@
 
     def column_sum(values):
         return jnp.sum(values, axis=0, keepdims=True)
-
-    def drain_down(unit):
-        for order in (straight, turned):
-
-            @pl.when(gather_turned(unit) == (order == turned))
-            def _():
-                gather_drain(unit, order)
 
     def down_gradient(layer, number):
         down = layer * NP + 4 + UP
@@ -714,7 +698,7 @@
             @pl.when(layer + 1 == L)
             def _():
                 for unit in (down + number, down + number + 1):
-                    drain_down(unit)
+                    gather_drain(unit, straight)
                 down_gradient(layer, number)
 
         return carry
@@ -785,7 +769,7 @@
     VG[L - 1, 5:6] = column_sum(DX[...])
     DMID = ACC
     for unit in range((L - 1) * NP + 4 + UP):
-        gather_drain(unit, gather_order(unit))
+        gather_drain(unit, straight)
     gather_drain(small_index, straight, True)
 
     def produced(m):
@@ -855,14 +839,20 @@
             done[index - 1] += 1
         return events
 
-    def pump_rest():
-        for index, m in rest_order():
-            name = m % NP
-            name = 4 + UP + name if name < UP else 4 + name - UP if name < 2 * UP else NP - 1 - name
-            unit = (L - 1 - m // NP) * NP + name
-            scatter_hop(index, unit, turned if m % TURN_EVERY == 0 else straight)
+    def named(m):
+        name = m % NP
+        name = 4 + UP + name if name < UP else 4 + name - UP if name < 2 * UP else NP - 1 - name
+        return (L - 1 - m // NP) * NP + name, turned if m % TURN_EVERY == 0 else straight
+
+    def pump_rest(aside):
+        events = rest_order()
+        for number, (index, m) in enumerate(events):
+            unit, order = named(m)
+            scatter_hop(index, unit, order)
             if m == L * NP - 1:
                 scatter_hop(index, small_index, straight, True)
+            if len(events) - 1 - number in aside:
+                aside[len(events) - 1 - number]()
 
     def backward_layer(step, carry):
         layer = L - 1 - step
@@ -962,19 +952,33 @@
     scatter_begin(depth - 1, small_index, straight, True)
     for part in range(2):
         exchange_send(2 * L - 1, 1, part, LAST[pl.ds(part * chunk, chunk)])
-    gin_ref[...] = DX[...]
+    gin_copy = pltpu.make_async_copy(DX, gin_ref, go_sem.at[L * NP])
+    out_copy = pltpu.make_async_copy(OUT, out_ref, go_sem.at[L * NP + 1])
+    gin_copy.start()
     scatter_hop(0, small_index, straight, True)
-    pump_rest()
-    for part in range(2):
-        region = pl.ds(part * chunk, chunk)
-        value = MID[region] + exchange_sum(2 * L - 1, 1, part) + VEC[L - 1, 5:6]
-        out_ref[region] = value.astype(BF)
-    exchange_done(2 * L - 1, 1)
+
+    def output():
+        for part in range(2):
+            region = pl.ds(part * chunk, chunk)
+            value = MID[region] + exchange_sum(2 * L - 1, 1, part) + VEC[L - 1, 5:6]
+            OUT[region] = value.astype(BF)
+        out_copy.start()
+        exchange_done(2 * L - 1, 1)
+        gin_copy.wait()
+
+    first_left = L * NP - NP // 2
+
+    def drain_first():
+        for m in range(first_left):
+            scatter_drain(*named(m))
+
+    pump_rest({14: output, 4: drain_first})
+    for m in range(first_left, L * NP):
+        scatter_drain(*named(m))
+    scatter_drain(small_index, straight, True)
+    out_copy.wait()
     for unit in range(L * NP):
-        name = unit % NP
-        turn = name - 4 - UP if name >= 4 + UP else name - 4 + UP if name >= 4 else NP - 1 - name
-        scatter_drain(unit, turned if turn % TURN_EVERY == 0 else straight)
-    scatter_drain(small_index, straight, True)
+        keep_copy(unit).wait()
 
 
 PUMPS = (
@@ -1045,6 +1049,9 @@
         pltpu.SemaphoreType.DMA((L * NP + 1, plan.slots)),
         pltpu.SemaphoreType.DMA((4 * L, 2)),
         pltpu.SemaphoreType.DMA((4 * L, 2)),
+        pltpu.VMEM((L * NP, rp, half), F32),
+        pltpu.VMEM((rows, Dp), BF),
+        pltpu.SemaphoreType.DMA((L * NP + 2,)),
     ]
     return pl.pallas_call(
         functools.partial(train_kernel, plan),
@@ -1055,7 +1062,7 @@
             jax.ShapeDtypeStruct((rp + BIAS_ROWS, LANES), F32),
         ),
         in_specs=[pl.BlockSpec(memory_space=pltpu.VMEM)] * 4,
-        out_specs=tuple([pl.BlockSpec(memory_space=pltpu.VMEM)] * 4),
+        out_specs=tuple([pl.BlockSpec(memory_space=pl.ANY)] * 3 + [pl.BlockSpec(memory_space=pltpu.VMEM)]),
         scratch_shapes=scratch,
         compiler_params=pltpu.CompilerParams(
             collective_id=0, has_side_effects=True, vmem_limit_bytes=67043328

time: 205 us -> 198 us (0.966)
  Pallas kernels: 185 us -> 178 us
    pallas_call x1, Pallas kernels: 185 us -> 178 us  [run_kernel(): pl.pallas_call(functools.partial(train_kernel, plan), out_shape=(jax.Shap...]
where the time goes in v4:
time: 198 us
  Pallas kernels  178 us (90%)
  other arithmetic  10.4 us (5%)
  local copies, waits for them, and re-layouts  8.37 us (4%)
    pallas_call x1, Pallas kernels, run_kernel(): pl.pallas_call(functools.partial(train_kernel, plan), out_shape=(jax.Shap...  178 us
    sub x7, other arithmetic, adamw(): weight - rate * (first_hat / (jnp.sqrt(second_hat) + adam_eps) + decay *...  7.57 us
    unnamed x75, local copies, waits for them, and re-layouts  5.09 us

profile of v4, /device:TPU:0, one launch (start us, length us, event | category | flops | bytes accessed | tf_op | source)
XLA Modules:
  0.0 197.6 jit_solution(6259982458423291199)
XLA Ops:
  0.7 0.0 copy-start
  0.7 0.0 copy-start.2
  0.7 1.1 convert_bitcast_fusion.1
  1.9 0.9 bitcast_dynamic-update-slice_fusion
  2.9 0.0 copy-done
  2.9 0.0 copy-start.21
  3.0 0.0 copy-start.16
  3.0 0.0 copy-start.18
  3.0 0.0 copy-done.2
  3.2 1.0 copy.117
  4.2 0.0 copy-done.21
  4.2 0.0 copy-done.16
  4.2 0.1 reshape.90
  4.3 0.1 maximum_bitcast_fusion.1
  4.4 0.1 reshape.91
  4.5 0.0 copy-done.18
  4.5 0.1 copy.119
  4.6 0.6 fusion.17.small_ref
  5.2 177.8 %train_step.1 = (bf16[256,768]{1,0:T(8,128)(2,1)}, f32[256,768]{1,0:T(8,128)}, f32[24,48,384]{2,1,0:T(8,128)}, f32[64,128]{1,0:T(8,128)}) custom-call(bf16[256,768]{1,0:T(8,128)(2,1)} %frames_ref.1, bf16[256,768]{1,0:T(8,128)(2,1)} %cot_ref.1, bf16[24,48,384]{2,1,0:T(8,128)(2,1)} %bitcast.132, bf16[64,128]{1,0:T(8,128)(2,1)} %fusion.17.small_ref), custom_call_target="tpu_custom_call" | custom-call | tf_op jit(solution)/shard_map/train_step/pallas_call | solution.py:1056
  183.0 0.0 copy-start.4
  183.0 0.0 copy-start.11
  183.0 0.0 copy-start.12
  183.0 1.7 slice_bitcast_fusion.3
  184.7 0.0 copy-done.4
  184.8 0.0 copy-done.11
  184.8 0.1 copy-done.12
  184.9 0.0 copy-start.6
  184.9 0.0 copy-start.7
  184.9 1.3 multiply_subtract_fusion.2
  186.2 0.0 copy-done.10
  186.2 0.0 copy-done.14
  186.2 0.0 copy-done.15
  186.3 1.8 multiply_subtract_fusion.3
  188.0 0.0 copy-done.1
  188.0 0.0 copy-done.6
  188.0 0.0 copy-done.7
  188.1 0.0 copy-start.3
  188.1 0.0 copy-start.8
  188.1 0.0 copy-start.9
  188.1 1.6 multiply_subtract_fusion.1
  189.7 0.0 copy-done.3
  189.7 0.0 copy-done.8
  189.7 0.6 copy-done.9
  190.3 0.0 copy-start.22
  190.3 0.0 copy-start.27
  190.3 0.0 copy-start.28
  190.3 0.0 copy-start.19
  190.3 0.0 copy-start.25
  190.3 0.0 copy-start.26
  190.3 0.0 copy-start.13
  190.4 1.6 multiply_subtract_fusion
  191.9 0.1 reshape.93
  192.0 0.1 reshape.94
  192.1 0.0 copy-done.24
  192.1 0.6 multiply_subtract_fusion.4
  192.8 0.7 multiply_subtract_fusion.5
  193.5 0.1 copy.135
  193.5 0.6 copy.144
  194.2 0.0 copy-done.25
  194.2 0.6 copy.145
  194.8 0.6 copy.146
  195.4 0.6 copy.147
  196.0 0.7 copy.194
  196.7 0.9 copy.195
  (45 shorter events, 0.4 us)
Async XLA Ops:
  0.7 2.2 %copy-start = (f32[2,48,1536]{2,1,0:T(8,128)S(1)}, f32[2,48,1536]{2,1,0:T(8,128)}, u32[]{:S(2)}) copy-start(f32[2,48,1536]{2,1,0:T(8,128)} %param.27) | copy-start | bytes 1769476
  0.7 2.4 %copy-start.2 = (f32[2,1536,48]{1,2,0:T(8,128)S(1)}, f32[2,1536,48]{1,2,0:T(8,128)}, u32[]{:S(2)}) copy-start(f32[2,1536,48]{1,2,0:T(8,128)} %param.28) | copy-start | bytes 1769476
  2.9 1.2 copy-start.21
  3.0 1.2 copy-start.16
  3.0 1.5 copy-start.18
  183.0 1.7 copy-start.4
  183.0 1.7 copy-start.11
  183.0 1.9 copy-start.12
  184.9 1.3 copy-start.10
  184.9 1.3 copy-start.14
  184.9 1.3 copy-start.15
  184.9 3.1 %copy-start.1 = (f32[2,48,1536]{2,1,0:T(8,128)S(1)}, f32[2,48,1536]{2,1,0:T(8,128)}, u32[]{:S(2)}) copy-start(f32[2,48,1536]{2,1,0:T(8,128)} %param.27) | copy-start | bytes 1769476
  184.9 3.1 %copy-start.6 = (f32[2,48,1536]{2,1,0:T(8,128)S(1)}, f32[2,48,1536]{2,1,0:T(8,128)}, u32[]{:S(2)}) copy-start(f32[2,48,1536]{2,1,0:T(8,128)} %param.34) | copy-start | bytes 1769476
  184.9 3.1 %copy-start.7 = (f32[2,48,1536]{2,1,0:T(8,128)S(1)}, f32[2,48,1536]{2,1,0:T(8,128)}, u32[]{:S(2)}) copy-start(f32[2,48,1536]{2,1,0:T(8,128)} %param.41) | copy-start | bytes 1769476
  188.1 1.6 copy-start.3
  188.1 1.6 copy-start.8
  188.1 2.2 %copy-start.9 = (f32[2,1536,48]{1,2,0:T(8,128)S(1)}, f32[2,1536,48]{1,2,0:T(8,128)}, u32[]{:S(2)}) copy-start(f32[2,1536,48]{1,2,0:T(8,128)} %param.42) | copy-start | bytes 1769476
  190.3 1.7 copy-start.20
  190.3 1.9 copy-start.17
  190.3 1.9 copy-start.23
  190.3 1.9 copy-start.24
  190.3 2.5 %copy-start.22 = (f32[2,24,4]{1,2,0:T(4,128)S(1)}, f32[2,24,4]{1,2,0:T(4,128)}, u32[]{:S(2)}) copy-start(f32[2,24,4]{1,2,0:T(4,128)} %param.30) | copy-start | bytes 2308
  190.3 2.5 %copy-start.27 = (f32[2,24,4]{1,2,0:T(4,128)S(1)}, f32[2,24,4]{1,2,0:T(4,128)}, u32[]{:S(2)}) copy-start(f32[2,24,4]{1,2,0:T(4,128)} %param.37) | copy-start | bytes 2308
  190.3 2.5 %copy-start.28 = (f32[2,24,4]{1,2,0:T(4,128)S(1)}, f32[2,24,4]{1,2,0:T(4,128)}, u32[]{:S(2)}) copy-start(f32[2,24,4]{1,2,0:T(4,128)} %param.44) | copy-start | bytes 2308
  190.3 3.8 %copy-start.19 = (f32[2,6,48]{2,0,1:T(2,128)S(1)}, f32[2,6,48]{2,0,1:T(2,128)}, u32[]{:S(2)}) copy-start(f32[2,6,48]{2,0,1:T(2,128)} %param.31) | copy-start | bytes 6916
  190.3 3.8 %copy-start.25 = (f32[2,6,48]{2,0,1:T(2,128)S(1)}, f32[2,6,48]{2,0,1:T(2,128)}, u32[]{:S(2)}) copy-start(f32[2,6,48]{2,0,1:T(2,128)} %param.38) | copy-start | bytes 6916
  190.3 3.8 %copy-start.26 = (f32[2,6,48]{2,0,1:T(2,128)S(1)}, f32[2,6,48]{2,0,1:T(2,128)}, u32[]{:S(2)}) copy-start(f32[2,6,48]{2,0,1:T(2,128)} %param.45) | copy-start | bytes 6916
  190.3 5.6 %copy-start.13 = (bf16[256,768]{1,0:T(8,128)(2,1)S(1)}, bf16[256,768]{1,0:T(8,128)(2,1)}, u32[]{:S(2)}) copy-start(bf16[256,768]{1,0:T(8,128)(2,1)} %get-tuple-element.196) | copy-start | bytes 1179652
  190.4 6.4 %copy-start.5 = (f32[256,768]{1,0:T(8,128)S(1)}, f32[256,768]{1,0:T(8,128)}, u32[]{:S(2)}) copy-start(f32[256,768]{1,0:T(8,128)} %get-tuple-element.197) | copy-start | bytes 2359300

commit v5 on v4

--- a/solution.py
+++ b/solution.py
@@ -79,6 +79,7 @@
         self.bias_cols = 2 * half + hidden
         self.hops = tuple(1 if size == 2 else 3 for size in self.axes)
         self.slots = sum(self.hops)
+        self.signals = sum(1 if size == 2 else 2 for size in self.axes)
         self.chunk = rows // 2
         self.early = EARLY if self.axes[:2] == (4, 2) else 0
 
@@ -124,6 +125,7 @@
     RSs,
     ag_send,
     ag_recv,
+    early_recv,
     rs_send,
     rs_recv,
     x_send,
@@ -146,7 +148,7 @@
     me = lax.axis_index("fsdp")
     side = lax.axis_index("tp")
     digit = [lax.rem(me // stride, size) for stride, size in zip(plan.strides, axes)]
-    slot_of = [sum(plan.hops[:k]) for k in range(depth)]
+    slot_of = [sum(1 if size == 2 else 2 for size in axes[:k]) for k in range(depth)]
     other = (me, 1 - side)
 
     def device(k, value):
@@ -199,6 +201,13 @@
     straight = tuple(range(depth))
     turned = (1, 0) + straight[2:]
     early = plan.early
+
+    late = L * NP - UP
+
+    def group_of(unit, small=False):
+        if small:
+            return 1 + UP // 2
+        return jnp.where(unit < late, 0, 1 + (unit - late) // 2)
 
     def gather_copy(k, hop, unit, order, small, sending):
         done = order[: order.index(k)]
@@ -224,29 +233,30 @@
         src = dst
         if sending and not done and hop == 0:
             src = small_ref if small else shard_ref.at[unit]
-        slot = slot_of[k] + hop
-        return remote(src, dst, ag_send.at[unit, slot], ag_recv.at[unit, slot], device(k, target))
-
-    def early_copy(value, slot, unit, sending):
+        slot = slot_of[k] + hop % 2
+        return remote(src, dst, ag_send.at[group_of(unit, small), slot], ag_recv.at[unit, slot], device(k, target))
+
+    def early_copy(value, number, unit, sending):
         own = value is digit[0]
         spot = (value, digit[1] if sending else 1 - digit[1]) + tuple(digit[2:])
         dst = W.at[(unit,) + spot]
         src = shard_ref.at[unit] if own and sending else dst
         target = device(1, 1 - digit[1])
-        return remote(src, dst, ag_send.at[unit, slot], ag_recv.at[unit, slot], target)
+        arrival = ag_recv.at[unit, slot_of[1]] if number == 1 else early_recv.at[unit, number // 2]
+        return remote(src, dst, ag_send.at[0, plan.signals + number], arrival, target)
 
     def early_own(unit, sending):
-        return early_copy(digit[0], plan.slots, unit, sending)
+        return early_copy(digit[0], 0, unit, sending)
 
     def early_rest(unit, sending, act):
         @pl.when(outer[0])
         def _():
-            act(early_copy(three[0], slot_of[1], unit, sending))
+            act(early_copy(three[0], 1, unit, sending))
 
         @pl.when(inner[0])
         def _():
-            act(early_copy(mine_out[0], slot_of[1], unit, sending))
-            act(early_copy(far[0], plan.slots + 1, unit, sending))
+            act(early_copy(mine_out[0], 1, unit, sending))
+            act(early_copy(far[0], 2, unit, sending))
 
     def is_early(k, order, small):
         return bool(early) and k == 1 and order == straight and not small
@@ -305,27 +315,46 @@
             if index > 0:
                 gather_next(k, unit, order, small)
 
-    def gather_drain(unit, order, small=False):
+    def gather_drain(group, first, number, small=False):
+        def sent(slot, spot, low, count):
+            ref = SB.at[spot] if small else W.at[(pl.ds(low, count),) + spot]
+            remote(ref, ref, ag_send.at[group, slot], ag_recv.at[0, 0], other).wait_send()
+
+        ahead = min(early, number) if group == 0 and not small else 0
         for k in range(depth):
-            for hop in range(plan.hops[k]):
-                if is_early(k, order, small):
-
-                    @pl.when(unit < early)
-                    def _():
-                        early_own(unit, True).wait_send()
-                        early_rest(unit, True, lambda copy: copy.wait_send())
-
-                    @pl.when(unit >= early)
-                    def _():
-                        gather_copy(k, hop, unit, order, small, True).wait_send()
-
-                elif axes[k] == 2:
-                    gather_copy(k, hop, unit, order, small, True).wait_send()
-                else:
-
-                    @pl.when(outer[k] if hop == 0 else inner[k])
-                    def _():
-                        gather_copy(k, hop, unit, order, small, True).wait_send()
+
+            def spot(value):
+                return tuple(
+                    slice(None) if a < k else value if a == k else digit[a] for a in range(depth)
+                )
+
+            if axes[k] == 2:
+                skipped = ahead if k == 1 else 0
+                if number > skipped:
+                    sent(slot_of[k], spot(digit[k]), first, number - skipped)
+            else:
+
+                @pl.when(outer[k])
+                def _():
+                    sent(slot_of[k], spot(digit[k]), first, number)
+
+                @pl.when(inner[k])
+                def _():
+                    sent(slot_of[k] + 1, spot(near[k]), first, number)
+                    sent(slot_of[k], spot(three[k]), first, number)
+
+        if ahead:
+            tail = (digit[1],) + tuple(digit[2:])
+            sent(plan.signals, (digit[0],) + tail, 0, ahead)
+
+            @pl.when(outer[0])
+            def _():
+                sent(plan.signals + 1, (three[0],) + tail, 0, ahead)
+
+            @pl.when(inner[0])
+            def _():
+                sent(plan.signals + 1, (mine_out[0],) + tail, 0, ahead)
+                sent(plan.signals + 2, (far[0],) + tail, 0, ahead)
 
     hops = plan.slots
     leads = spread_leads(LEADS, hops)
@@ -423,7 +452,7 @@
         return remote(
             XS.at[slot, region],
             XR.at[slot, region],
-            x_send.at[number, part],
+            x_send.at[slot, part],
             x_recv.at[number, part],
             other,
         )
@@ -491,8 +520,9 @@
             src, dst = SG.at[spot], RSs[k].at[land(k, order, slots)]
         else:
             src, dst = W.at[(unit,) + spot], landing_ref(k, order).at[(landing(k, order, unit),) + land(k, order, slots)]
-        slot = slot_of[k] + hop
-        return remote(src, dst, rs_send.at[unit, slot], rs_recv.at[unit, slot], device(k, target))
+        slot = slot_of[k] + hop % 2
+        kind = 2 if small else 1 if order == turned else 0
+        return remote(src, dst, rs_send.at[kind, slot], rs_recv.at[unit, slot], device(k, target))
 
     def scatter_begin(k, unit, order, small=False):
         if axes[k] == 2:
@@ -519,7 +549,7 @@
             W[(unit,) + spot] = value.astype(BF)
 
     def keep_copy(unit):
-        return pltpu.make_async_copy(GO.at[unit], gout_ref.at[unit], go_sem.at[unit])
+        return pltpu.make_async_copy(GO.at[unit], gout_ref.at[unit], go_sem.at[0])
 
     def finish(k, unit, order, small, slots):
         spot = scatter_spot(k, order, digit[k])
@@ -561,16 +591,26 @@
             else:
                 finish(k, unit, order, small, 0)
 
-    def scatter_drain(unit, order, small=False):
+    def scatter_drain(kind, order, number):
+        def sent(k, hop, value, count):
+            spot = scatter_spot(k, order, value)
+            ref = SG.at[spot] if kind == 2 else W.at[(pl.ds(0, count),) + spot]
+            remote(ref, ref, rs_send.at[kind, slot_of[k] + hop], rs_recv.at[0, 0], other).wait_send()
+
         for k in range(depth):
-            for hop in range(plan.hops[k]):
-                if axes[k] == 2:
-                    scatter_copy(k, hop, unit, order, small).wait_send()
-                else:
-
-                    @pl.when(outer[k] if hop == 0 else inner[k])
-                    def _():
-                        scatter_copy(k, hop, unit, order, small).wait_send()
+            if axes[k] == 2:
+                if k < depth - 1 or kind != 1:
+                    sent(k, 0, 1 - digit[k], L * NP if k == depth - 1 else number)
+            else:
+
+                @pl.when(outer[k])
+                def _():
+                    sent(k, 0, three[k], number)
+
+                @pl.when(inner[k])
+                def _():
+                    sent(k, 1, far[k], number)
+                    sent(k, 0, mine_out[k], number)
 
     block_shape = axes + (rp,)
 
@@ -697,8 +737,7 @@
 
             @pl.when(layer + 1 == L)
             def _():
-                for unit in (down + number, down + number + 1):
-                    gather_drain(unit, straight)
+                gather_drain(1 + number // 2, late + number, 2)
                 down_gradient(layer, number)
 
         return carry
@@ -768,9 +807,8 @@
     DX[...] = cot_ref[...].astype(F32)
     VG[L - 1, 5:6] = column_sum(DX[...])
     DMID = ACC
-    for unit in range((L - 1) * NP + 4 + UP):
-        gather_drain(unit, straight)
-    gather_drain(small_index, straight, True)
+    gather_drain(0, 0, late)
+    gather_drain(group_of(0, True), 0, 1, True)
 
     def produced(m):
         turn = lax.rem(m, NP)
@@ -952,8 +990,8 @@
     scatter_begin(depth - 1, small_index, straight, True)
     for part in range(2):
         exchange_send(2 * L - 1, 1, part, LAST[pl.ds(part * chunk, chunk)])
-    gin_copy = pltpu.make_async_copy(DX, gin_ref, go_sem.at[L * NP])
-    out_copy = pltpu.make_async_copy(OUT, out_ref, go_sem.at[L * NP + 1])
+    gin_copy = pltpu.make_async_copy(DX, gin_ref, go_sem.at[1])
+    out_copy = pltpu.make_async_copy(OUT, out_ref, go_sem.at[2])
     gin_copy.start()
     scatter_hop(0, small_index, straight, True)
 
@@ -966,19 +1004,13 @@
         exchange_done(2 * L - 1, 1)
         gin_copy.wait()
 
-    first_left = L * NP - NP // 2
-
-    def drain_first():
-        for m in range(first_left):
-            scatter_drain(*named(m))
-
-    pump_rest({14: output, 4: drain_first})
-    for m in range(first_left, L * NP):
-        scatter_drain(*named(m))
-    scatter_drain(small_index, straight, True)
+    pump_rest({14: output})
+    turned_number = -(-L * NP // TURN_EVERY)
+    scatter_drain(0, straight, L * NP - turned_number)
+    scatter_drain(1, turned, turned_number)
+    scatter_drain(2, straight, 1)
     out_copy.wait()
-    for unit in range(L * NP):
-        keep_copy(unit).wait()
+    pltpu.make_async_copy(GO, gout_ref, go_sem.at[0]).wait()
 
 
 PUMPS = (
@@ -1043,15 +1075,16 @@
         landings,
         turned_landings,
         small_landings,
-        pltpu.SemaphoreType.DMA((L * NP + 1, plan.slots + (2 if plan.early else 0))),
-        pltpu.SemaphoreType.DMA((L * NP + 1, plan.slots + (2 if plan.early else 0))),
-        pltpu.SemaphoreType.DMA((L * NP + 1, plan.slots)),
-        pltpu.SemaphoreType.DMA((L * NP + 1, plan.slots)),
-        pltpu.SemaphoreType.DMA((4 * L, 2)),
+        pltpu.SemaphoreType.DMA((2 + plan.ups // 2, plan.signals + 3)),
+        pltpu.SemaphoreType.DMA((L * NP + 1, plan.signals)),
+        pltpu.SemaphoreType.DMA((max(plan.early, 1), 2)),
+        pltpu.SemaphoreType.DMA((3, plan.signals)),
+        pltpu.SemaphoreType.DMA((L * NP + 1, plan.signals)),
+        pltpu.SemaphoreType.DMA((2, 2)),
         pltpu.SemaphoreType.DMA((4 * L, 2)),
         pltpu.VMEM((L * NP, rp, half), F32),
         pltpu.VMEM((rows, Dp), BF),
-        pltpu.SemaphoreType.DMA((L * NP + 2,)),
+        pltpu.SemaphoreType.DMA((3,)),
     ]
     return pl.pallas_call(
         functools.partial(train_kernel, plan),

time: 198 us -> 194 us (0.980)
  Pallas kernels: 178 us -> 174 us
    pallas_call x1, Pallas kernels: 178 us -> 174 us  [run_kernel(): pl.pallas_call(functools.partial(train_kernel, plan), out_shape=(jax.Shap...]
where the time goes in v5:
time: 194 us
  Pallas kernels  174 us (90%)
  other arithmetic  10.4 us (5%)
  local copies, waits for them, and re-layouts  8.37 us (4%)
    pallas_call x1, Pallas kernels, run_kernel(): pl.pallas_call(functools.partial(train_kernel, plan), out_shape=(jax.Shap...  174 us
    sub x7, other arithmetic, adamw(): weight - rate * (first_hat / (jnp.sqrt(second_hat) + adam_eps) + decay *...  7.57 us
    unnamed x75, local copies, waits for them, and re-layouts  5.09 us

profile of v5, /device:TPU:0, one launch (start us, length us, event | category | flops | bytes accessed | tf_op | source)
XLA Modules:
  0.0 194.0 jit_solution(17486853712649300955)
XLA Ops:
  0.7 0.0 copy-start
  0.7 0.0 copy-start.2
  0.7 1.1 convert_bitcast_fusion.1
  1.9 0.9 bitcast_dynamic-update-slice_fusion
  2.9 0.0 copy-done
  2.9 0.0 copy-start.21
  3.0 0.0 copy-start.16
  3.0 0.0 copy-start.18
  3.0 0.0 copy-done.2
  3.2 1.0 copy.117
  4.2 0.0 copy-done.21
  4.2 0.0 copy-done.16
  4.2 0.1 reshape.90
  4.3 0.1 maximum_bitcast_fusion.1
  4.4 0.1 reshape.91
  4.5 0.0 copy-done.18
  4.5 0.1 copy.119
  4.6 0.6 fusion.17.small_ref
  5.2 174.2 %train_step.1 = (bf16[256,768]{1,0:T(8,128)(2,1)}, f32[256,768]{1,0:T(8,128)}, f32[24,48,384]{2,1,0:T(8,128)}, f32[64,128]{1,0:T(8,128)}) custom-call(bf16[256,768]{1,0:T(8,128)(2,1)} %frames_ref.1, bf16[256,768]{1,0:T(8,128)(2,1)} %cot_ref.1, bf16[24,48,384]{2,1,0:T(8,128)(2,1)} %bitcast.132, bf16[64,128]{1,0:T(8,128)(2,1)} %fusion.17.small_ref), custom_call_target="tpu_custom_call" | custom-call | tf_op jit(solution)/shard_map/train_step/pallas_call | solution.py:1089
  179.4 0.0 copy-start.4
  179.4 0.0 copy-start.11
  179.4 0.0 copy-start.12
  179.5 1.7 slice_bitcast_fusion.3
  181.2 0.0 copy-done.4
  181.2 0.0 copy-done.11
  181.2 0.1 copy-done.12
  181.3 0.0 copy-start.6
  181.3 0.0 copy-start.7
  181.3 1.3 multiply_subtract_fusion.2
  182.7 0.0 copy-done.10
  182.7 0.0 copy-done.14
  182.7 0.0 copy-done.15
  182.7 1.8 multiply_subtract_fusion.3
  184.5 0.0 copy-done.1
  184.5 0.0 copy-done.6
  184.5 0.0 copy-start.3
  184.5 0.0 copy-start.8
  184.5 0.0 copy-start.9
  184.5 1.6 multiply_subtract_fusion.1
  186.1 0.0 copy-done.8
  186.1 0.6 copy-done.9
  186.7 0.0 copy-start.22
  186.7 0.0 copy-start.27
  186.7 0.0 copy-start.28
  186.7 0.0 copy-start.19
  186.7 0.0 copy-start.25
  186.7 0.0 copy-start.26
  186.8 1.6 multiply_subtract_fusion
  188.3 0.0 copy-done.20
  188.4 0.1 reshape.93
  188.4 0.1 reshape.94
  188.5 0.0 copy-done.17
  188.5 0.0 copy-done.24
  188.5 0.6 multiply_subtract_fusion.4
  189.2 0.0 copy-done.27
  189.2 0.7 multiply_subtract_fusion.5
  189.9 0.1 copy.135
  190.0 0.6 copy.144
  190.6 0.6 copy.145
  191.2 0.6 copy.146
  191.8 0.6 copy.147
  192.4 0.7 copy.194
  193.1 0.0 copy-done.5
  193.1 0.9 copy.195
  (45 shorter events, 0.4 us)
Async XLA Ops:
  0.7 2.2 %copy-start = (f32[2,48,1536]{2,1,0:T(8,128)S(1)}, f32[2,48,1536]{2,1,0:T(8,128)}, u32[]{:S(2)}) copy-start(f32[2,48,1536]{2,1,0:T(8,128)} %param.27) | copy-start | bytes 1769476
  0.7 2.4 %copy-start.2 = (f32[2,1536,48]{1,2,0:T(8,128)S(1)}, f32[2,1536,48]{1,2,0:T(8,128)}, u32[]{:S(2)}) copy-start(f32[2,1536,48]{1,2,0:T(8,128)} %param.28) | copy-start | bytes 1769476
  2.9 1.2 copy-start.21
  3.0 1.2 copy-start.16
  3.0 1.5 copy-start.18
  179.4 1.7 copy-start.4
  179.4 1.7 copy-start.11
  179.4 1.9 copy-start.12
  181.3 1.3 copy-start.10
  181.3 1.3 copy-start.14
  181.3 1.3 copy-start.15
  181.3 3.1 %copy-start.1 = (f32[2,48,1536]{2,1,0:T(8,128)S(1)}, f32[2,48,1536]{2,1,0:T(8,128)}, u32[]{:S(2)}) copy-start(f32[2,48,1536]{2,1,0:T(8,128)} %param.27) | copy-start | bytes 1769476
  181.3 3.1 %copy-start.6 = (f32[2,48,1536]{2,1,0:T(8,128)S(1)}, f32[2,48,1536]{2,1,0:T(8,128)}, u32[]{:S(2)}) copy-start(f32[2,48,1536]{2,1,0:T(8,128)} %param.34) | copy-start | bytes 1769476
  181.3 3.1 %copy-start.7 = (f32[2,48,1536]{2,1,0:T(8,128)S(1)}, f32[2,48,1536]{2,1,0:T(8,128)}, u32[]{:S(2)}) copy-start(f32[2,48,1536]{2,1,0:T(8,128)} %param.41) | copy-start | bytes 1769476
  184.5 1.6 copy-start.3
  184.5 1.6 copy-start.8
  184.5 2.2 %copy-start.9 = (f32[2,1536,48]{1,2,0:T(8,128)S(1)}, f32[2,1536,48]{1,2,0:T(8,128)}, u32[]{:S(2)}) copy-start(f32[2,1536,48]{1,2,0:T(8,128)} %param.42) | copy-start | bytes 1769476
  186.7 1.7 copy-start.20
  186.7 1.9 copy-start.17
  186.7 1.9 copy-start.23
  186.7 1.9 copy-start.24
  186.7 2.5 %copy-start.22 = (f32[2,24,4]{1,2,0:T(4,128)S(1)}, f32[2,24,4]{1,2,0:T(4,128)}, u32[]{:S(2)}) copy-start(f32[2,24,4]{1,2,0:T(4,128)} %param.30) | copy-start | bytes 2308
  186.7 2.5 %copy-start.27 = (f32[2,24,4]{1,2,0:T(4,128)S(1)}, f32[2,24,4]{1,2,0:T(4,128)}, u32[]{:S(2)}) copy-start(f32[2,24,4]{1,2,0:T(4,128)} %param.37) | copy-start | bytes 2308
  186.7 2.5 %copy-start.28 = (f32[2,24,4]{1,2,0:T(4,128)S(1)}, f32[2,24,4]{1,2,0:T(4,128)}, u32[]{:S(2)}) copy-start(f32[2,24,4]{1,2,0:T(4,128)} %param.44) | copy-start | bytes 2308
  186.7 3.8 %copy-start.19 = (f32[2,6,48]{2,0,1:T(2,128)S(1)}, f32[2,6,48]{2,0,1:T(2,128)}, u32[]{:S(2)}) copy-start(f32[2,6,48]{2,0,1:T(2,128)} %param.31) | copy-start | bytes 6916
  186.7 3.8 %copy-start.25 = (f32[2,6,48]{2,0,1:T(2,128)S(1)}, f32[2,6,48]{2,0,1:T(2,128)}, u32[]{:S(2)}) copy-start(f32[2,6,48]{2,0,1:T(2,128)} %param.38) | copy-start | bytes 6916
  186.7 3.8 %copy-start.26 = (f32[2,6,48]{2,0,1:T(2,128)S(1)}, f32[2,6,48]{2,0,1:T(2,128)}, u32[]{:S(2)}) copy-start(f32[2,6,48]{2,0,1:T(2,128)} %param.45) | copy-start | bytes 6916
  186.8 5.6 %copy-start.13 = (bf16[256,768]{1,0:T(8,128)(2,1)S(1)}, bf16[256,768]{1,0:T(8,128)(2,1)}, u32[]{:S(2)}) copy-start(bf16[256,768]{1,0:T(8,128)(2,1)} %get-tuple-element.196) | copy-start | bytes 1179652
  186.8 6.4 %copy-start.5 = (f32[256,768]{1,0:T(8,128)S(1)}, f32[256,768]{1,0:T(8,128)}, u32[]{:S(2)}) copy-start(f32[256,768]{1,0:T(8,128)} %get-tuple-element.197) | copy-start | bytes 2359300
